TPU v7x, 32 devices: a whole 2x2x4 slice. The times are simulated.
32 devices in a mesh: dp: 8 (over z, y), mp: 4 (over x, core).
Axes of the slice: x: 2, y: 2, z: 4, core: 2. Of those that a mesh axis runs over, the one named last changes fastest.
Arguments:
- streams: bfloat16 [2048, 4, 8192], P('dp', None, 'mp'), may hold values from -200 to 200
- branch_out: bfloat16 [2048, 8192], P('dp', 'mp'), may hold values from -6 to 6
- merge_weight: float32 [20, 4, 8192], P(None, None, ('mp', 'dp')), may hold values from -0.03125 to 0.03125
- next_weight: float32 [24, 4, 8192], P(None, None, ('mp', 'dp')), may hold values from -0.03125 to 0.03125
- blend_bias: float32 [44], replicated, may hold values from -3 to 3
- blend_scale: float32 [5], replicated, may hold values from 0.5 to 3
- norm_gain: float32 [8192], P('mp'), may hold values from 0.5 to 1.5
Outputs:
- streams_out: bfloat16 [2048, 4, 8192], P('dp', None, 'mp')
- branch_in: bfloat16 [2048, 8192], P('dp', 'mp')
- next_mix: float32 [2048, 20], P('dp')
All inputs are finite; a program needn't handle non-finite values.
Results may differ from a plain program's by a relative error of at most 0.001.
Values sent between devices are 32-bit elements; how exact they have to be, the bound alone decides.
No kernel may reach another device: no remote copies, remote signals or barrier semaphores. Data moves between devices by JAX's collectives and lax.ppermute only.
A program may use at most 64 MiB of HBM per device.

v0:
```python
import jax
import jax.numpy as jnp
from jax import lax
from jax.sharding import PartitionSpec as P

D = 8192
STREAMS = 4
BALANCE_ROUNDS = 6


epsilon = 1e-06


def balance_normalize(balanced_matrix):
    for balance_round in range(BALANCE_ROUNDS):
        balanced_matrix = balanced_matrix / jnp.sum(balanced_matrix, axis=2, keepdims=True)
        balanced_matrix = balanced_matrix / jnp.sum(balanced_matrix, axis=1, keepdims=True)
    return balanced_matrix


def settle(columns, finish):
    summed = lax.psum(columns, "mp")
    result = finish(summed)
    return result


def first_coef(raw_sums, squares, blend_bias, blend_scale):
    rms_root = jnp.sqrt(squares / (STREAMS * D) + epsilon)
    score_logits = raw_sums / rms_root[:, None]
    post_mix = 2.0 * jax.nn.sigmoid(blend_scale[0] * score_logits[:, :4] + blend_bias[:4])
    residual_blend = balance_normalize(
        jnp.exp(
            blend_scale[1] * score_logits[:, 4:20].reshape(-1, 4, 4)
            + blend_bias[4:20].reshape(4, 4)
        )
    )
    return (post_mix, residual_blend)


def second_coef(raw_sums, squares, blend_bias, blend_scale):
    rms_root = jnp.sqrt(squares / (STREAMS * D) + epsilon)
    score_logits = raw_sums / rms_root[:, None]
    pre_next = jax.nn.sigmoid(blend_scale[2] * score_logits[:, :4] + blend_bias[20:24])
    post_next = 2.0 * jax.nn.sigmoid(blend_scale[3] * score_logits[:, 4:8] + blend_bias[24:28])
    residual_following = balance_normalize(
        jnp.exp(
            blend_scale[4] * score_logits[:, 8:24].reshape(-1, 4, 4)
            + blend_bias[28:44].reshape(4, 4)
        )
    )
    return (pre_next, post_next, residual_following)


def mix_streams(residual_blend, post_mix, streams, branch_out):
    branch_wide = branch_out.astype(jnp.float32)
    outputs = []
    for target in range(STREAMS):
        total = post_mix[:, target, None] * branch_wide
        for source in range(STREAMS):
            total = total + residual_blend[:, target, source, None] * streams[:, source, :].astype(
                jnp.float32
            )
        outputs.append(total)
    return jnp.stack(outputs, axis=1)


def unite(pre_next, mixed):
    total = pre_next[:, 0, None] * mixed[:, 0, :]
    for source in range(1, STREAMS):
        total = total + pre_next[:, source, None] * mixed[:, source, :]
    return total


def local(streams, branch_out, merge_weight, next_weight, blend_bias, blend_scale, norm_gain):
    merge_rows, next_rows = (
        lax.all_gather(merge_weight, "dp", axis=2, tiled=True),
        lax.all_gather(next_weight, "dp", axis=2, tiled=True),
    )
    highest = lax.Precision.HIGHEST
    raw_part = jnp.einsum(
        "tic,kic->tk", streams, merge_rows, precision=highest, preferred_element_type=jnp.float32
    )
    gram_part = jnp.einsum("tic,tjc->tij", streams, streams, preferred_element_type=jnp.float32)
    columns = jnp.concatenate([raw_part, jnp.trace(gram_part, axis1=1, axis2=2)[:, None]], axis=1)

    def finish_first(summed):
        post_mix, residual_blend = first_coef(
            summed[:, :20], summed[:, 20], blend_bias, blend_scale
        )
        return jnp.concatenate([post_mix, residual_blend.reshape(-1, 16)], axis=1)

    merge_coef = settle(columns, finish_first)
    post_mix = merge_coef[:, :4]
    residual_blend = merge_coef[:, 4:20].reshape(-1, 4, 4)
    mixed = mix_streams(residual_blend, post_mix, streams, branch_out)
    streams_out = mixed.astype(jnp.bfloat16)
    raw_next = jnp.einsum("tic,kic->tk", mixed, next_rows, precision=highest)
    extra_cols = jnp.sum(mixed * mixed, axis=(1, 2))[:, None]
    columns_next = jnp.concatenate([raw_next, extra_cols], axis=1)

    def finish_second(summed):
        squares = summed[:, 24]
        pre_next, post_next, residual_following = second_coef(
            summed[:, :24], squares, blend_bias, blend_scale
        )
        pieces = [pre_next, post_next, residual_following.reshape(-1, 16)]
        return jnp.concatenate(pieces, axis=1)

    next_coef = settle(columns_next, finish_second)
    pre_next = next_coef[:, :4]
    next_mix = next_coef[:, 4:24]
    united = unite(pre_next, mixed)
    united_sq = lax.psum(jnp.sum(united * united, axis=1), "mp")
    branch_in = (united / jnp.sqrt(united_sq / D + epsilon)[:, None] * norm_gain).astype(
        jnp.bfloat16
    )
    return (streams_out, branch_in, next_mix)


def solution(mesh):
    placed = (
        P("dp", None, "mp"),
        P("dp", "mp"),
        P(None, None, ("mp", "dp")),
        P(None, None, ("mp", "dp")),
        P(),
        P(),
        P("mp"),
    )
    return jax.shard_map(
        local,
        mesh=mesh,
        in_specs=placed,
        out_specs=(P("dp", None, "mp"), P("dp", "mp"), P("dp", None)),
        check_vma=False,
    )
```

profile of v0, /device:TPU:0, one launch (start us, length us, event | category | flops | bytes accessed | tf_op | source)
XLA Modules:
  0.0 152.0 jit_solution(15976659351027897930)
XLA Ops:
  0.6 0.0 copy-start.7
  0.7 0.0 copy-start.8
  0.7 0.0 copy-start.6
  0.7 0.0 copy-start.5
  0.7 9.4 %fusion.28 = f32[256]{0:T(256)S(1)} fusion(bf16[256,4,2048]{2,1,0:T(4,128)(2,1)} %param.7, pred[4,4]{1,0:T(4,128)(4,1)S(1)} %iota_compare_fusion), kind=kOutput, calls=%fused_computation.54 | convolution fusion | flops 16785152 | bytes 4195344 | tf_op jit(solution)/shard_map/tic,tjc->tij/dot_general | solution.py:83
  10.1 0.0 copy-done.7
  10.1 0.1 fusion.80
  10.2 0.1 add.136
  10.2 0.1 fusion.79
  10.3 0.1 add.168
  10.4 0.0 copy-done.8
  10.4 0.6 fusion.78
  11.0 0.0 copy-done.6
  11.0 0.0 copy-done.5
  11.1 33.9 %all_gather.7 = f32[24,4,2048]{2,0,1:T(8,128)S(1)} all-gather(f32[24,4,256]{2,0,1:T(8,128)S(1)} %copy.16), channel_id=1, replica_groups=mesh['dp'=8,'mp'=4] {'dp'}, dimensions={2}, use_global_device_ids=true | all-gather | bytes 884736 | tf_op jit(solution)/shard_map/all_gather | solution.py:77
  45.0 32.1 %all_gather.6 = f32[20,4,2048]{2,0,1:T(8,128)S(1)} all-gather(f32[20,4,256]{2,0,1:T(8,128)S(1)} %copy.10), channel_id=1, replica_groups=mesh['dp'=8,'mp'=4] {'dp'}, dimensions={2}, use_global_device_ids=true | all-gather | bytes 737280 | tf_op jit(solution)/shard_map/all_gather | solution.py:76
  77.1 9.2 %convolution_bitcast_fusion = f32[256,20]{0,1:T(8,128)S(1)} fusion(f32[20,4,2048]{2,0,1:T(8,128)S(1)} %all_gather.6, bf16[256,4,2048]{2,1,0:T(4,128)(2,1)} %param.7), kind=kOutput, calls=%fused_computation.56 | convolution fusion | flops 503316480 | bytes 4870144 | tf_op jit(solution)/shard_map/tic,kic->tk/dot_general | solution.py:80
  86.3 10.4 %psum.21 = f32[256,21]{0,1:T(8,128)S(1)} all-reduce(f32[256,21]{0,1:T(8,128)S(1)} %pad_maximum_fusion.5), channel_id=1, replica_groups=mesh['dp'=8,'mp'=4] {'mp'}, use_global_device_ids=true, to_apply=%region_1.2 | all-reduce | flops 5376 | bytes 43008 | tf_op jit(solution)/shard_map/psum | solution.py:22
  96.7 0.8 fusion.56
  97.5 0.7 slice_multiply_fusion.1
  98.2 0.1 fusion.74
  98.6 0.0 copy-start.4
  98.6 4.6 %copy.11 = bf16[256,4,2048]{2,0,1:T(8,128)(2,1)S(1)} copy(bf16[256,4,2048]{2,1,0:T(4,128)(2,1)} %param.7) | data formatting | bytes 8388608 | tf_op args[0]
  103.2 0.0 copy-done.4
  103.2 2.3 %fusion.13 = (f32[256,2048]{1,0:T(8,128)S(1)}, f32[256,2048]{1,0:T(8,128)S(1)}) fusion(bf16[256,2048]{1,0:T(8,128)(2,1)S(1)} %copy-done.4, f32[256]{0:T(256)S(1)} %bitcast.135, f32[256]{0:T(256)S(1)} %bitcast.136, f32[256]{0:T(256)S(1)} %bitcast.137, f32[256]{0:T(256)S(1)} %bitcast.130, f32[256]{0:T(256)S(1)} %bitcast.140, ...), kind=kLoop, calls=%fused_computation.35 | loop fusion | flops 12058624 | bytes 9447424 | tf_op jit(solution)/shard_map/add | solution.py:60
  105.5 0.0 copy-start
  105.5 2.3 %fusion.21 = (f32[256,2048]{1,0:T(8,128)S(1)}, f32[256,2048]{1,0:T(8,128)S(1)}) fusion(bf16[256,2048]{1,0:T(8,128)(2,1)S(1)} %copy-done.4, f32[256]{0:T(256)S(1)} %bitcast.126, f32[256]{0:T(256)S(1)} %bitcast.127, f32[256]{0:T(256)S(1)} %bitcast.128, f32[256]{0:T(256)S(1)} %bitcast.129, f32[256]{0:T(256)S(1)} %bitcast.139, ...), kind=kLoop, calls=%fused_computation.43 | loop fusion | flops 12058624 | bytes 9447424 | tf_op jit(solution)/shard_map/add | solution.py:60
  107.8 0.0 copy-start.2
  107.8 0.0 copy-start.3
  107.8 6.6 %fusion.29 = f32[256,24]{0,1:T(8,128)S(1)} fusion(f32[24,4,2048]{2,0,1:T(8,128)S(1)} %all_gather.7, f32[256,1,2048]{2,0,1:T(8,128)S(1)} %bitcast.111, f32[256,1,2048]{2,0,1:T(8,128)S(1)} %bitcast.108, f32[256,1,2048]{2,0,1:T(8,128)S(1)} %bitcast.105, f32[256,1,2048]{2,0,1:T(8,128)S(1)} %bitcast.102), kind=kOutput, calls=%fused_computation.55 | convolution fusion | flops 610271232 | bytes 9199616 | tf_op jit(solution)/shard_map/tic,kic->tk/dot_general | solution.py:97
  114.4 0.0 copy-done
  114.4 0.0 copy-done.2
  114.4 0.0 copy-done.3
  114.4 0.9 multiply_reduce_fusion
  115.3 10.8 %psum.22 = f32[256,25]{0,1:T(8,128)S(1)} all-reduce(f32[256,25]{0,1:T(8,128)S(1)} %pad_maximum_fusion.4), channel_id=1, replica_groups=mesh['dp'=8,'mp'=4] {'mp'}, use_global_device_ids=true, to_apply=%region_15.16 | all-reduce | flops 6400 | bytes 51200 | tf_op jit(solution)/shard_map/psum | solution.py:22
  126.1 1.4 fusion.45
  127.5 0.6 slice_multiply_fusion
  128.1 0.1 fusion.72
  128.2 0.1 divide_reduce_fusion
  128.3 0.1 divide_reduce_fusion.6
  128.4 0.1 divide_reduce_fusion.5
  128.5 0.1 divide_reduce_fusion.4
  128.7 0.1 divide_reduce_fusion.3
  128.8 0.1 divide_reduce_fusion.2
  128.9 0.7 exponential_divide_fusion
  129.6 0.6 pad_maximum_fusion.6
  130.2 0.0 copy-start.9
  130.2 4.9 %multiply_reduce_fusion.1 = (f32[256]{0:T(256)S(1)}, f32[256,2048]{1,0:T(8,128)}) fusion(f32[256,2048]{1,0:T(8,128)} %copy-done.3, f32[256]{0:T(256)S(1)} %bitcast.143, f32[256,2048]{1,0:T(8,128)} %copy-done.2, f32[256]{0:T(256)S(1)} %bitcast.144, f32[256,2048]{1,0:T(8,128)} %copy-done, f32[256]{0:T(256)S(1)} %bitcast.145, ...), kind=kLoop, calls=%fused_computation.49 | loop fusion | flops 4718336 | bytes 10490880 | tf_op jit(solution)/shard_map/reduce_sum | solution.py:113
  135.1 5.9 %psum.23 = f32[256]{0:T(256)S(1)} all-reduce(f32[256]{0:T(256)S(1)} %get-tuple-element.6), channel_id=1, replica_groups=mesh['dp'=8,'mp'=4] {'mp'}, use_global_device_ids=true, to_apply=%region_17.18 | all-reduce | flops 256 | bytes 2048 | tf_op jit(solution)/shard_map/psum | solution.py:113
  141.0 0.0 copy-start.1
  141.0 0.0 copy-done.9
  141.1 3.0 %multiply_convert_fusion = bf16[256,2048]{1,0:T(8,128)(2,1)} fusion(f32[256,2048]{1,0:T(8,128)} %get-tuple-element.7, f32[2048]{0:T(1024)S(1)} %copy-done.9, f32[256]{0:T(256)S(1)} %add_sqrt_fusion), kind=kLoop, calls=%fused_computation.48 | loop fusion | flops 1572864 | bytes 3154944 | tf_op jit(solution)/shard_map/convert_element_type | solution.py:114
  144.1 0.0 copy-done.1
  144.1 2.6 %fusion.27 = bf16[256,4,2048]{2,0,1:T(8,128)(2,1)S(1)} fusion(f32[256,1,2048]{2,0,1:T(8,128)} %bitcast.113, f32[256,1,2048]{2,0,1:T(8,128)} %bitcast.110, f32[256,1,2048]{2,0,1:T(8,128)S(1)} %bitcast.107, f32[256,1,2048]{2,0,1:T(8,128)S(1)} %bitcast.104), kind=kLoop, calls=%fused_computation.52 | loop fusion | flops 6291456 | bytes 12582912 | tf_op jit(solution)/shard_map/convert_element_type | solution.py:96
  146.7 5.3 %copy.17 = bf16[256,4,2048]{2,1,0:T(4,128)(2,1)} copy(bf16[256,4,2048]{2,0,1:T(8,128)(2,1)S(1)} %fusion.27) | data formatting | bytes 8388608
  (26 shorter events, 0.4 us)
Async XLA Ops:
  0.6 9.4 %copy-start.7 = (f32[44]{0:T(128)S(1)}, f32[44]{0:T(128)}, u32[]{:S(2)}) copy-start(f32[44]{0:T(128)} %param.11) | copy-start | bytes 532
  0.7 9.8 %copy-start.8 = (f32[5]{0:T(128)S(1)}, f32[5]{0:T(128)}, u32[]{:S(2)}) copy-start(f32[5]{0:T(128)} %param.12) | copy-start | bytes 64
  0.7 10.4 %copy-start.6 = (f32[20,4,256]{2,1,0:T(4,128)S(1)}, f32[20,4,256]{2,1,0:T(4,128)}, u32[]{:S(2)}) copy-start(f32[20,4,256]{2,1,0:T(4,128)} %param.9) | copy-start | bytes 245764
  0.7 10.4 %copy-start.5 = (f32[24,4,256]{2,1,0:T(4,128)S(1)}, f32[24,4,256]{2,1,0:T(4,128)}, u32[]{:S(2)}) copy-start(f32[24,4,256]{2,1,0:T(4,128)} %param.10) | copy-start | bytes 294916
  98.6 4.6 %copy-start.4 = (bf16[256,2048]{1,0:T(8,128)(2,1)S(1)}, bf16[256,2048]{1,0:T(8,128)(2,1)}, u32[]{:S(2)}) copy-start(bf16[256,2048]{1,0:T(8,128)(2,1)} %param.8) | copy-start | bytes 3145732
  105.5 8.9 %copy-start = (f32[256,2048]{1,0:T(8,128)}, f32[256,2048]{1,0:T(8,128)S(1)}, u32[]{:S(2)}) copy-start(f32[256,2048]{1,0:T(8,128)S(1)} %get-tuple-element.11) | copy-start | bytes 6291460
  107.8 6.6 %copy-start.2 = (f32[256,2048]{1,0:T(8,128)}, f32[256,2048]{1,0:T(8,128)S(1)}, u32[]{:S(2)}) copy-start(f32[256,2048]{1,0:T(8,128)S(1)} %get-tuple-element.12) | copy-start | bytes 6291460
  107.8 6.6 %copy-start.3 = (f32[256,2048]{1,0:T(8,128)}, f32[256,2048]{1,0:T(8,128)S(1)}, u32[]{:S(2)}) copy-start(f32[256,2048]{1,0:T(8,128)S(1)} %get-tuple-element.13) | copy-start | bytes 6291460
  130.2 10.8 %copy-start.9 = (f32[2048]{0:T(1024)S(1)}, f32[2048]{0:T(1024)}, u32[]{:S(2)}) copy-start(f32[2048]{0:T(1024)} %param.13) | copy-start | bytes 24580
  141.0 3.1 %copy-start.1 = (f32[256,2048]{1,0:T(8,128)S(1)}, f32[256,2048]{1,0:T(8,128)}, u32[]{:S(2)}) copy-start(f32[256,2048]{1,0:T(8,128)} %copy-done) | copy-start | bytes 6291460
where the time goes:
time: 152 us
  blocking collectives  93.1 us (61%)
  matrix products  25.2 us (17%)
  other arithmetic  21.8 us (14%)
  local copies, waits for them, and re-layouts  10.9 us (7%)
    all_gather x1, blocking collectives, local(): lax.all_gather(next_weight, 'dp', axis=2, tiled=True)  33.9 us
    all_gather x1, blocking collectives, local(): lax.all_gather(merge_weight, 'dp', axis=2, tiled=True)  32.1 us
    psum x2, blocking collectives, settle(): summed = lax.psum(columns, 'mp')  21.2 us
    unnamed x26, local copies, waits for them, and re-layouts  9.92 us
    dot_general x1, matrix products, local(): jnp.einsum('tic,tjc->tij', streams, streams, preferred_element_type=jnp.f...  9.4 us
    dot_general x1, matrix products, local(): jnp.einsum('tic,kic->tk', streams, merge_rows, precision=highest, preferr...  9.18 us
    dot_general x1, matrix products, local(): raw_next = jnp.einsum('tic,kic->tk', mixed, next_rows, precision=highest)  6.59 us
    psum x1, blocking collectives, local(): united_sq = lax.psum(jnp.sum(united * united, axis=1), 'mp')  5.92 us

commit v1 on v0

v1 whole, which is shorter than its diff:
```python
import functools

import jax
import jax.numpy as jnp
from jax import lax
from jax.experimental import pallas as pl
from jax.experimental.pallas import tpu as pltpu
from jax.sharding import PartitionSpec as P

BALANCE_ROUNDS = 6
EPS = 1e-06
FB = 256
GT = 64
F32 = jnp.float32
BF16 = jnp.bfloat16
MIB = 2**20

VMEM = pl.BlockSpec(memory_space=pltpu.VMEM)
SMEM = pl.BlockSpec(memory_space=pltpu.SMEM)
HBM = pl.BlockSpec(memory_space=pltpu.HBM)

PAIRS = [(i, j) for i in range(4) for j in range(i, 4)]


def _nt(a, b, precision=None):
    return lax.dot_general(
        a, b, (((1,), (1,)), ((), ())), precision=precision, preferred_element_type=F32
    )


def _split(x):
    hi = x.astype(BF16)
    return hi, (x - hi.astype(F32)).astype(BF16)


def _iota(shape, dim):
    return lax.broadcasted_iota(jnp.int32, shape, dim)


def _store_by_column(ref, rows, start):
    ref[0:start, :] = rows[0:start]
    for j in range(4):
        for i in range(4):
            source = start + 4 * j + i
            ref[start + 4 * i + j : start + 4 * i + j + 1, :] = rows[source : source + 1]
    if ref.shape[0] > start + 16:
        ref[start + 16 :, :] = rows[start + 16 :]


def pre_kernel(s_hbm, b_ref, sil_ref, sde_ref, g_ref, acc_ref, sems):
    tokens, width = b_ref.shape
    tiles = width // 128
    rows = 4 * tokens
    blocks = width // FB

    def copy(c):
        return pltpu.make_async_copy(
            s_hbm.at[:, :, pl.ds(pl.multiple_of(c * 128, 128), 128)], sil_ref.at[c], sems.at[c]
        )

    for c in range(tiles):
        copy(c).start()
    r, q = _iota((4 * GT, 4 * GT), 0), _iota((4 * GT, 4 * GT), 1)
    perm = jnp.where(q == 4 * (r % GT) + r // GT, 1.0, 0.0).astype(BF16)
    acc_ref[...] = jnp.zeros_like(acc_ref)

    def body(k, _):
        copy(2 * k).wait()
        copy(2 * k + 1).wait()
        left = sil_ref.at[2 * k].reshape(rows, 128)
        right = sil_ref.at[2 * k + 1].reshape(rows, 128)
        for g in range(tokens // GT):
            own = pl.ds(g * 4 * GT, 4 * GT)
            x = jnp.concatenate([left[own, :], right[own, :]], axis=1)
            y = jnp.dot(perm, x, preferred_element_type=F32)
            for i in range(4):
                sde_ref[k, i, pl.ds(g * GT, GT), :] = y[i * GT : (i + 1) * GT].astype(BF16)

        def grams(c, _):
            at = pl.ds(pl.multiple_of(c * 16, 16), 16)
            wide = [sde_ref[k, i, at, :].astype(F32) for i in range(4)]
            lanes = pl.ds(pl.multiple_of(k * FB, FB), FB)
            wide.append(b_ref[at, lanes].astype(F32))
            products = [wide[i] * wide[j] for i, j in PAIRS]
            products += [wide[i] * wide[4] for i in range(5)]
            for p, product in enumerate(products):
                acc_ref[p, at, :] += product[:, :128] + product[:, 128:]
            return 0

        lax.fori_loop(0, tokens // 16, grams, 0)
        return 0

    lax.fori_loop(0, blocks, body, 0)
    ones = jnp.ones((8, 128), F32)
    for p in range(15):
        g_ref[p : p + 1, :] = _nt(ones, acc_ref[p], lax.Precision.HIGHEST)[0:1]
    g_ref[15:16, :] = jnp.zeros((1, tokens), F32)


def pre(streams, branch):
    tokens, _, width = streams.shape
    return pl.pallas_call(
        pre_kernel,
        out_shape=(
            jax.ShapeDtypeStruct((width // 128, tokens, 4, 128), BF16),
            jax.ShapeDtypeStruct((width // FB, 4, tokens, FB), BF16),
            jax.ShapeDtypeStruct((16, tokens), F32),
        ),
        in_specs=[HBM, VMEM],
        out_specs=(VMEM, VMEM, VMEM),
        scratch_shapes=[
            pltpu.VMEM((15, tokens, 128), F32),
            pltpu.SemaphoreType.DMA((width // 128,)),
        ],
        compiler_params=pltpu.CompilerParams(vmem_limit_bytes=20 * MIB),
        cost_estimate=pl.CostEstimate(
            flops=12_000_000_000, bytes_accessed=10 * MIB, transcendentals=0
        ),
        name="pre",
    )(streams, branch)


def _owner(s, permuted):
    return jnp.bitwise_xor(lax.axis_index("dp"), s) if permuted else s


def raw_kernel(permuted, *refs):
    w_refs, (sde_ref, out_ref, wide_ref, lhs_ref) = refs[:-4], refs[-4:]
    count = w_refs[0].shape[0]
    pad = wide_ref.shape[1]
    blocks = sde_ref.shape[0]
    wide_ref[...] = jnp.zeros_like(wide_ref)
    for s in range(blocks):
        owner = _owner(s, permuted)
        for i in range(4):
            wide_ref[i, 0:count, :] = w_refs[s][:, i, :]
            hi, lo = _split(wide_ref[i])
            lhs_ref[owner, i, 0:pad, :] = hi
            lhs_ref[owner, i, pad : 2 * pad, :] = lo
    total = None
    for s in range(blocks):
        for i in range(4):
            part = _nt(lhs_ref[s, i], sde_ref[s, i])
            total = part if total is None else total + part
    rows = out_ref.shape[0]
    _store_by_column(out_ref, total[0:rows] + total[pad : pad + rows], 4)


def raw(weights, sde, permuted):
    blocks, _, tokens, _ = sde.shape
    return pl.pallas_call(
        functools.partial(raw_kernel, permuted),
        out_shape=jax.ShapeDtypeStruct((24, tokens), F32),
        in_specs=[VMEM] * (len(weights) + 1),
        out_specs=VMEM,
        scratch_shapes=[
            pltpu.VMEM((4, 32, FB), F32),
            pltpu.VMEM((blocks, 4, 64, FB), BF16),
        ],
        compiler_params=pltpu.CompilerParams(vmem_limit_bytes=12 * MIB),
        cost_estimate=pl.CostEstimate(
            flops=2_000_000_000, bytes_accessed=5 * MIB, transcendentals=0
        ),
        name="raw",
    )(*weights, sde)


def next_kernel(permuted, *refs):
    w_refs, (sde_ref, b_ref, out_ref, wide_ref, lhs_ref) = refs[:-5], refs[-5:]
    count = w_refs[0].shape[0]
    blocks = sde_ref.shape[0]
    rows = 4 * count
    for s in range(blocks):
        owner = _owner(s, permuted)
        for j in range(4):
            wide_ref[j * count : (j + 1) * count, :] = w_refs[s][:, j, :]
        hi, lo = _split(wide_ref[...])
        lhs_ref[owner, 0:rows, :] = hi
        lhs_ref[owner, rows : 2 * rows, :] = lo
    for i in range(5):
        total = None
        for s in range(blocks):
            right = sde_ref[s, i] if i < 4 else b_ref[:, s * FB : (s + 1) * FB]
            part = _nt(lhs_ref[s], right)
            total = part if total is None else total + part
        out_ref[i] = total[0:rows] + total[rows : 2 * rows]


def project_next(weights, sde, branch, permuted):
    blocks, _, tokens, _ = sde.shape
    rows = 4 * weights[0].shape[0]
    return pl.pallas_call(
        functools.partial(next_kernel, permuted),
        out_shape=jax.ShapeDtypeStruct((5, rows, tokens), F32),
        in_specs=[VMEM] * (len(weights) + 2),
        out_specs=VMEM,
        scratch_shapes=[
            pltpu.VMEM((rows, FB), F32),
            pltpu.VMEM((blocks, 2 * rows, FB), BF16),
        ],
        compiler_params=pltpu.CompilerParams(vmem_limit_bytes=14 * MIB),
        cost_estimate=pl.CostEstimate(
            flops=3_000_000_000, bytes_accessed=6 * MIB, transcendentals=0
        ),
        name="project_next",
    )(*weights, sde, branch)


def _balance(columns):
    for _ in range(BALANCE_ROUNDS):
        inverse = 1.0 / (columns[0] + columns[1] + columns[2] + columns[3])
        columns = [c * inverse for c in columns]
        columns = [c * (1.0 / jnp.sum(c, axis=0, keepdims=True)) for c in columns]
    return columns


def _sum4(refs, at):
    return (refs[0][at] + refs[1][at]) + (refs[2][at] + refs[3][at])


def first_kernel(features, *refs):
    r_refs, g_refs = refs[0:4], refs[4:8]
    bias_ref, scale_ref, pq_ref, coef_ref, next_ref, gram_ref = refs[8:]
    everything = (slice(None), slice(None))
    gram = _sum4(g_refs, everything)
    gram_ref[...] = gram
    squares = gram[0:1] + gram[4:5] + gram[7:8] + gram[9:10]
    inverse = 1.0 / jnp.sqrt(squares / features + EPS)
    raw_post = _sum4(r_refs, (slice(0, 4), slice(None)))
    post = 2.0 * jax.nn.sigmoid(scale_ref[0] * (raw_post * inverse) + bias_ref[0:4, :])
    columns = []
    for i in range(4):
        at = (slice(4 + 4 * i, 8 + 4 * i), slice(None))
        score = _sum4(r_refs, at) * inverse
        columns.append(jnp.exp(scale_ref[1] * score + bias_ref[at]))
    columns = _balance(columns)
    count = next_ref.shape[0]
    total = None
    for i in range(5):
        source = columns[i] if i < 4 else post
        coef_ref[4 * i : 4 * i + 4, :] = source
        for j in range(4):
            part = source[j : j + 1] * pq_ref[i, j * count : (j + 1) * count, :]
            total = part if total is None else total + part
    coef_ref[20:24, :] = jnp.zeros_like(coef_ref[20:24, :])
    _store_by_column(next_ref, total, 8)


def first(raws, grams, bias, scale, pq, features):
    tokens = pq.shape[2]
    return pl.pallas_call(
        functools.partial(first_kernel, features),
        out_shape=(
            jax.ShapeDtypeStruct((24, tokens), F32),
            jax.ShapeDtypeStruct((pq.shape[1] // 4, tokens), F32),
            jax.ShapeDtypeStruct((16, tokens), F32),
        ),
        in_specs=[VMEM] * 9 + [SMEM, VMEM],
        out_specs=(VMEM, VMEM, VMEM),
        compiler_params=pltpu.CompilerParams(vmem_limit_bytes=8 * MIB),
        cost_estimate=pl.CostEstimate(
            flops=1_000_000_000, bytes_accessed=MIB, transcendentals=20000
        ),
        name="first",
    )(*raws, *grams, bias, scale, pq)


def mix_kernel(coef_ref, sil_ref, b_ref, out_hbm, stage_ref, sems):
    tiles, tokens = sil_ref.shape[0], sil_ref.shape[1]
    rows = 4 * GT
    r32, m32 = _iota((rows, 32), 0), _iota((rows, 32), 1)
    keep = ((m32 % 4) == (r32 % 4)) & (m32 < 20)
    m_s, q_s = _iota((32, rows), 0), _iota((32, rows), 1)
    pick_stream = jnp.where((m_s // 4) == (q_s % 4), 1.0, 0.0).astype(BF16)
    m_b, q_b = _iota((32, GT), 0), _iota((32, GT), 1)
    pick_branch = jnp.where((m_b // 4) == 4, 1.0, 0.0).astype(BF16)
    same_stream = (_iota((rows, rows), 0) // 4) == (_iota((rows, rows), 1) // 4)
    same_branch = (_iota((rows, GT), 0) // 4) == _iota((rows, GT), 1)
    zero8 = jnp.zeros((8, tokens), F32)
    coef = jnp.concatenate([coef_ref[...], zero8], axis=0)
    parts = _split(coef)
    streams_of, branch_of = [], []
    for g in range(tokens // GT):
        half = g * GT // 128
        expand = jnp.where(
            _iota((rows, 128), 1) == (g * GT) % 128 + _iota((rows, 128), 0) // 4, 1.0, 0.0
        ).astype(BF16)
        for part in parts:
            held = _nt(expand, part[:, half * 128 : (half + 1) * 128])
            held = jnp.where(keep, held, 0.0).astype(BF16)
            wide = jnp.dot(held, pick_stream, preferred_element_type=F32)
            streams_of.append(jnp.where(same_stream, wide, 0.0).astype(BF16))
            wide = jnp.dot(held, pick_branch, preferred_element_type=F32)
            branch_of.append(jnp.where(same_branch, wide, 0.0).astype(BF16))

    def copy(c):
        return pltpu.make_async_copy(
            stage_ref.at[c],
            out_hbm.at[:, :, pl.ds(pl.multiple_of(c * 128, 128), 128)],
            sems.at[c],
        )

    def body(k, _):
        left = sil_ref.at[2 * k].reshape(4 * tokens, 128)
        right = sil_ref.at[2 * k + 1].reshape(4 * tokens, 128)
        out_left = stage_ref.at[2 * k].reshape(4 * tokens, 128)
        out_right = stage_ref.at[2 * k + 1].reshape(4 * tokens, 128)
        lanes = pl.ds(pl.multiple_of(k * FB, FB), FB)
        for g in range(tokens // GT):
            own = pl.ds(g * rows, rows)
            x = jnp.concatenate([left[own, :], right[own, :]], axis=1)
            b = b_ref[pl.ds(g * GT, GT), lanes]
            y = jnp.dot(streams_of[2 * g], x, preferred_element_type=F32)
            y += jnp.dot(streams_of[2 * g + 1], x, preferred_element_type=F32)
            y += jnp.dot(branch_of[2 * g], b, preferred_element_type=F32)
            y += jnp.dot(branch_of[2 * g + 1], b, preferred_element_type=F32)
            y = y.astype(BF16)
            out_left[own, :] = y[:, :128]
            out_right[own, :] = y[:, 128:]
        copy(2 * k).start()
        copy(2 * k + 1).start()
        return 0

    lax.fori_loop(0, tiles // 2, body, 0)
    for c in range(tiles):
        copy(c).wait()


def mix(coef, sil, branch):
    tiles, tokens = sil.shape[0], sil.shape[1]
    return pl.pallas_call(
        mix_kernel,
        out_shape=jax.ShapeDtypeStruct((tokens, 4, tiles * 128), BF16),
        in_specs=[VMEM, VMEM, VMEM],
        out_specs=HBM,
        scratch_shapes=[
            pltpu.VMEM((tiles, tokens, 4, 128), BF16),
            pltpu.SemaphoreType.DMA((tiles,)),
        ],
        compiler_params=pltpu.CompilerParams(vmem_limit_bytes=16 * MIB),
        cost_estimate=pl.CostEstimate(
            flops=5_000_000_000, bytes_accessed=8 * MIB, transcendentals=0
        ),
        name="mix",
    )(coef, sil, branch)


def second_kernel(features, *refs):
    r_refs = refs[0:4]
    coef_ref, gram_ref, bias_ref, scale_ref, sde_ref, b_ref, gain_ref = refs[4:11]
    out_ref, mix_ref, column_ref = refs[11:]
    tokens, width = b_ref.shape
    gram = gram_ref[...]
    columns = [coef_ref[4 * i : 4 * i + 4, :] for i in range(5)]

    def quadratic(terms):
        total = None
        for p, (i, j) in enumerate(PAIRS):
            part = terms[i] * terms[j] * gram[p : p + 1]
            part = part if i == j else 2.0 * part
            total = part if total is None else total + part
        for i in range(4):
            total = total + 2.0 * (terms[i] * terms[4]) * gram[10 + i : 11 + i]
        return total + terms[4] * terms[4] * gram[14:15]

    squares = jnp.maximum(jnp.sum(quadratic(columns), axis=0, keepdims=True), 0.0)
    inverse = 1.0 / jnp.sqrt(squares / features + EPS)
    everything = slice(None)
    pre_raw = _sum4(r_refs, (slice(0, 4), everything)) * inverse
    pre_next = jax.nn.sigmoid(scale_ref[2] * pre_raw + bias_ref[20:24, :])
    post_raw = _sum4(r_refs, (slice(4, 8), everything)) * inverse
    mix_ref[0:4, :] = 2.0 * jax.nn.sigmoid(scale_ref[3] * post_raw + bias_ref[24:28, :])
    following = []
    for i in range(4):
        score = _sum4(r_refs, (slice(8 + 4 * i, 12 + 4 * i), everything)) * inverse
        bias = bias_ref[28 + 4 * i : 32 + 4 * i, :]
        following.append(jnp.exp(scale_ref[4] * score + bias))
    following = _balance(following)
    for i in range(4):
        for j in range(4):
            mix_ref[4 + 4 * j + i : 5 + 4 * j + i, :] = following[i][j : j + 1]

    joint = [jnp.sum(pre_next * c, axis=0, keepdims=True) for c in columns]
    united = jnp.maximum(quadratic(joint), 0.0)
    root = 1.0 / jnp.sqrt(united / (features // 4) + EPS)
    stacked = jnp.concatenate([j * root for j in joint] + [jnp.zeros((3, tokens), F32)], axis=0)
    column_ref[:, 0:8] = stacked.T
    blocks = sde_ref.shape[0]

    def body(c, _):
        at = pl.ds(pl.multiple_of(c * 16, 16), 16)
        weights = [column_ref[at, i : i + 1] for i in range(5)]
        for k in range(blocks):
            lanes = pl.ds(k * FB, FB)
            total = weights[4] * b_ref[at, lanes].astype(F32)
            for i in range(4):
                total = total + weights[i] * sde_ref[k, i, at, :].astype(F32)
            out_ref[at, lanes] = (total * gain_ref[:, lanes]).astype(BF16)
        return 0

    lax.fori_loop(0, tokens // 16, body, 0)


def second(raws, coef, gram, bias, scale, sde, branch, gain, features):
    tokens, width = branch.shape
    return pl.pallas_call(
        functools.partial(second_kernel, features),
        out_shape=(
            jax.ShapeDtypeStruct((tokens, width), BF16),
            jax.ShapeDtypeStruct((20, tokens), F32),
        ),
        in_specs=[VMEM] * 7 + [SMEM] + [VMEM] * 3,
        out_specs=(VMEM, VMEM),
        scratch_shapes=[pltpu.VMEM((tokens, 128), F32)],
        compiler_params=pltpu.CompilerParams(vmem_limit_bytes=14 * MIB),
        cost_estimate=pl.CostEstimate(
            flops=3_000_000_000, bytes_accessed=6 * MIB, transcendentals=20000
        ),
        name="second",
    )(*raws, coef, gram, bias, scale, sde, branch, gain)


def _swap(x, axis, count, s):
    return lax.ppermute(x, axis, [(i, i ^ s) for i in range(count)])


def gather_blocks(weight, count, width):
    if weight.shape[2] == FB and count & (count - 1) == 0 and count * FB == width:
        even = {0: weight}
        for s in reversed(range(2, count, 2)):
            even[s] = _swap(weight, "dp", count, s)
        blocks = [None] * count
        for s in range(0, count, 2):
            blocks[s] = even[s]
            blocks[s + 1] = _swap(even[s], "dp", count, 1)
        return blocks, True
    whole = lax.all_gather(weight, "dp", axis=2, tiled=True)
    return [whole[:, :, k * FB : (k + 1) * FB] for k in range(width // FB)], False


def everyone(x, count):
    return [x] + [_swap(x, "mp", count, s) for s in range(1, count)]


def solution(mesh):
    n_dp, n_mp = mesh.shape["dp"], mesh.shape["mp"]

    def local(streams, branch, merge_weight, next_weight, blend_bias, blend_scale, norm_gain):
        tokens, count, width = streams.shape
        features = count * width * n_mp
        merge_blocks, permuted = gather_blocks(merge_weight, n_dp, width)
        next_blocks, _ = gather_blocks(next_weight, n_dp, width)
        by_column = [blend_bias[:4], blend_bias[4:20].reshape(4, 4).T.reshape(16)]
        by_column += [blend_bias[20:28], blend_bias[28:].reshape(4, 4).T.reshape(16)]
        bias = jnp.concatenate(by_column + [jnp.zeros((4,), F32)])
        bias = jnp.broadcast_to(bias[:, None], (48, tokens))
        gain = norm_gain[None, :]
        sil, sde, gram = pre(streams, branch)
        grams = everyone(gram, n_mp)
        raws = everyone(raw(merge_blocks, sde, permuted), n_mp)
        pq = project_next(next_blocks, sde, branch, permuted)
        coef, next_raw, gram_sum = first(raws, grams, bias, blend_scale, pq, features)
        next_raws = everyone(next_raw, n_mp)
        streams_out = mix(coef, sil, branch)
        branch_in, next_mix = second(
            next_raws, coef, gram_sum, bias, blend_scale, sde, branch, gain, features
        )
        return streams_out, branch_in, next_mix.T

    placed = (
        P("dp", None, "mp"),
        P("dp", "mp"),
        P(None, None, ("mp", "dp")),
        P(None, None, ("mp", "dp")),
        P(),
        P(),
        P("mp"),
    )
    return jax.shard_map(
        local,
        mesh=mesh,
        in_specs=placed,
        out_specs=(P("dp", None, "mp"), P("dp", "mp"), P("dp", None)),
        check_vma=False,
    )
```

time: 152 us -> 67.4 us (0.44)
  blocking collectives: 93.1 us -> 0 us
  Pallas kernels: 0 us -> 27.2 us
  matrix products: 25.2 us -> 0 us
  starting transfers between devices: 0 us -> 24 us
  other arithmetic: 21.8 us -> 0 us
  waiting for transfers between devices: 0 us -> 4.63 us
    all_gather x2 -> x0, blocking collectives: 66 us -> none  [the longest x1 33.9 us: local(): lax.all_gather(next_weight, 'dp', axis=2, tiled=True)]
    pallas_call x0 -> x6, Pallas kernels: none -> 27.2 us  [the longest x1 10 us: pre(): pl.pallas_call(pre_kernel, out_shape=(jax.ShapeDtypeStruct((width // 128,...]
    psum x3 -> x0, blocking collectives: 27.1 us -> none  [the longest x2 21.2 us: settle(): summed = lax.psum(columns, 'mp')]
    dot_general x3 -> x0, matrix products: 25.2 us -> none  [the longest x1 9.4 us: local(): jnp.einsum('tic,tjc->tij', streams, streams, preferred_element_type=jnp.f...]
    ppermute x0 -> x23, starting transfers between devices: none -> 24 us  [_swap(): return lax.ppermute(x, axis, [(i, i ^ s) for i in range(count)])]
    reduce_sum x6 -> x0, other arithmetic: 6.05 us -> none  [the longest x1 4.88 us: local(): united_sq = lax.psum(jnp.sum(united * united, axis=1), 'mp')]
    convert_element_type x2 -> x0, other arithmetic: 5.65 us -> none  [the longest x1 3.04 us: local(): (united / jnp.sqrt(united_sq / D + epsilon)[:, None] * norm_gain).astype(...]
    ppermute x0 -> x23, waiting for transfers between devices: none -> 4.63 us  [_swap(): return lax.ppermute(x, axis, [(i, i ^ s) for i in range(count)])]
  transfers between devices with their start and end apart: 0 -> 23, of which waited for: 0 -> 3; matrix products, arithmetic and copies ran while one was open for 0% -> 1% of each run, Pallas kernels for 0% -> 34%
where the time goes in v1:
time: 67.4 us; the launch traced here: 67.1 us
  Pallas kernels  27.2 us (40%)
  starting transfers between devices  24 us (36%)
  local copies, waits for them, and re-layouts  10.4 us (15%)
  waiting for transfers between devices  4.63 us (7%)
  between operations  0.81 us (1%)
    ppermute x23, starting transfers between devices, _swap(): return lax.ppermute(x, axis, [(i, i ^ s) for i in range(count)])  24 us
    pallas_call x1, Pallas kernels, pre(): pl.pallas_call(pre_kernel, out_shape=(jax.ShapeDtypeStruct((width // 128,...  10 us
    unnamed x26, local copies, waits for them, and re-layouts  9.62 us
    pallas_call x1, Pallas kernels, mix(): pl.pallas_call(mix_kernel, out_shape=jax.ShapeDtypeStruct((tokens, 4, til...  8.66 us
    ppermute x23, waiting for transfers between devices, _swap(): return lax.ppermute(x, axis, [(i, i ^ s) for i in range(count)])  4.63 us
    pallas_call x1, Pallas kernels, second(): pl.pallas_call(functools.partial(second_kernel, features), out_shape=(jax...  3.95 us
    pallas_call x1, Pallas kernels, project_next(): pl.pallas_call(functools.partial(next_kernel, permuted), out_shape=jax.Sh...  2.13 us
    pallas_call x1, Pallas kernels, raw(): pl.pallas_call(functools.partial(raw_kernel, permuted), out_shape=jax.Sha...  1.68 us
  transfers between devices with their start and end apart: 23, of which 3 were waited for; matrix products, arithmetic and copies ran while one was open for 1% of the time, Pallas kernels for 34%

profile of v1, /device:TPU:0, one launch (start us, length us, event | category | flops | bytes accessed | tf_op | source)
XLA Modules:
  0.0 67.1 jit_solution(13358081155355835601)
XLA Ops:
  0.6 3.1 %collective-permute-start.1 = (f32[20,4,256]{2,1,0:T(4,128)}, f32[20,4,256]{2,1,0:T(4,128)S(1)}, u32[]{:S(2)}, u32[]{:S(2)}) collective-permute-start(f32[20,4,256]{2,1,0:T(4,128)} %refs_0_.2), channel_id=1, source_target_pairs={{0,8},{4,12},{8,0},{12,4},{16,24},{20,28},{24,16},{28,20},{1,9},{5... | collective-permute-start | bytes 245768 | tf_op jit(solution)/shard_map/ppermute | solution.py:424
  3.7 2.6 %collective-permute-start.3 = (f32[20,4,256]{2,1,0:T(4,128)}, f32[20,4,256]{2,1,0:T(4,128)S(1)}, u32[]{:S(2)}, u32[]{:S(2)}) collective-permute-start(f32[20,4,256]{2,1,0:T(4,128)} %refs_0_.2), channel_id=1, source_target_pairs={{0,16},{4,20},{8,24},{12,28},{16,0},{20,4},{24,8},{28,12},{1,17},{... | collective-permute-start | bytes 245768 | tf_op jit(solution)/shard_map/ppermute | solution.py:424
  6.3 0.0 collective-permute-start.5
  6.3 1.7 %collective-permute-start = (f32[20,4,256]{2,1,0:T(4,128)}, f32[20,4,256]{2,1,0:T(4,128)S(1)}, u32[]{:S(2)}, u32[]{:S(2)}) collective-permute-start(f32[20,4,256]{2,1,0:T(4,128)} %refs_0_.2), channel_id=1, source_target_pairs={{0,4},{4,0},{8,12},{12,8},{16,20},{20,16},{24,28},{28,24},{1,5},{5... | collective-permute-start | bytes 245768 | tf_op jit(solution)/shard_map/ppermute | solution.py:424
  8.1 0.7 %collective-permute-start.14 = (f32[24,4,256]{2,1,0:T(4,128)}, f32[24,4,256]{2,1,0:T(4,128)S(1)}, u32[]{:S(2)}, u32[]{:S(2)}) collective-permute-start(f32[24,4,256]{2,1,0:T(4,128)} %refs_0_.3), channel_id=1, source_target_pairs={{0,8},{4,12},{8,0},{12,4},{16,24},{20,28},{24,16},{28,20},{1,9},{5... | collective-permute-start | bytes 294920 | tf_op jit(solution)/shard_map/ppermute | solution.py:424
  8.8 2.2 %copy-done = bf16[256,4,2048]{2,1,0:T(4,128)(2,1)S(1)} copy-done((bf16[256,4,2048]{2,1,0:T(4,128)(2,1)S(1)}, bf16[256,4,2048]{2,1,0:T(4,128)(2,1)}, u32[]{:S(2)}) %copy-start) | copy-done | bytes 4194328
  10.9 1.2 %copy-done.1 = bf16[256,2048]{1,0:T(8,128)(2,1)S(1)} copy-done((bf16[256,2048]{1,0:T(8,128)(2,1)S(1)}, bf16[256,2048]{1,0:T(8,128)(2,1)}, u32[]{:S(2)}) %copy-start.1) | copy-done | bytes 1048600
  12.2 10.0 %pre.1 = (bf16[16,256,4,128]{3,2,1,0:T(4,128)(2,1)S(1)}, bf16[8,4,256,256]{3,2,1,0:T(8,128)(2,1)S(1)}, f32[16,256]{1,0:T(8,128)S(1)}) custom-call(bf16[256,4,2048]{2,1,0:T(4,128)(2,1)S(1)} %copy-done, bf16[256,2048]{1,0:T(8,128)(2,1)S(1)} %copy-done.1), custom_call_target="tpu_custom_call" | custom-call | flops 12000000000 | bytes 10485760 | tf_op jit(solution)/shard_map/pre/pallas_call | solution.py:102
  22.2 0.0 copy-start.7
  22.2 2.0 %copy-done.7 = bf16[8,4,256,256]{3,2,1,0:T(8,128)(2,1)} copy-done((bf16[8,4,256,256]{3,2,1,0:T(8,128)(2,1)}, bf16[8,4,256,256]{3,2,1,0:T(8,128)(2,1)S(1)}, u32[]{:S(2)}) %copy-start.7) | copy-done | bytes 4194328
  24.2 2.0 %copy-done.10 = bf16[16,256,4,128]{3,2,1,0:T(4,128)(2,1)} copy-done((bf16[16,256,4,128]{3,2,1,0:T(4,128)(2,1)}, bf16[16,256,4,128]{3,2,1,0:T(4,128)(2,1)S(1)}, u32[]{:S(2)}) %copy-start.10) | copy-done | bytes 4194328
  26.2 0.0 collective-permute-done.1.refs_2_
  26.2 3.5 %collective-permute-start.16 = (f32[24,4,256]{2,1,0:T(4,128)S(1)}, f32[24,4,256]{2,1,0:T(4,128)S(1)}, u32[]{:S(2)}, u32[]{:S(2)}) collective-permute-start(f32[24,4,256]{2,1,0:T(4,128)S(1)} %copy-done.3), channel_id=1, source_target_pairs={{0,16},{4,20},{8,24},{12,28},{16,0},{20,4},{24,8},{28,12},{1,17},{... | collective-permute-start | bytes 294920 | tf_op jit(solution)/shard_map/ppermute | solution.py:424
  29.8 0.0 collective-permute-done.3.refs_4_
  29.8 0.2 collective-permute-start.18
  30.0 0.0 collective-permute-done.5.refs_6_
  30.0 0.4 collective-permute-start.2
  30.4 0.0 collective-permute-done.refs_1_
  30.4 1.7 %collective-permute-start.4 = (f32[20,4,256]{2,1,0:T(4,128)S(1)}, f32[20,4,256]{2,1,0:T(4,128)S(1)}, u32[]{:S(2)}, u32[]{:S(2)}) collective-permute-start(f32[20,4,256]{2,1,0:T(4,128)S(1)} %collective-permute-done.3.refs_4_), channel_id=1, source_target_pairs={{0,4},{4,0},{8,12},{12,8},{16,20},{20,16},{24,28},{28,24},{1,5},{5... | collective-permute-start | bytes 245768 | tf_op jit(solution)/shard_map/ppermute | solution.py:424
  32.0 0.0 collective-permute-done.14.refs_2_
  32.0 0.4 collective-permute-start.6
  32.4 0.1 fusion
  32.5 0.1 slice.30
  32.5 0.1 reshape.35
  32.6 0.1 copy.10
  32.7 0.1 reshape.36
  32.8 0.1 reshape.37
  32.9 0.1 copy.11
  33.0 0.1 reshape.38
  33.1 0.1 concatenate.3
  33.2 3.3 %collective-permute-done.16.refs_4_ = f32[24,4,256]{2,1,0:T(4,128)S(1)} collective-permute-done((f32[24,4,256]{2,1,0:T(4,128)S(1)}, f32[24,4,256]{2,1,0:T(4,128)S(1)}, u32[]{:S(2)}, u32[]{:S(2)}) %collective-permute-start.16) | collective-permute-done | bytes 98336 | tf_op jit(solution)/shard_map/ppermute | solution.py:424
  36.4 0.5 collective-permute-start.13
  36.9 0.0 collective-permute-done.18.refs_6_
  36.9 0.0 collective-permute-start.10
  36.9 0.0 collective-permute-done.2.refs_3_
  37.0 1.6 %collective-permute-start.15 = (f32[24,4,256]{2,1,0:T(4,128)S(1)}, f32[24,4,256]{2,1,0:T(4,128)S(1)}, u32[]{:S(2)}, u32[]{:S(2)}) collective-permute-start(f32[24,4,256]{2,1,0:T(4,128)S(1)} %collective-permute-done.14.refs_2_), channel_id=1, source_target_pairs={{0,4},{4,0},{8,12},{12,8},{16,20},{20,16},{24,28},{28,24},{1,5},{5... | collective-permute-start | bytes 294920 | tf_op jit(solution)/shard_map/ppermute | solution.py:424
  38.5 0.0 collective-permute-done.4.refs_5_
  38.5 0.5 collective-permute-start.17
  39.0 0.0 collective-permute-done.6.refs_7_
  39.1 1.5 %collective-permute-start.19 = (f32[24,4,256]{2,1,0:T(4,128)S(1)}, f32[24,4,256]{2,1,0:T(4,128)S(1)}, u32[]{:S(2)}, u32[]{:S(2)}) collective-permute-start(f32[24,4,256]{2,1,0:T(4,128)S(1)} %collective-permute-done.18.refs_6_), channel_id=1, source_target_pairs={{0,4},{4,0},{8,12},{12,8},{16,20},{20,16},{24,28},{28,24},{1,5},{5... | collective-permute-start | bytes 294920 | tf_op jit(solution)/shard_map/ppermute | solution.py:424
  40.6 2.2 %copy-done.8 = bf16[8,4,256,256]{3,2,1,0:T(8,128)(2,1)S(1)} copy-done((bf16[8,4,256,256]{3,2,1,0:T(8,128)(2,1)S(1)}, bf16[8,4,256,256]{3,2,1,0:T(8,128)(2,1)}, u32[]{:S(2)}) %copy-start.8) | copy-done | bytes 4194328
  42.8 1.7 %raw.1.refs_0_ = f32[24,256]{1,0:T(8,128)S(1)} custom-call(f32[20,4,256]{2,1,0:T(4,128)S(1)} %copy-done.4, f32[20,4,256]{2,1,0:T(4,128)S(1)} %collective-permute-done.refs_1_, f32[20,4,256]{2,1,0:T(4,128)S(1)} %collective-permute-done.1.refs_2_, f32[20,4,256]{2,1,0:T(4,128)S(1)} %collective-permute-done.2.refs_3_, ...), custom_call_target="tpu_custom_call" | custom-call | flops 2000000000 | bytes 5242880 | tf_op jit(solution)/shard_map/raw/pallas_call | solution.py:151
  44.5 0.0 copy-start.6
  44.5 0.0 collective-permute-done.10.refs_5_
  44.5 1.6 %collective-permute-start.11 = (f32[16,256]{1,0:T(8,128)S(1)}, f32[16,256]{1,0:T(8,128)S(1)}, u32[]{:S(2)}, u32[]{:S(2)}) collective-permute-start(f32[16,256]{1,0:T(8,128)S(1)} %get-tuple-element.12.refs_4_), channel_id=1, source_target_pairs={{0,2},{1,3},{2,0},{3,1},{4,6},{5,7},{6,4},{7,5},{8,10},{9,11},{10,... | collective-permute-start | bytes 49160 | tf_op jit(solution)/shard_map/ppermute | solution.py:424
  46.0 0.0 collective-permute-done.13.refs_1_
  46.1 0.6 collective-permute-start.7
  46.7 0.0 collective-permute-done.17.refs_5_
  46.7 1.5 %collective-permute-start.8 = (f32[24,256]{1,0:T(8,128)S(1)}, f32[24,256]{1,0:T(8,128)S(1)}, u32[]{:S(2)}, u32[]{:S(2)}) collective-permute-start(f32[24,256]{1,0:T(8,128)S(1)} %raw.1.refs_0_), channel_id=1, source_target_pairs={{0,2},{1,3},{2,0},{3,1},{4,6},{5,7},{6,4},{7,5},{8,10},{9,11},{10,... | collective-permute-start | bytes 73736 | tf_op jit(solution)/shard_map/ppermute | solution.py:424
  48.2 0.0 collective-permute-done.19.refs_7_
  48.2 0.0 collective-permute-start.9
  48.2 2.1 %project_next.1.refs_10_ = f32[5,96,256]{2,1,0:T(8,128)S(1)} custom-call(f32[24,4,256]{2,1,0:T(4,128)S(1)} %copy-done.3, f32[24,4,256]{2,1,0:T(4,128)S(1)} %collective-permute-done.13.refs_1_, f32[24,4,256]{2,1,0:T(4,128)S(1)} %collective-permute-done.14.refs_2_, f32[24,4,256]{2,1,0:T(4,128)S(1)} %collective-permute-done.15.refs_3_, ...), custom_call_target="tpu_custom_call" | custom-call | flops 3000000000 | bytes 6291456 | tf_op jit(solution)/shard_map/project_next/pallas_call | solution.py:192
  50.4 0.0 collective-permute-done.12.refs_7_
  50.4 0.0 collective-permute-done.7.refs_1_
  50.4 0.2 collective-permute-done.8.refs_2_
  50.5 1.1 %collective-permute-done.9.refs_3_ = f32[24,256]{1,0:T(8,128)S(1)} collective-permute-done((f32[24,256]{1,0:T(8,128)S(1)}, f32[24,256]{1,0:T(8,128)S(1)}, u32[]{:S(2)}, u32[]{:S(2)}) %collective-permute-start.9) | collective-permute-done | bytes 24608 | tf_op jit(solution)/shard_map/ppermute | solution.py:424
  51.7 0.1 broadcast_in_dim.4.refs_8_.refs_6_
  51.8 0.8 %first.1 = (f32[24,256]{1,0:T(8,128)S(1)}, f32[24,256]{1,0:T(8,128)S(1)}, f32[16,256]{1,0:T(8,128)S(1)}) custom-call(f32[24,256]{1,0:T(8,128)S(1)} %raw.1.refs_0_, f32[24,256]{1,0:T(8,128)S(1)} %collective-permute-done.7.refs_1_, f32[24,256]{1,0:T(8,128)S(1)} %collective-permute-done.8.refs_2_, f32[24,256]{1,0:T(8,128)S(1)} %collective-permute-done.9.refs_3_, ...), custom_call_target="tpu_custom_call" | custom-call | flops 1000000000 | bytes 1048576 | tf_op jit(solution)/shard_map/first/pallas_call | solution.py:251
  52.5 0.1 collective-permute-start.20
  52.7 0.8 %collective-permute-start.21 = (f32[24,256]{1,0:T(8,128)S(1)}, f32[24,256]{1,0:T(8,128)S(1)}, u32[]{:S(2)}, u32[]{:S(2)}) collective-permute-start(f32[24,256]{1,0:T(8,128)S(1)} %get-tuple-element.15.refs_0_), channel_id=1, source_target_pairs={{0,2},{1,3},{2,0},{3,1},{4,6},{5,7},{6,4},{7,5},{8,10},{9,11},{10,... | collective-permute-start | bytes 73736 | tf_op jit(solution)/shard_map/ppermute | solution.py:424
  53.5 1.0 %collective-permute-start.22 = (f32[24,256]{1,0:T(8,128)S(1)}, f32[24,256]{1,0:T(8,128)S(1)}, u32[]{:S(2)}, u32[]{:S(2)}) collective-permute-start(f32[24,256]{1,0:T(8,128)S(1)} %get-tuple-element.15.refs_0_), channel_id=1, source_target_pairs={{0,3},{1,2},{2,1},{3,0},{4,7},{5,6},{6,5},{7,4},{8,11},{9,10},{10,... | collective-permute-start | bytes 73736 | tf_op jit(solution)/shard_map/ppermute | solution.py:424
  54.5 8.7 %mix.1 = bf16[256,4,2048]{2,1,0:T(4,128)(2,1)} custom-call(f32[24,256]{1,0:T(8,128)S(1)} %get-tuple-element.13.coef_ref.refs_4_, bf16[16,256,4,128]{3,2,1,0:T(4,128)(2,1)S(1)} %copy-done.11, bf16[256,2048]{1,0:T(8,128)(2,1)S(1)} %copy-done.2), custom_call_target="tpu_custom_call" | custom-call | flops 5000000000 | bytes 8388608 | tf_op jit(solution)/shard_map/mix/pallas_call | solution.py:331
  63.2 0.0 collective-permute-done.21.refs_2_
  63.2 4.0 %second.1 = (bf16[256,2048]{1,0:T(8,128)(2,1)}, f32[20,256]{1,0:T(8,128)}) custom-call(f32[24,256]{1,0:T(8,128)S(1)} %get-tuple-element.15.refs_0_, f32[24,256]{1,0:T(8,128)S(1)} %collective-permute-done.20.refs_1_, f32[24,256]{1,0:T(8,128)S(1)} %collective-permute-done.21.refs_2_, f32[24,256]{1,0:T(8,128)S(1)} %collective-permute-done.22.refs_3_, ...), custom_call_target="tpu_custom_call" | custom-call | flops 3000000000 | bytes 6291456 | tf_op jit(solution)/shard_map/second/pallas_call | solution.py:406
  (25 shorter events, 0.0 us)
Async XLA Ops:
  0.6 25.6 %collective-permute-start.1 = (f32[20,4,256]{2,1,0:T(4,128)}, f32[20,4,256]{2,1,0:T(4,128)S(1)}, u32[]{:S(2)}, u32[]{:S(2)}) collective-permute-start(f32[20,4,256]{2,1,0:T(4,128)} %refs_0_.2), channel_id=1, source_target_pairs={{0,8},{4,12},{8,0},{12,4},{16,24},{20,28},{24,16},{28,20},{1,9},{5... | collective-permute-start | bytes 245768 | tf_op jit(solution)/shard_map/ppermute | solution.py:424
  3.7 26.0 %collective-permute-start.3 = (f32[20,4,256]{2,1,0:T(4,128)}, f32[20,4,256]{2,1,0:T(4,128)S(1)}, u32[]{:S(2)}, u32[]{:S(2)}) collective-permute-start(f32[20,4,256]{2,1,0:T(4,128)} %refs_0_.2), channel_id=1, source_target_pairs={{0,16},{4,20},{8,24},{12,28},{16,0},{20,4},{24,8},{28,12},{1,17},{... | collective-permute-start | bytes 245768 | tf_op jit(solution)/shard_map/ppermute | solution.py:424
  6.3 23.7 %collective-permute-start.5 = (f32[20,4,256]{2,1,0:T(4,128)}, f32[20,4,256]{2,1,0:T(4,128)S(1)}, u32[]{:S(2)}, u32[]{:S(2)}) collective-permute-start(f32[20,4,256]{2,1,0:T(4,128)} %refs_0_.2), channel_id=1, source_target_pairs={{0,24},{4,28},{8,16},{12,20},{16,8},{20,12},{24,0},{28,4},{1,25},{... | collective-permute-start | bytes 245768 | tf_op jit(solution)/shard_map/ppermute | solution.py:424
  6.3 24.0 %collective-permute-start = (f32[20,4,256]{2,1,0:T(4,128)}, f32[20,4,256]{2,1,0:T(4,128)S(1)}, u32[]{:S(2)}, u32[]{:S(2)}) collective-permute-start(f32[20,4,256]{2,1,0:T(4,128)} %refs_0_.2), channel_id=1, source_target_pairs={{0,4},{4,0},{8,12},{12,8},{16,20},{20,16},{24,28},{28,24},{1,5},{5... | collective-permute-start | bytes 245768 | tf_op jit(solution)/shard_map/ppermute | solution.py:424
  8.1 24.0 %collective-permute-start.14 = (f32[24,4,256]{2,1,0:T(4,128)}, f32[24,4,256]{2,1,0:T(4,128)S(1)}, u32[]{:S(2)}, u32[]{:S(2)}) collective-permute-start(f32[24,4,256]{2,1,0:T(4,128)} %refs_0_.3), channel_id=1, source_target_pairs={{0,8},{4,12},{8,0},{12,4},{16,24},{20,28},{24,16},{28,20},{1,9},{5... | collective-permute-start | bytes 294920 | tf_op jit(solution)/shard_map/ppermute | solution.py:424
  8.8 2.2 %copy-start = (bf16[256,4,2048]{2,1,0:T(4,128)(2,1)S(1)}, bf16[256,4,2048]{2,1,0:T(4,128)(2,1)}, u32[]{:S(2)}) copy-start(bf16[256,4,2048]{2,1,0:T(4,128)(2,1)} %s_hbm.1) | copy-start | bytes 12582916
  10.9 1.2 %copy-start.1 = (bf16[256,2048]{1,0:T(8,128)(2,1)S(1)}, bf16[256,2048]{1,0:T(8,128)(2,1)}, u32[]{:S(2)}) copy-start(bf16[256,2048]{1,0:T(8,128)(2,1)} %refs_9_.5) | copy-start | bytes 3145732
  12.2 14.1 %copy-start.3 = (f32[24,4,256]{2,1,0:T(4,128)S(1)}, f32[24,4,256]{2,1,0:T(4,128)}, u32[]{:S(2)}) copy-start(f32[24,4,256]{2,1,0:T(4,128)} %refs_0_.3) | copy-start | bytes 294916
  12.2 20.2 %copy-start.12 = (f32[44]{0:T(128)S(1)}, f32[44]{0:T(128)}, u32[]{:S(2)}) copy-start(f32[44]{0:T(128)} %param.11) | copy-start | bytes 532
  12.2 28.4 %copy-start.4 = (f32[20,4,256]{2,1,0:T(4,128)S(1)}, f32[20,4,256]{2,1,0:T(4,128)}, u32[]{:S(2)}) copy-start(f32[20,4,256]{2,1,0:T(4,128)} %refs_0_.2) | copy-start | bytes 245764
  22.2 2.0 %copy-start.7 = (bf16[8,4,256,256]{3,2,1,0:T(8,128)(2,1)}, bf16[8,4,256,256]{3,2,1,0:T(8,128)(2,1)S(1)}, u32[]{:S(2)}) copy-start(bf16[8,4,256,256]{3,2,1,0:T(8,128)(2,1)S(1)} %get-tuple-element.11.refs_8_) | copy-start | bytes 12582916
  24.2 2.0 %copy-start.10 = (bf16[16,256,4,128]{3,2,1,0:T(4,128)(2,1)}, bf16[16,256,4,128]{3,2,1,0:T(4,128)(2,1)S(1)}, u32[]{:S(2)}) copy-start(bf16[16,256,4,128]{3,2,1,0:T(4,128)(2,1)S(1)} %get-tuple-element.14.sil_ref) | copy-start | bytes 12582916
  26.2 22.0 %copy-start.2 = (bf16[256,2048]{1,0:T(8,128)(2,1)S(1)}, bf16[256,2048]{1,0:T(8,128)(2,1)}, u32[]{:S(2)}) copy-start(bf16[256,2048]{1,0:T(8,128)(2,1)} %refs_9_.5) | copy-start | bytes 3145732
  26.2 10.2 %collective-permute-start.16 = (f32[24,4,256]{2,1,0:T(4,128)S(1)}, f32[24,4,256]{2,1,0:T(4,128)S(1)}, u32[]{:S(2)}, u32[]{:S(2)}) collective-permute-start(f32[24,4,256]{2,1,0:T(4,128)S(1)} %copy-done.3), channel_id=1, source_target_pairs={{0,16},{4,20},{8,24},{12,28},{16,0},{20,4},{24,8},{28,12},{1,17},{... | collective-permute-start | bytes 294920 | tf_op jit(solution)/shard_map/ppermute | solution.py:424
  29.8 7.2 %collective-permute-start.18 = (f32[24,4,256]{2,1,0:T(4,128)S(1)}, f32[24,4,256]{2,1,0:T(4,128)S(1)}, u32[]{:S(2)}, u32[]{:S(2)}) collective-permute-start(f32[24,4,256]{2,1,0:T(4,128)S(1)} %copy-done.3), channel_id=1, source_target_pairs={{0,24},{4,28},{8,16},{12,20},{16,8},{20,12},{24,0},{28,4},{1,25},{... | collective-permute-start | bytes 294920 | tf_op jit(solution)/shard_map/ppermute | solution.py:424
  30.0 6.9 %collective-permute-start.2 = (f32[20,4,256]{2,1,0:T(4,128)S(1)}, f32[20,4,256]{2,1,0:T(4,128)S(1)}, u32[]{:S(2)}, u32[]{:S(2)}) collective-permute-start(f32[20,4,256]{2,1,0:T(4,128)S(1)} %collective-permute-done.1.refs_2_), channel_id=1, source_target_pairs={{0,4},{4,0},{8,12},{12,8},{16,20},{20,16},{24,28},{28,24},{1,5},{5... | collective-permute-start | bytes 245768 | tf_op jit(solution)/shard_map/ppermute | solution.py:424
  30.4 8.2 %collective-permute-start.4 = (f32[20,4,256]{2,1,0:T(4,128)S(1)}, f32[20,4,256]{2,1,0:T(4,128)S(1)}, u32[]{:S(2)}, u32[]{:S(2)}) collective-permute-start(f32[20,4,256]{2,1,0:T(4,128)S(1)} %collective-permute-done.3.refs_4_), channel_id=1, source_target_pairs={{0,4},{4,0},{8,12},{12,8},{16,20},{20,16},{24,28},{28,24},{1,5},{5... | collective-permute-start | bytes 245768 | tf_op jit(solution)/shard_map/ppermute | solution.py:424
  32.0 7.0 %collective-permute-start.6 = (f32[20,4,256]{2,1,0:T(4,128)S(1)}, f32[20,4,256]{2,1,0:T(4,128)S(1)}, u32[]{:S(2)}, u32[]{:S(2)}) collective-permute-start(f32[20,4,256]{2,1,0:T(4,128)S(1)} %collective-permute-done.5.refs_6_), channel_id=1, source_target_pairs={{0,4},{4,0},{8,12},{12,8},{16,20},{20,16},{24,28},{28,24},{1,5},{5... | collective-permute-start | bytes 245768 | tf_op jit(solution)/shard_map/ppermute | solution.py:424
  36.4 9.6 %collective-permute-start.13 = (f32[24,4,256]{2,1,0:T(4,128)S(1)}, f32[24,4,256]{2,1,0:T(4,128)S(1)}, u32[]{:S(2)}, u32[]{:S(2)}) collective-permute-start(f32[24,4,256]{2,1,0:T(4,128)S(1)} %copy-done.3), channel_id=1, source_target_pairs={{0,4},{4,0},{8,12},{12,8},{16,20},{20,16},{24,28},{28,24},{1,5},{5... | collective-permute-start | bytes 294920 | tf_op jit(solution)/shard_map/ppermute | solution.py:424
  36.9 7.5 %collective-permute-start.10 = (f32[16,256]{1,0:T(8,128)S(1)}, f32[16,256]{1,0:T(8,128)S(1)}, u32[]{:S(2)}, u32[]{:S(2)}) collective-permute-start(f32[16,256]{1,0:T(8,128)S(1)} %get-tuple-element.12.refs_4_), channel_id=1, source_target_pairs={{0,1},{1,0},{2,3},{3,2},{4,5},{5,4},{6,7},{7,6},{8,9},{9,8},{10,11... | collective-permute-start | bytes 49160 | tf_op jit(solution)/shard_map/ppermute | solution.py:424
  37.0 9.1 %collective-permute-start.15 = (f32[24,4,256]{2,1,0:T(4,128)S(1)}, f32[24,4,256]{2,1,0:T(4,128)S(1)}, u32[]{:S(2)}, u32[]{:S(2)}) collective-permute-start(f32[24,4,256]{2,1,0:T(4,128)S(1)} %collective-permute-done.14.refs_2_), channel_id=1, source_target_pairs={{0,4},{4,0},{8,12},{12,8},{16,20},{20,16},{24,28},{28,24},{1,5},{5... | collective-permute-start | bytes 294920 | tf_op jit(solution)/shard_map/ppermute | solution.py:424
  38.5 8.2 %collective-permute-start.17 = (f32[24,4,256]{2,1,0:T(4,128)S(1)}, f32[24,4,256]{2,1,0:T(4,128)S(1)}, u32[]{:S(2)}, u32[]{:S(2)}) collective-permute-start(f32[24,4,256]{2,1,0:T(4,128)S(1)} %collective-permute-done.16.refs_4_), channel_id=1, source_target_pairs={{0,4},{4,0},{8,12},{12,8},{16,20},{20,16},{24,28},{28,24},{1,5},{5... | collective-permute-start | bytes 294920 | tf_op jit(solution)/shard_map/ppermute | solution.py:424
  39.1 9.1 %collective-permute-start.19 = (f32[24,4,256]{2,1,0:T(4,128)S(1)}, f32[24,4,256]{2,1,0:T(4,128)S(1)}, u32[]{:S(2)}, u32[]{:S(2)}) collective-permute-start(f32[24,4,256]{2,1,0:T(4,128)S(1)} %collective-permute-done.18.refs_6_), channel_id=1, source_target_pairs={{0,4},{4,0},{8,12},{12,8},{16,20},{20,16},{24,28},{28,24},{1,5},{5... | collective-permute-start | bytes 294920 | tf_op jit(solution)/shard_map/ppermute | solution.py:424
  40.6 2.2 %copy-start.8 = (bf16[8,4,256,256]{3,2,1,0:T(8,128)(2,1)S(1)}, bf16[8,4,256,256]{3,2,1,0:T(8,128)(2,1)}, u32[]{:S(2)}) copy-start(bf16[8,4,256,256]{3,2,1,0:T(8,128)(2,1)} %copy-done.7) | copy-start | bytes 12582916
  42.8 5.4 %copy-start.9 = (bf16[8,4,256,256]{3,2,1,0:T(8,128)(2,1)S(1)}, bf16[8,4,256,256]{3,2,1,0:T(8,128)(2,1)}, u32[]{:S(2)}) copy-start(bf16[8,4,256,256]{3,2,1,0:T(8,128)(2,1)} %copy-done.7) | copy-start | bytes 12582916
  44.5 7.3 %copy-start.6 = (f32[5]{0:T(128)S(1)}, f32[5]{0:T(128)}, u32[]{:S(2)}) copy-start(f32[5]{0:T(128)} %refs_7_.1) | copy-start | bytes 64
  44.5 10.0 %copy-start.11 = (bf16[16,256,4,128]{3,2,1,0:T(4,128)(2,1)S(1)}, bf16[16,256,4,128]{3,2,1,0:T(4,128)(2,1)}, u32[]{:S(2)}) copy-start(bf16[16,256,4,128]{3,2,1,0:T(4,128)(2,1)} %copy-done.10) | copy-start | bytes 12582916
  44.5 5.9 %collective-permute-start.11 = (f32[16,256]{1,0:T(8,128)S(1)}, f32[16,256]{1,0:T(8,128)S(1)}, u32[]{:S(2)}, u32[]{:S(2)}) collective-permute-start(f32[16,256]{1,0:T(8,128)S(1)} %get-tuple-element.12.refs_4_), channel_id=1, source_target_pairs={{0,2},{1,3},{2,0},{3,1},{4,6},{5,7},{6,4},{7,5},{8,10},{9,11},{10,... | collective-permute-start | bytes 49160 | tf_op jit(solution)/shard_map/ppermute | solution.py:424
  46.0 4.3 %collective-permute-start.12 = (f32[16,256]{1,0:T(8,128)S(1)}, f32[16,256]{1,0:T(8,128)S(1)}, u32[]{:S(2)}, u32[]{:S(2)}) collective-permute-start(f32[16,256]{1,0:T(8,128)S(1)} %get-tuple-element.12.refs_4_), channel_id=1, source_target_pairs={{0,3},{1,2},{2,1},{3,0},{4,7},{5,6},{6,5},{7,4},{8,11},{9,10},{10,... | collective-permute-start | bytes 49160 | tf_op jit(solution)/shard_map/ppermute | solution.py:424
  46.1 4.3 %collective-permute-start.7 = (f32[24,256]{1,0:T(8,128)S(1)}, f32[24,256]{1,0:T(8,128)S(1)}, u32[]{:S(2)}, u32[]{:S(2)}) collective-permute-start(f32[24,256]{1,0:T(8,128)S(1)} %raw.1.refs_0_), channel_id=1, source_target_pairs={{0,1},{1,0},{2,3},{3,2},{4,5},{5,4},{6,7},{7,6},{8,9},{9,8},{10,11... | collective-permute-start | bytes 73736 | tf_op jit(solution)/shard_map/ppermute | solution.py:424
  46.7 3.8 %collective-permute-start.8 = (f32[24,256]{1,0:T(8,128)S(1)}, f32[24,256]{1,0:T(8,128)S(1)}, u32[]{:S(2)}, u32[]{:S(2)}) collective-permute-start(f32[24,256]{1,0:T(8,128)S(1)} %raw.1.refs_0_), channel_id=1, source_target_pairs={{0,2},{1,3},{2,0},{3,1},{4,6},{5,7},{6,4},{7,5},{8,10},{9,11},{10,... | collective-permute-start | bytes 73736 | tf_op jit(solution)/shard_map/ppermute | solution.py:424
  48.2 3.5 %collective-permute-start.9 = (f32[24,256]{1,0:T(8,128)S(1)}, f32[24,256]{1,0:T(8,128)S(1)}, u32[]{:S(2)}, u32[]{:S(2)}) collective-permute-start(f32[24,256]{1,0:T(8,128)S(1)} %raw.1.refs_0_), channel_id=1, source_target_pairs={{0,3},{1,2},{2,1},{3,0},{4,7},{5,6},{6,5},{7,4},{8,11},{9,10},{10,... | collective-permute-start | bytes 73736 | tf_op jit(solution)/shard_map/ppermute | solution.py:424
  52.5 10.6 %collective-permute-start.20 = (f32[24,256]{1,0:T(8,128)S(1)}, f32[24,256]{1,0:T(8,128)S(1)}, u32[]{:S(2)}, u32[]{:S(2)}) collective-permute-start(f32[24,256]{1,0:T(8,128)S(1)} %get-tuple-element.15.refs_0_), channel_id=1, source_target_pairs={{0,1},{1,0},{2,3},{3,2},{4,5},{5,4},{6,7},{7,6},{8,9},{9,8},{10,11... | collective-permute-start | bytes 73736 | tf_op jit(solution)/shard_map/ppermute | solution.py:424
  52.7 10.5 %collective-permute-start.21 = (f32[24,256]{1,0:T(8,128)S(1)}, f32[24,256]{1,0:T(8,128)S(1)}, u32[]{:S(2)}, u32[]{:S(2)}) collective-permute-start(f32[24,256]{1,0:T(8,128)S(1)} %get-tuple-element.15.refs_0_), channel_id=1, source_target_pairs={{0,2},{1,3},{2,0},{3,1},{4,6},{5,7},{6,4},{7,5},{8,10},{9,11},{10,... | collective-permute-start | bytes 73736 | tf_op jit(solution)/shard_map/ppermute | solution.py:424
  53.5 9.7 %collective-permute-start.22 = (f32[24,256]{1,0:T(8,128)S(1)}, f32[24,256]{1,0:T(8,128)S(1)}, u32[]{:S(2)}, u32[]{:S(2)}) collective-permute-start(f32[24,256]{1,0:T(8,128)S(1)} %get-tuple-element.15.refs_0_), channel_id=1, source_target_pairs={{0,3},{1,2},{2,1},{3,0},{4,7},{5,6},{6,5},{7,4},{8,11},{9,10},{10,... | collective-permute-start | bytes 73736 | tf_op jit(solution)/shard_map/ppermute | solution.py:424
  54.5 8.7 %copy-start.5 = (f32[2048]{0:T(1024)S(1)}, f32[2048]{0:T(1024)}, u32[]{:S(2)}) copy-start(f32[2048]{0:T(1024)} %param.13) | copy-start | bytes 24580

commit v2 on v1

v2 whole, which is shorter than its diff:
```python
import functools

import jax
import jax.numpy as jnp
from jax import lax
from jax.experimental import pallas as pl
from jax.experimental.pallas import tpu as pltpu
from jax.sharding import PartitionSpec as P


BALANCE_ROUNDS = 6
EPS = 1e-06
FB = 256
GT = 64
MT = 32
F32 = jnp.float32
BF16 = jnp.bfloat16
MIB = 2**20

VMEM = pl.BlockSpec(memory_space=pltpu.VMEM)
SMEM = pl.BlockSpec(memory_space=pltpu.SMEM)
HBM = pl.BlockSpec(memory_space=pltpu.HBM)

PAIRS = [(i, j) for i in range(4) for j in range(i, 4)]


def _nt(a, b, precision=None):
    return lax.dot_general(
        a, b, (((1,), (1,)), ((), ())), precision=precision, preferred_element_type=F32
    )


def _split(x):
    hi = x.astype(BF16)
    return hi, (x - hi.astype(F32)).astype(BF16)


def _iota(shape, dim):
    return lax.broadcasted_iota(jnp.int32, shape, dim)


def _store_by_column(ref, rows, start):
    ref[0:start, :] = rows[0:start]
    for j in range(4):
        for i in range(4):
            source = start + 4 * j + i
            ref[start + 4 * i + j : start + 4 * i + j + 1, :] = rows[source : source + 1]
    if rows.shape[0] > start + 16:
        ref[start + 16 : rows.shape[0], :] = rows[start + 16 :]


def deal_kernel(s_hbm, sil_ref, sde_ref, sems):
    tokens, _, width = s_hbm.shape
    rows = 4 * tokens

    def copy(c):
        return pltpu.make_async_copy(
            s_hbm.at[:, :, pl.ds(pl.multiple_of(c * 128, 128), 128)], sil_ref.at[c], sems.at[c]
        )

    for c in range(width // 128):
        copy(c).start()
    r, q = _iota((4 * GT, 4 * GT), 0), _iota((4 * GT, 4 * GT), 1)
    perm = jnp.where(q == 4 * (r % GT) + r // GT, 1.0, 0.0).astype(BF16)

    def body(k, _):
        copy(2 * k).wait()
        copy(2 * k + 1).wait()
        left = sil_ref.at[2 * k].reshape(rows, 128)
        right = sil_ref.at[2 * k + 1].reshape(rows, 128)
        for g in range(tokens // GT):
            own = pl.ds(g * 4 * GT, 4 * GT)
            x = jnp.concatenate([left[own, :], right[own, :]], axis=1)
            y = jnp.dot(perm, x, preferred_element_type=F32)
            for i in range(4):
                sde_ref[k, i, pl.ds(g * GT, GT), :] = y[i * GT : (i + 1) * GT].astype(BF16)
        return 0

    lax.fori_loop(0, width // FB, body, 0)


def deal(streams):
    tokens, _, width = streams.shape
    return pl.pallas_call(
        deal_kernel,
        out_shape=(
            jax.ShapeDtypeStruct((width // 128, tokens, 4, 128), BF16),
            jax.ShapeDtypeStruct((width // FB, 4, tokens, FB), BF16),
        ),
        in_specs=[HBM],
        out_specs=(VMEM, VMEM),
        scratch_shapes=[pltpu.SemaphoreType.DMA((width // 128,))],
        compiler_params=pltpu.CompilerParams(vmem_limit_bytes=14 * MIB),
        cost_estimate=pl.CostEstimate(
            flops=4_000_000_000, bytes_accessed=10 * MIB, transcendentals=0
        ),
        name="deal",
    )(pltpu.with_memory_space_constraint(streams, pltpu.HBM))


def grams_kernel(sde_ref, b_ref, g_ref, column_ref):
    blocks, _, tokens, _ = sde_ref.shape

    def chunk(c, _):
        at = pl.ds(pl.multiple_of(c * 16, 16), 16)
        sums = [None] * 15
        for k in range(blocks):
            for h in range(FB // 128):
                lanes = slice(h * 128, (h + 1) * 128)
                wide = [sde_ref[k, i, at, lanes].astype(F32) for i in range(4)]
                wide.append(b_ref[at, k * FB + h * 128 : k * FB + (h + 1) * 128].astype(F32))
                products = [wide[i] * wide[j] for i, j in PAIRS]
                products += [wide[i] * wide[4] for i in range(5)]
                sums = [p if s is None else s + p for s, p in zip(sums, products)]
        lane = _iota((16, 128), 1)
        column = jnp.zeros((16, 128), F32)
        for p in range(15):
            column = jnp.where(lane == p, jnp.sum(sums[p], axis=1, keepdims=True), column)
        column_ref[at, :] = column
        return 0

    lax.fori_loop(0, tokens // 16, chunk, 0)
    g_ref[...] = column_ref[...].T[0:16]


def grams_of(sde, branch):
    tokens = sde.shape[2]
    return pl.pallas_call(
        grams_kernel,
        out_shape=jax.ShapeDtypeStruct((16, tokens), F32),
        in_specs=[VMEM, VMEM],
        out_specs=VMEM,
        scratch_shapes=[pltpu.VMEM((tokens, 128), F32)],
        compiler_params=pltpu.CompilerParams(vmem_limit_bytes=8 * MIB),
        cost_estimate=pl.CostEstimate(
            flops=3_000_000_000, bytes_accessed=5 * MIB, transcendentals=0
        ),
        name="grams",
    )(sde, branch)


def _owner(s, permuted):
    return jnp.bitwise_xor(lax.axis_index("dp"), s) if permuted else s


def raw_kernel(permuted, *refs):
    w_refs, (sde_ref, g_ref, out_ref, wide_ref, lhs_ref) = refs[:-5], refs[-5:]
    count = w_refs[0].shape[0]
    pad = wide_ref.shape[1]
    blocks = sde_ref.shape[0]
    wide_ref[...] = jnp.zeros_like(wide_ref)
    for s in range(blocks):
        owner = _owner(s, permuted)
        for i in range(4):
            wide_ref[i, 0:count, :] = w_refs[s][:, i, :]
            hi, lo = _split(wide_ref[i])
            lhs_ref[owner, i, 0:pad, :] = hi
            lhs_ref[owner, i, pad : 2 * pad, :] = lo
    total = None
    for s in range(blocks):
        for i in range(4):
            part = _nt(lhs_ref[s, i], sde_ref[s, i])
            total = part if total is None else total + part
    _store_by_column(out_ref, total[0:24] + total[pad : pad + 24], 4)
    out_ref[24:40, :] = g_ref[...]


def raw(weights, sde, gram, permuted):
    blocks, _, tokens, _ = sde.shape
    return pl.pallas_call(
        functools.partial(raw_kernel, permuted),
        out_shape=jax.ShapeDtypeStruct((40, tokens), F32),
        in_specs=[VMEM] * (len(weights) + 2),
        out_specs=VMEM,
        scratch_shapes=[
            pltpu.VMEM((4, 32, FB), F32),
            pltpu.VMEM((blocks, 4, 64, FB), BF16),
        ],
        compiler_params=pltpu.CompilerParams(vmem_limit_bytes=12 * MIB),
        cost_estimate=pl.CostEstimate(
            flops=2_000_000_000, bytes_accessed=5 * MIB, transcendentals=0
        ),
        name="raw",
    )(*weights, sde, gram)


def next_kernel(permuted, *refs):
    w_refs, (sde_ref, b_ref, coef_ref, out_ref, wide_ref, lhs_ref) = refs[:-6], refs[-6:]
    count = w_refs[0].shape[0]
    blocks = sde_ref.shape[0]
    rows = 4 * count
    for s in range(blocks):
        owner = _owner(s, permuted)
        for j in range(4):
            wide_ref[j * count : (j + 1) * count, :] = w_refs[s][:, j, :]
        hi, lo = _split(wide_ref[...])
        lhs_ref[owner, 0:rows, :] = hi
        lhs_ref[owner, rows : 2 * rows, :] = lo
    mixed = None
    for i in range(5):
        total = None
        for s in range(blocks):
            right = sde_ref[s, i] if i < 4 else b_ref[:, s * FB : (s + 1) * FB]
            part = _nt(lhs_ref[s], right)
            total = part if total is None else total + part
        total = total[0:rows] + total[rows : 2 * rows]
        for j in range(4):
            part = coef_ref[4 * i + j : 4 * i + j + 1, :] * total[j * count : (j + 1) * count]
            mixed = part if mixed is None else mixed + part
    _store_by_column(out_ref, mixed, 8)


def project_next(weights, sde, branch, coef, permuted):
    blocks, _, tokens, _ = sde.shape
    rows = 4 * weights[0].shape[0]
    return pl.pallas_call(
        functools.partial(next_kernel, permuted),
        out_shape=jax.ShapeDtypeStruct((rows // 4, tokens), F32),
        in_specs=[VMEM] * (len(weights) + 3),
        out_specs=VMEM,
        scratch_shapes=[
            pltpu.VMEM((rows, FB), F32),
            pltpu.VMEM((blocks, 2 * rows, FB), BF16),
        ],
        compiler_params=pltpu.CompilerParams(vmem_limit_bytes=14 * MIB),
        cost_estimate=pl.CostEstimate(
            flops=3_000_000_000, bytes_accessed=6 * MIB, transcendentals=0
        ),
        name="project_next",
    )(*weights, sde, branch, coef)


def _balance(columns):
    for _ in range(BALANCE_ROUNDS):
        inverse = 1.0 / (columns[0] + columns[1] + columns[2] + columns[3])
        columns = [c * inverse for c in columns]
        columns = [c * (1.0 / jnp.sum(c, axis=0, keepdims=True)) for c in columns]
    return columns


def _sum4(refs, at):
    return (refs[0][at] + refs[1][at]) + (refs[2][at] + refs[3][at])


def _bias(bias_ref, start, step):
    row = _iota((4, 128), 0)
    column = jnp.full((4, 128), bias_ref[start], F32)
    for j in range(1, 4):
        column = jnp.where(row == j, bias_ref[start + j * step], column)
    return column


def _scored(raw_rows, inverse, scale, bias):
    score = scale * (raw_rows * inverse)
    return score + jnp.concatenate([bias] * (score.shape[1] // 128), axis=1)


def first_kernel(features, *refs):
    r_refs = refs[0:4]
    bias_ref, scale_ref, coef_ref, gram_ref = refs[4:]
    gram = _sum4(r_refs, (slice(24, 40), slice(None)))
    gram_ref[...] = gram
    squares = gram[0:1] + gram[4:5] + gram[7:8] + gram[9:10]
    inverse = 1.0 / jnp.sqrt(squares / features + EPS)
    raw_post = _sum4(r_refs, (slice(0, 4), slice(None)))
    score = _scored(raw_post, inverse, scale_ref[0], _bias(bias_ref, 0, 1))
    coef_ref[16:20, :] = 2.0 * jax.nn.sigmoid(score)
    columns = []
    for i in range(4):
        raw_rows = _sum4(r_refs, (slice(4 + 4 * i, 8 + 4 * i), slice(None)))
        score = _scored(raw_rows, inverse, scale_ref[1], _bias(bias_ref, 4 + i, 4))
        columns.append(jnp.exp(score))
    columns = _balance(columns)
    for i in range(4):
        coef_ref[4 * i : 4 * i + 4, :] = columns[i]
    coef_ref[20:24, :] = jnp.zeros_like(coef_ref[20:24, :])


def first(raws, bias, scale, features):
    tokens = raws[0].shape[1]
    return pl.pallas_call(
        functools.partial(first_kernel, features),
        out_shape=(
            jax.ShapeDtypeStruct((24, tokens), F32),
            jax.ShapeDtypeStruct((16, tokens), F32),
        ),
        in_specs=[VMEM] * 4 + [SMEM, SMEM],
        out_specs=(VMEM, VMEM),
        compiler_params=pltpu.CompilerParams(vmem_limit_bytes=4 * MIB),
        cost_estimate=pl.CostEstimate(
            flops=1_000_000_000, bytes_accessed=MIB, transcendentals=20000
        ),
        name="first",
    )(*raws, bias, scale)


def mix_kernel(coef_ref, sil_ref, b_ref, out_hbm, stage_ref, left_ref, sems):
    tiles, tokens = sil_ref.shape[0], sil_ref.shape[1]
    rows = 4 * MT
    wide = 2 * rows + 2 * MT
    m, q = _iota((64, wide), 0), _iota((64, wide), 1)
    of_branch = q >= 2 * rows
    low = jnp.where(of_branch, (q - 2 * rows) // MT, q // rows)
    source = jnp.where(of_branch, 4, q % 4)
    pick = jnp.where(m // 4 == low * 8 + source, 1.0, 0.0).astype(BF16)
    r, q = _iota((rows, wide), 0), _iota((rows, wide), 1)
    token = jnp.where(q >= 2 * rows, (q - 2 * rows) % MT, (q % rows) // 4)
    same = token == r // 4
    r, m = _iota((rows, 64), 0), _iota((rows, 64), 1)
    keep = (m % 4) == (r % 4)
    hi, lo = _split(jnp.concatenate([coef_ref[...], jnp.zeros((8, tokens), F32)], axis=0))
    coef = jnp.concatenate([hi, lo], axis=0)
    for g in range(tokens // MT):
        start = g * MT // 128 * 128
        lane, r = _iota((rows, 128), 1), _iota((rows, 128), 0)
        expand = jnp.where(lane == g * MT - start + r // 4, 1.0, 0.0).astype(BF16)
        held = _nt(expand, coef[:, start : start + 128])
        held = jnp.where(keep, held, 0.0).astype(BF16)
        spread = jnp.dot(held, pick, preferred_element_type=F32)
        left_ref[g] = jnp.where(same, spread, 0.0).astype(BF16)

    def copy(c):
        return pltpu.make_async_copy(
            stage_ref.at[c],
            out_hbm.at[:, :, pl.ds(pl.multiple_of(c * 128, 128), 128)],
            sems.at[c],
        )

    def body(k, _):
        ins = [sil_ref.at[2 * k + h].reshape(4 * tokens, 128) for h in range(2)]
        outs = [stage_ref.at[2 * k + h].reshape(4 * tokens, 128) for h in range(2)]
        lanes = pl.ds(pl.multiple_of(k * FB, FB), FB)
        for g in range(tokens // MT):
            own = pl.ds(g * rows, rows)
            x = jnp.concatenate([ins[0][own, :], ins[1][own, :]], axis=1)
            b = b_ref[pl.ds(g * MT, MT), lanes]
            y = jnp.dot(
                left_ref[g, :, 0 : 2 * rows],
                jnp.concatenate([x, x], axis=0),
                preferred_element_type=F32,
            )
            y += jnp.dot(
                left_ref[g, :, 2 * rows : wide],
                jnp.concatenate([b, b], axis=0),
                preferred_element_type=F32,
            )
            y = y.astype(BF16)
            outs[0][own, :] = y[:, :128]
            outs[1][own, :] = y[:, 128:]
        copy(2 * k).start()
        copy(2 * k + 1).start()
        return 0

    lax.fori_loop(0, tiles // 2, body, 0)
    for c in range(tiles):
        copy(c).wait()


def mix(coef, sil, branch):
    tiles, tokens = sil.shape[0], sil.shape[1]
    return pl.pallas_call(
        mix_kernel,
        out_shape=jax.ShapeDtypeStruct((tokens, 4, tiles * 128), BF16),
        in_specs=[VMEM, VMEM, VMEM],
        out_specs=HBM,
        scratch_shapes=[
            pltpu.VMEM((tiles, tokens, 4, 128), BF16),
            pltpu.VMEM((tokens // MT, 4 * MT, 10 * MT), BF16),
            pltpu.SemaphoreType.DMA((tiles,)),
        ],
        compiler_params=pltpu.CompilerParams(vmem_limit_bytes=14 * MIB),
        cost_estimate=pl.CostEstimate(
            flops=5_000_000_000, bytes_accessed=8 * MIB, transcendentals=0
        ),
        name="mix",
    )(coef, sil, branch)


def second_kernel(features, *refs):
    r_refs = refs[0:4]
    coef_ref, gram_ref, bias_ref, scale_ref, sde_ref, b_ref, gain_ref = refs[4:11]
    out_ref, mix_ref, column_ref = refs[11:]
    tokens, _ = b_ref.shape
    gram = gram_ref[...]
    columns = [coef_ref[4 * i : 4 * i + 4, :] for i in range(5)]

    def quadratic(terms):
        total = None
        for p, (i, j) in enumerate(PAIRS):
            part = terms[i] * terms[j] * gram[p : p + 1]
            part = part if i == j else 2.0 * part
            total = part if total is None else total + part
        for i in range(4):
            total = total + 2.0 * (terms[i] * terms[4]) * gram[10 + i : 11 + i]
        return total + terms[4] * terms[4] * gram[14:15]

    squares = jnp.maximum(jnp.sum(quadratic(columns), axis=0, keepdims=True), 0.0)
    inverse = 1.0 / jnp.sqrt(squares / features + EPS)
    everything = slice(None)
    pre_raw = _sum4(r_refs, (slice(0, 4), everything))
    score = _scored(pre_raw, inverse, scale_ref[2], _bias(bias_ref, 20, 1))
    pre_next = jax.nn.sigmoid(score)
    post_raw = _sum4(r_refs, (slice(4, 8), everything))
    score = _scored(post_raw, inverse, scale_ref[3], _bias(bias_ref, 24, 1))
    mix_ref[0:4, :] = 2.0 * jax.nn.sigmoid(score)
    following = []
    for i in range(4):
        raw_rows = _sum4(r_refs, (slice(8 + 4 * i, 12 + 4 * i), everything))
        score = _scored(raw_rows, inverse, scale_ref[4], _bias(bias_ref, 28 + i, 4))
        following.append(jnp.exp(score))
    following = _balance(following)
    for i in range(4):
        for j in range(4):
            mix_ref[4 + 4 * j + i : 5 + 4 * j + i, :] = following[i][j : j + 1]

    joint = [jnp.sum(pre_next * c, axis=0, keepdims=True) for c in columns]
    united = jnp.maximum(quadratic(joint), 0.0)
    root = 1.0 / jnp.sqrt(united / (features // 4) + EPS)
    stacked = jnp.concatenate([j * root for j in joint] + [jnp.zeros((3, tokens), F32)], axis=0)
    column_ref[:, 0:8] = stacked.T
    blocks = sde_ref.shape[0]

    def body(c, _):
        at = pl.ds(pl.multiple_of(c * 16, 16), 16)
        weights = [column_ref[at, i : i + 1] for i in range(5)]
        for k in range(blocks):
            lanes = pl.ds(k * FB, FB)
            total = weights[4] * b_ref[at, lanes].astype(F32)
            for i in range(4):
                total = total + weights[i] * sde_ref[k, i, at, :].astype(F32)
            out_ref[at, lanes] = (total * gain_ref[:, lanes]).astype(BF16)
        return 0

    lax.fori_loop(0, tokens // 16, body, 0)


def second(raws, coef, gram, bias, scale, sde, branch, gain, features):
    tokens, width = branch.shape
    return pl.pallas_call(
        functools.partial(second_kernel, features),
        out_shape=(
            jax.ShapeDtypeStruct((tokens, width), BF16),
            jax.ShapeDtypeStruct((20, tokens), F32),
        ),
        in_specs=[VMEM] * 6 + [SMEM] * 2 + [VMEM] * 3,
        out_specs=(VMEM, VMEM),
        scratch_shapes=[pltpu.VMEM((tokens, 128), F32)],
        compiler_params=pltpu.CompilerParams(vmem_limit_bytes=14 * MIB),
        cost_estimate=pl.CostEstimate(
            flops=3_000_000_000, bytes_accessed=6 * MIB, transcendentals=20000
        ),
        name="second",
    )(*raws, coef, gram, bias, scale, sde, branch, gain)


def _swap(x, axis, count, s):
    return lax.ppermute(x, axis, [(i, i ^ s) for i in range(count)])


def gather_blocks(weight, count, width):
    if weight.shape[2] == FB and count & (count - 1) == 0 and count * FB == width:
        even = {0: weight}
        for s in range(2, count, 2):
            even[s] = _swap(weight, "dp", count, s)
        blocks = [None] * count
        for s in range(0, count, 2):
            blocks[s] = even[s]
            blocks[s + 1] = _swap(even[s], "dp", count, 1)
        return blocks, True
    whole = lax.all_gather(weight, "dp", axis=2, tiled=True)
    return [whole[:, :, k * FB : (k + 1) * FB] for k in range(width // FB)], False


def everyone(x, count):
    return [x] + [_swap(x, "mp", count, s) for s in range(1, count)]


def solution(mesh):
    n_dp, n_mp = mesh.shape["dp"], mesh.shape["mp"]

    def local(streams, branch, merge_weight, next_weight, blend_bias, blend_scale, norm_gain):
        count, width = streams.shape[1:]
        features = count * width * n_mp
        merge_blocks, permuted = gather_blocks(merge_weight, n_dp, width)
        next_blocks, _ = gather_blocks(next_weight, n_dp, width)
        gain = norm_gain[None, :]
        sil, sde = deal(streams)
        gram = grams_of(sde, branch)
        raws = everyone(raw(merge_blocks, sde, gram, permuted), n_mp)
        coef, gram_sum = first(raws, blend_bias, blend_scale, features)
        streams_out = mix(coef, sil, branch)
        next_raw = project_next(next_blocks, sde, branch, coef, permuted)
        next_raws = everyone(next_raw, n_mp)
        branch_in, next_mix = second(
            next_raws, coef, gram_sum, blend_bias, blend_scale, sde, branch, gain, features
        )
        return streams_out, branch_in, next_mix.T

    placed = (
        P("dp", None, "mp"),
        P("dp", "mp"),
        P(None, None, ("mp", "dp")),
        P(None, None, ("mp", "dp")),
        P(),
        P(),
        P("mp"),
    )
    return jax.shard_map(
        local,
        mesh=mesh,
        in_specs=placed,
        out_specs=(P("dp", None, "mp"), P("dp", "mp"), P("dp", None)),
        check_vma=False,
    )
```

time: 67.4 us -> 52.1 us (0.77)
  local copies, waits for them, and re-layouts: 10.4 us -> 0.02 us
  Pallas kernels: 27.2 us -> 22 us
  waiting for transfers between devices: 4.63 us -> 5.97 us
  starting transfers between devices: 24 us -> 23.2 us
    unnamed x26 -> x12, local copies, waits for them, and re-layouts: 9.62 us -> 0.02 us
    pallas_call x1, Pallas kernels: 8.66 us -> 5.95 us  [mix(): pl.pallas_call(mix_kernel, out_shape=jax.ShapeDtypeStruct((tokens, 4, til...]
    pallas_call x1 -> x2, Pallas kernels: 10 us -> 7.52 us  [the longest x1 3.81 us: deal(): pl.pallas_call(deal_kernel, out_shape=(jax.ShapeDtypeStruct((width // 128...]
    ppermute x23 -> x20, waiting for transfers between devices: 4.63 us -> 5.97 us  [_swap(): return lax.ppermute(x, axis, [(i, i ^ s) for i in range(count)])]
    ppermute x23 -> x20, starting transfers between devices: 24 us -> 23.2 us  [_swap(): return lax.ppermute(x, axis, [(i, i ^ s) for i in range(count)])]
  transfers between devices with their start and end apart: 23 -> 20, of which waited for: 3 -> 5; matrix products, arithmetic and copies ran while one was open for 1% -> 0% of each run, Pallas kernels for 34% -> 31%
where the time goes in v2:
time: 52.1 us; the launch traced here: 52 us
  starting transfers between devices  23.2 us (45%)
  Pallas kernels  22 us (42%)
  waiting for transfers between devices  5.97 us (11%)
  between operations  0.8 us (2%)
    ppermute x20, starting transfers between devices, _swap(): return lax.ppermute(x, axis, [(i, i ^ s) for i in range(count)])  23.2 us
    ppermute x20, waiting for transfers between devices, _swap(): return lax.ppermute(x, axis, [(i, i ^ s) for i in range(count)])  5.97 us
    pallas_call x1, Pallas kernels, mix(): pl.pallas_call(mix_kernel, out_shape=jax.ShapeDtypeStruct((tokens, 4, til...  5.95 us
    pallas_call x1, Pallas kernels, second(): pl.pallas_call(functools.partial(second_kernel, features), out_shape=(jax...  3.95 us
    pallas_call x1, Pallas kernels, deal(): pl.pallas_call(deal_kernel, out_shape=(jax.ShapeDtypeStruct((width // 128...  3.81 us
    pallas_call x1, Pallas kernels, grams_of(): pl.pallas_call(grams_kernel, out_shape=jax.ShapeDtypeStruct((16, tokens),...  3.71 us
    pallas_call x1, Pallas kernels, project_next(): pl.pallas_call(functools.partial(next_kernel, permuted), out_shape=jax.Sh...  2.14 us
    pallas_call x1, Pallas kernels, raw(): pl.pallas_call(functools.partial(raw_kernel, permuted), out_shape=jax.Sha...  1.68 us
  transfers between devices with their start and end apart: 20, of which 5 were waited for; matrix products, arithmetic and copies ran while one was open for 0% of the time, Pallas kernels for 31%

profile of v2, /device:TPU:0, one launch (start us, length us, event | category | flops | bytes accessed | tf_op | source)
XLA Modules:
  0.0 52.0 jit_solution(15859089336443081327)
XLA Ops:
  0.6 0.0 copy-start
  0.6 3.1 %collective-permute-start.1 = (f32[20,4,256]{2,1,0:T(4,128)}, f32[20,4,256]{2,1,0:T(4,128)S(1)}, u32[]{:S(2)}, u32[]{:S(2)}) collective-permute-start(f32[20,4,256]{2,1,0:T(4,128)} %refs_0_.2), channel_id=1, source_target_pairs={{0,8},{4,12},{8,0},{12,4},{16,24},{20,28},{24,16},{28,20},{1,9},{5... | collective-permute-start | bytes 245768 | tf_op jit(solution)/shard_map/ppermute | solution.py:457
  3.8 2.6 %collective-permute-start.3 = (f32[20,4,256]{2,1,0:T(4,128)}, f32[20,4,256]{2,1,0:T(4,128)S(1)}, u32[]{:S(2)}, u32[]{:S(2)}) collective-permute-start(f32[20,4,256]{2,1,0:T(4,128)} %refs_0_.2), channel_id=1, source_target_pairs={{0,16},{4,20},{8,24},{12,28},{16,0},{20,4},{24,8},{28,12},{1,17},{... | collective-permute-start | bytes 245768 | tf_op jit(solution)/shard_map/ppermute | solution.py:457
  6.3 0.0 collective-permute-start.5
  6.3 1.7 %collective-permute-start = (f32[20,4,256]{2,1,0:T(4,128)}, f32[20,4,256]{2,1,0:T(4,128)S(1)}, u32[]{:S(2)}, u32[]{:S(2)}) collective-permute-start(f32[20,4,256]{2,1,0:T(4,128)} %refs_0_.2), channel_id=1, source_target_pairs={{0,4},{4,0},{8,12},{12,8},{16,20},{20,16},{24,28},{28,24},{1,5},{5... | collective-permute-start | bytes 245768 | tf_op jit(solution)/shard_map/ppermute | solution.py:457
  8.1 0.7 %collective-permute-start.11 = (f32[24,4,256]{2,1,0:T(4,128)}, f32[24,4,256]{2,1,0:T(4,128)S(1)}, u32[]{:S(2)}, u32[]{:S(2)}) collective-permute-start(f32[24,4,256]{2,1,0:T(4,128)} %refs_0_.3), channel_id=1, source_target_pairs={{0,8},{4,12},{8,0},{12,4},{16,24},{20,28},{24,16},{28,20},{1,9},{5... | collective-permute-start | bytes 294920 | tf_op jit(solution)/shard_map/ppermute | solution.py:457
  8.8 3.8 %deal.1 = (bf16[16,256,4,128]{3,2,1,0:T(4,128)(2,1)S(1)}, bf16[8,4,256,256]{3,2,1,0:T(8,128)(2,1)S(1)}) custom-call(bf16[256,4,2048]{2,1,0:T(4,128)(2,1)} %s_hbm.1), custom_call_target="tpu_custom_call" | custom-call | flops 4000000000 | bytes 10485760 | tf_op jit(solution)/shard_map/deal/pallas_call | solution.py:84
  12.6 0.0 collective-permute-done.1.refs_2_
  12.6 0.6 %collective-permute-start.2 = (f32[20,4,256]{2,1,0:T(4,128)S(1)}, f32[20,4,256]{2,1,0:T(4,128)S(1)}, u32[]{:S(2)}, u32[]{:S(2)}) collective-permute-start(f32[20,4,256]{2,1,0:T(4,128)S(1)} %collective-permute-done.1.refs_2_), channel_id=1, source_target_pairs={{0,4},{4,0},{8,12},{12,8},{16,20},{20,16},{24,28},{28,24},{1,5},{5... | collective-permute-start | bytes 245768 | tf_op jit(solution)/shard_map/ppermute | solution.py:457
  13.2 0.0 collective-permute-done.3.refs_4_
  13.2 1.5 %collective-permute-start.4 = (f32[20,4,256]{2,1,0:T(4,128)S(1)}, f32[20,4,256]{2,1,0:T(4,128)S(1)}, u32[]{:S(2)}, u32[]{:S(2)}) collective-permute-start(f32[20,4,256]{2,1,0:T(4,128)S(1)} %collective-permute-done.3.refs_4_), channel_id=1, source_target_pairs={{0,4},{4,0},{8,12},{12,8},{16,20},{20,16},{24,28},{28,24},{1,5},{5... | collective-permute-start | bytes 245768 | tf_op jit(solution)/shard_map/ppermute | solution.py:457
  14.7 0.0 collective-permute-done.5.refs_6_
  14.7 0.5 collective-permute-start.6
  15.2 0.0 copy-done
  15.2 0.0 copy-start.1
  15.2 0.0 copy-start.2
  15.2 3.7 %grams.1.refs_9_ = f32[16,256]{1,0:T(8,128)S(1)} custom-call(bf16[8,4,256,256]{3,2,1,0:T(8,128)(2,1)S(1)} %get-tuple-element.9.sde_ref.refs_8_, bf16[256,2048]{1,0:T(8,128)(2,1)S(1)} %copy-done), custom_call_target="tpu_custom_call" | custom-call | flops 3000000000 | bytes 5242880 | tf_op jit(solution)/shard_map/grams/pallas_call | solution.py:128
  18.9 0.0 copy-start.4
  18.9 0.0 copy-start.5
  18.9 0.0 collective-permute-done.refs_1_
  18.9 0.0 copy-done.1
  18.9 3.6 %collective-permute-start.13 = (f32[24,4,256]{2,1,0:T(4,128)S(1)}, f32[24,4,256]{2,1,0:T(4,128)S(1)}, u32[]{:S(2)}, u32[]{:S(2)}) collective-permute-start(f32[24,4,256]{2,1,0:T(4,128)S(1)} %copy-done.1), channel_id=1, source_target_pairs={{0,16},{4,20},{8,24},{12,28},{16,0},{20,4},{24,8},{28,12},{1,17},{... | collective-permute-start | bytes 294920 | tf_op jit(solution)/shard_map/ppermute | solution.py:457
  22.5 0.0 collective-permute-done.2.refs_3_
  22.5 0.0 collective-permute-start.15
  22.5 0.0 collective-permute-done.4.refs_5_
  22.5 0.0 collective-permute-done.6.refs_7_
  22.5 0.0 copy-done.2
  22.5 1.7 %raw.1.refs_0_ = f32[40,256]{1,0:T(8,128)S(1)} custom-call(f32[20,4,256]{2,1,0:T(4,128)S(1)} %copy-done.2, f32[20,4,256]{2,1,0:T(4,128)S(1)} %collective-permute-done.refs_1_, f32[20,4,256]{2,1,0:T(4,128)S(1)} %collective-permute-done.1.refs_2_, f32[20,4,256]{2,1,0:T(4,128)S(1)} %collective-permute-done.2.refs_3_, ...), custom_call_target="tpu_custom_call" | custom-call | flops 2000000000 | bytes 5242880 | tf_op jit(solution)/shard_map/raw/pallas_call | solution.py:170
  24.2 0.1 collective-permute-start.7
  24.3 1.8 %collective-permute-start.8 = (f32[40,256]{1,0:T(8,128)S(1)}, f32[40,256]{1,0:T(8,128)S(1)}, u32[]{:S(2)}, u32[]{:S(2)}) collective-permute-start(f32[40,256]{1,0:T(8,128)S(1)} %raw.1.refs_0_), channel_id=1, source_target_pairs={{0,2},{1,3},{2,0},{3,1},{4,6},{5,7},{6,4},{7,5},{8,10},{9,11},{10,... | collective-permute-start | bytes 122888 | tf_op jit(solution)/shard_map/ppermute | solution.py:457
  26.1 0.0 collective-permute-done.11.refs_2_
  26.1 0.1 collective-permute-start.9
  26.2 1.1 %collective-permute-done.13.refs_4_ = f32[24,4,256]{2,1,0:T(4,128)S(1)} collective-permute-done((f32[24,4,256]{2,1,0:T(4,128)S(1)}, f32[24,4,256]{2,1,0:T(4,128)S(1)}, u32[]{:S(2)}, u32[]{:S(2)}) %collective-permute-start.13) | collective-permute-done | bytes 98336 | tf_op jit(solution)/shard_map/ppermute | solution.py:457
  27.3 1.5 %collective-permute-start.10 = (f32[24,4,256]{2,1,0:T(4,128)S(1)}, f32[24,4,256]{2,1,0:T(4,128)S(1)}, u32[]{:S(2)}, u32[]{:S(2)}) collective-permute-start(f32[24,4,256]{2,1,0:T(4,128)S(1)} %copy-done.1), channel_id=1, source_target_pairs={{0,4},{4,0},{8,12},{12,8},{16,20},{20,16},{24,28},{28,24},{1,5},{5... | collective-permute-start | bytes 294920 | tf_op jit(solution)/shard_map/ppermute | solution.py:457
  28.8 0.2 collective-permute-done.15.refs_6_
  29.0 1.5 %collective-permute-start.12 = (f32[24,4,256]{2,1,0:T(4,128)S(1)}, f32[24,4,256]{2,1,0:T(4,128)S(1)}, u32[]{:S(2)}, u32[]{:S(2)}) collective-permute-start(f32[24,4,256]{2,1,0:T(4,128)S(1)} %collective-permute-done.11.refs_2_), channel_id=1, source_target_pairs={{0,4},{4,0},{8,12},{12,8},{16,20},{20,16},{24,28},{28,24},{1,5},{5... | collective-permute-start | bytes 294920 | tf_op jit(solution)/shard_map/ppermute | solution.py:457
  30.5 0.0 collective-permute-done.7.refs_1_
  30.6 0.5 collective-permute-start.14
  31.1 0.0 collective-permute-done.8.refs_2_
  31.1 1.5 %collective-permute-start.16 = (f32[24,4,256]{2,1,0:T(4,128)S(1)}, f32[24,4,256]{2,1,0:T(4,128)S(1)}, u32[]{:S(2)}, u32[]{:S(2)}) collective-permute-start(f32[24,4,256]{2,1,0:T(4,128)S(1)} %collective-permute-done.15.refs_6_), channel_id=1, source_target_pairs={{0,4},{4,0},{8,12},{12,8},{16,20},{20,16},{24,28},{28,24},{1,5},{5... | collective-permute-start | bytes 294920 | tf_op jit(solution)/shard_map/ppermute | solution.py:457
  32.6 0.0 collective-permute-done.9.refs_3_
  32.6 0.0 copy-done.4
  32.6 0.0 copy-done.5
  32.6 0.7 %first.1 = (f32[24,256]{1,0:T(8,128)S(1)}, f32[16,256]{1,0:T(8,128)S(1)}) custom-call(f32[40,256]{1,0:T(8,128)S(1)} %raw.1.refs_0_, f32[40,256]{1,0:T(8,128)S(1)} %collective-permute-done.7.refs_1_, f32[40,256]{1,0:T(8,128)S(1)} %collective-permute-done.8.refs_2_, f32[40,256]{1,0:T(8,128)S(1)} %collective-permute-done.9.refs_3_, f32[44]{0:T(128)S(1)} %copy-done.4, ...), custom_call_target="tpu_custom_call" | custom-call | flops 1000000000 | bytes 1048576 | tf_op jit(solution)/shard_map/first/pallas_call | solution.py:281
  33.3 0.0 collective-permute-done.10.refs_1_
  33.4 1.7 %collective-permute-done.12.refs_3_ = f32[24,4,256]{2,1,0:T(4,128)S(1)} collective-permute-done((f32[24,4,256]{2,1,0:T(4,128)S(1)}, f32[24,4,256]{2,1,0:T(4,128)S(1)}, u32[]{:S(2)}, u32[]{:S(2)}) %collective-permute-start.12) | collective-permute-done | bytes 98336 | tf_op jit(solution)/shard_map/ppermute | solution.py:457
  35.0 1.8 %collective-permute-done.14.refs_5_ = f32[24,4,256]{2,1,0:T(4,128)S(1)} collective-permute-done((f32[24,4,256]{2,1,0:T(4,128)S(1)}, f32[24,4,256]{2,1,0:T(4,128)S(1)}, u32[]{:S(2)}, u32[]{:S(2)}) %collective-permute-start.14) | collective-permute-done | bytes 98336 | tf_op jit(solution)/shard_map/ppermute | solution.py:457
  36.9 1.1 %collective-permute-done.16.refs_7_ = f32[24,4,256]{2,1,0:T(4,128)S(1)} collective-permute-done((f32[24,4,256]{2,1,0:T(4,128)S(1)}, f32[24,4,256]{2,1,0:T(4,128)S(1)}, u32[]{:S(2)}, u32[]{:S(2)}) %collective-permute-start.16) | collective-permute-done | bytes 98336 | tf_op jit(solution)/shard_map/ppermute | solution.py:457
  37.9 2.1 %project_next.1.refs_0_ = f32[24,256]{1,0:T(8,128)S(1)} custom-call(f32[24,4,256]{2,1,0:T(4,128)S(1)} %copy-done.1, f32[24,4,256]{2,1,0:T(4,128)S(1)} %collective-permute-done.10.refs_1_, f32[24,4,256]{2,1,0:T(4,128)S(1)} %collective-permute-done.11.refs_2_, f32[24,4,256]{2,1,0:T(4,128)S(1)} %collective-permute-done.12.refs_3_, ...), custom_call_target="tpu_custom_call" | custom-call | flops 3000000000 | bytes 6291456 | tf_op jit(solution)/shard_map/project_next/pallas_call | solution.py:216
  40.1 0.1 collective-permute-start.17
  40.2 1.6 %collective-permute-start.18 = (f32[24,256]{1,0:T(8,128)S(1)}, f32[24,256]{1,0:T(8,128)S(1)}, u32[]{:S(2)}, u32[]{:S(2)}) collective-permute-start(f32[24,256]{1,0:T(8,128)S(1)} %project_next.1.refs_0_), channel_id=1, source_target_pairs={{0,2},{1,3},{2,0},{3,1},{4,6},{5,7},{6,4},{7,5},{8,10},{9,11},{10,... | collective-permute-start | bytes 73736 | tf_op jit(solution)/shard_map/ppermute | solution.py:457
  41.7 0.3 collective-permute-start.19
  42.0 0.0 copy-start.3
  42.0 6.0 %mix.1 = bf16[256,4,2048]{2,1,0:T(4,128)(2,1)} custom-call(f32[24,256]{1,0:T(8,128)S(1)} %get-tuple-element.10.coef_ref.refs_10_.refs_4_, bf16[16,256,4,128]{3,2,1,0:T(4,128)(2,1)S(1)} %get-tuple-element.11.sil_ref, bf16[256,2048]{1,0:T(8,128)(2,1)S(1)} %copy-done), custom_call_target="tpu_custom_call" | custom-call | flops 5000000000 | bytes 8388608 | tf_op jit(solution)/shard_map/mix/pallas_call | solution.py:361
  48.0 0.0 collective-permute-done.17.refs_1_
  48.0 0.0 collective-permute-done.18.refs_2_
  48.0 0.0 collective-permute-done.19.refs_3_
  48.0 0.0 copy-done.3
  48.0 3.9 %second.1 = (bf16[256,2048]{1,0:T(8,128)(2,1)}, f32[20,256]{1,0:T(8,128)}) custom-call(f32[24,256]{1,0:T(8,128)S(1)} %project_next.1.refs_0_, f32[24,256]{1,0:T(8,128)S(1)} %collective-permute-done.17.refs_1_, f32[24,256]{1,0:T(8,128)S(1)} %collective-permute-done.18.refs_2_, f32[24,256]{1,0:T(8,128)S(1)} %collective-permute-done.19.refs_3_, ...), custom_call_target="tpu_custom_call" | custom-call | flops 3000000000 | bytes 6291456 | tf_op jit(solution)/shard_map/second/pallas_call | solution.py:439
Async XLA Ops:
  0.6 14.6 %copy-start = (bf16[256,2048]{1,0:T(8,128)(2,1)S(1)}, bf16[256,2048]{1,0:T(8,128)(2,1)}, u32[]{:S(2)}) copy-start(bf16[256,2048]{1,0:T(8,128)(2,1)} %refs_9_.3) | copy-start | bytes 3145732
  0.6 12.0 %collective-permute-start.1 = (f32[20,4,256]{2,1,0:T(4,128)}, f32[20,4,256]{2,1,0:T(4,128)S(1)}, u32[]{:S(2)}, u32[]{:S(2)}) collective-permute-start(f32[20,4,256]{2,1,0:T(4,128)} %refs_0_.2), channel_id=1, source_target_pairs={{0,8},{4,12},{8,0},{12,4},{16,24},{20,28},{24,16},{28,20},{1,9},{5... | collective-permute-start | bytes 245768 | tf_op jit(solution)/shard_map/ppermute | solution.py:457
  3.8 9.4 %collective-permute-start.3 = (f32[20,4,256]{2,1,0:T(4,128)}, f32[20,4,256]{2,1,0:T(4,128)S(1)}, u32[]{:S(2)}, u32[]{:S(2)}) collective-permute-start(f32[20,4,256]{2,1,0:T(4,128)} %refs_0_.2), channel_id=1, source_target_pairs={{0,16},{4,20},{8,24},{12,28},{16,0},{20,4},{24,8},{28,12},{1,17},{... | collective-permute-start | bytes 245768 | tf_op jit(solution)/shard_map/ppermute | solution.py:457
  6.3 8.4 %collective-permute-start.5 = (f32[20,4,256]{2,1,0:T(4,128)}, f32[20,4,256]{2,1,0:T(4,128)S(1)}, u32[]{:S(2)}, u32[]{:S(2)}) collective-permute-start(f32[20,4,256]{2,1,0:T(4,128)} %refs_0_.2), channel_id=1, source_target_pairs={{0,24},{4,28},{8,16},{12,20},{16,8},{20,12},{24,0},{28,4},{1,25},{... | collective-permute-start | bytes 245768 | tf_op jit(solution)/shard_map/ppermute | solution.py:457
  6.3 12.6 %collective-permute-start = (f32[20,4,256]{2,1,0:T(4,128)}, f32[20,4,256]{2,1,0:T(4,128)S(1)}, u32[]{:S(2)}, u32[]{:S(2)}) collective-permute-start(f32[20,4,256]{2,1,0:T(4,128)} %refs_0_.2), channel_id=1, source_target_pairs={{0,4},{4,0},{8,12},{12,8},{16,20},{20,16},{24,28},{28,24},{1,5},{5... | collective-permute-start | bytes 245768 | tf_op jit(solution)/shard_map/ppermute | solution.py:457
  8.1 18.0 %collective-permute-start.11 = (f32[24,4,256]{2,1,0:T(4,128)}, f32[24,4,256]{2,1,0:T(4,128)S(1)}, u32[]{:S(2)}, u32[]{:S(2)}) collective-permute-start(f32[24,4,256]{2,1,0:T(4,128)} %refs_0_.3), channel_id=1, source_target_pairs={{0,8},{4,12},{8,0},{12,4},{16,24},{20,28},{24,16},{28,20},{1,9},{5... | collective-permute-start | bytes 294920 | tf_op jit(solution)/shard_map/ppermute | solution.py:457
  12.6 9.9 %collective-permute-start.2 = (f32[20,4,256]{2,1,0:T(4,128)S(1)}, f32[20,4,256]{2,1,0:T(4,128)S(1)}, u32[]{:S(2)}, u32[]{:S(2)}) collective-permute-start(f32[20,4,256]{2,1,0:T(4,128)S(1)} %collective-permute-done.1.refs_2_), channel_id=1, source_target_pairs={{0,4},{4,0},{8,12},{12,8},{16,20},{20,16},{24,28},{28,24},{1,5},{5... | collective-permute-start | bytes 245768 | tf_op jit(solution)/shard_map/ppermute | solution.py:457
  13.2 9.3 %collective-permute-start.4 = (f32[20,4,256]{2,1,0:T(4,128)S(1)}, f32[20,4,256]{2,1,0:T(4,128)S(1)}, u32[]{:S(2)}, u32[]{:S(2)}) collective-permute-start(f32[20,4,256]{2,1,0:T(4,128)S(1)} %collective-permute-done.3.refs_4_), channel_id=1, source_target_pairs={{0,4},{4,0},{8,12},{12,8},{16,20},{20,16},{24,28},{28,24},{1,5},{5... | collective-permute-start | bytes 245768 | tf_op jit(solution)/shard_map/ppermute | solution.py:457
  14.7 7.8 %collective-permute-start.6 = (f32[20,4,256]{2,1,0:T(4,128)S(1)}, f32[20,4,256]{2,1,0:T(4,128)S(1)}, u32[]{:S(2)}, u32[]{:S(2)}) collective-permute-start(f32[20,4,256]{2,1,0:T(4,128)S(1)} %collective-permute-done.5.refs_6_), channel_id=1, source_target_pairs={{0,4},{4,0},{8,12},{12,8},{16,20},{20,16},{24,28},{28,24},{1,5},{5... | collective-permute-start | bytes 245768 | tf_op jit(solution)/shard_map/ppermute | solution.py:457
  15.2 3.7 %copy-start.1 = (f32[24,4,256]{2,1,0:T(4,128)S(1)}, f32[24,4,256]{2,1,0:T(4,128)}, u32[]{:S(2)}) copy-start(f32[24,4,256]{2,1,0:T(4,128)} %refs_0_.3) | copy-start | bytes 294916
  15.2 7.3 %copy-start.2 = (f32[20,4,256]{2,1,0:T(4,128)S(1)}, f32[20,4,256]{2,1,0:T(4,128)}, u32[]{:S(2)}) copy-start(f32[20,4,256]{2,1,0:T(4,128)} %refs_0_.2) | copy-start | bytes 245764
  18.9 13.7 %copy-start.4 = (f32[44]{0:T(128)S(1)}, f32[44]{0:T(128)}, u32[]{:S(2)}) copy-start(f32[44]{0:T(128)} %refs_6_.1) | copy-start | bytes 532
  18.9 13.7 %copy-start.5 = (f32[5]{0:T(128)S(1)}, f32[5]{0:T(128)}, u32[]{:S(2)}) copy-start(f32[5]{0:T(128)} %refs_7_.1) | copy-start | bytes 64
  18.9 8.3 %collective-permute-start.13 = (f32[24,4,256]{2,1,0:T(4,128)S(1)}, f32[24,4,256]{2,1,0:T(4,128)S(1)}, u32[]{:S(2)}, u32[]{:S(2)}) collective-permute-start(f32[24,4,256]{2,1,0:T(4,128)S(1)} %copy-done.1), channel_id=1, source_target_pairs={{0,16},{4,20},{8,24},{12,28},{16,0},{20,4},{24,8},{28,12},{1,17},{... | collective-permute-start | bytes 294920 | tf_op jit(solution)/shard_map/ppermute | solution.py:457
  22.5 6.5 %collective-permute-start.15 = (f32[24,4,256]{2,1,0:T(4,128)S(1)}, f32[24,4,256]{2,1,0:T(4,128)S(1)}, u32[]{:S(2)}, u32[]{:S(2)}) collective-permute-start(f32[24,4,256]{2,1,0:T(4,128)S(1)} %copy-done.1), channel_id=1, source_target_pairs={{0,24},{4,28},{8,16},{12,20},{16,8},{20,12},{24,0},{28,4},{1,25},{... | collective-permute-start | bytes 294920 | tf_op jit(solution)/shard_map/ppermute | solution.py:457
  24.2 6.3 %collective-permute-start.7 = (f32[40,256]{1,0:T(8,128)S(1)}, f32[40,256]{1,0:T(8,128)S(1)}, u32[]{:S(2)}, u32[]{:S(2)}) collective-permute-start(f32[40,256]{1,0:T(8,128)S(1)} %raw.1.refs_0_), channel_id=1, source_target_pairs={{0,1},{1,0},{2,3},{3,2},{4,5},{5,4},{6,7},{7,6},{8,9},{9,8},{10,11... | collective-permute-start | bytes 122888 | tf_op jit(solution)/shard_map/ppermute | solution.py:457
  24.3 6.7 %collective-permute-start.8 = (f32[40,256]{1,0:T(8,128)S(1)}, f32[40,256]{1,0:T(8,128)S(1)}, u32[]{:S(2)}, u32[]{:S(2)}) collective-permute-start(f32[40,256]{1,0:T(8,128)S(1)} %raw.1.refs_0_), channel_id=1, source_target_pairs={{0,2},{1,3},{2,0},{3,1},{4,6},{5,7},{6,4},{7,5},{8,10},{9,11},{10,... | collective-permute-start | bytes 122888 | tf_op jit(solution)/shard_map/ppermute | solution.py:457
  26.1 6.5 %collective-permute-start.9 = (f32[40,256]{1,0:T(8,128)S(1)}, f32[40,256]{1,0:T(8,128)S(1)}, u32[]{:S(2)}, u32[]{:S(2)}) collective-permute-start(f32[40,256]{1,0:T(8,128)S(1)} %raw.1.refs_0_), channel_id=1, source_target_pairs={{0,3},{1,2},{2,1},{3,0},{4,7},{5,6},{6,5},{7,4},{8,11},{9,10},{10,... | collective-permute-start | bytes 122888 | tf_op jit(solution)/shard_map/ppermute | solution.py:457
  27.3 6.1 %collective-permute-start.10 = (f32[24,4,256]{2,1,0:T(4,128)S(1)}, f32[24,4,256]{2,1,0:T(4,128)S(1)}, u32[]{:S(2)}, u32[]{:S(2)}) collective-permute-start(f32[24,4,256]{2,1,0:T(4,128)S(1)} %copy-done.1), channel_id=1, source_target_pairs={{0,4},{4,0},{8,12},{12,8},{16,20},{20,16},{24,28},{28,24},{1,5},{5... | collective-permute-start | bytes 294920 | tf_op jit(solution)/shard_map/ppermute | solution.py:457
  29.0 6.0 %collective-permute-start.12 = (f32[24,4,256]{2,1,0:T(4,128)S(1)}, f32[24,4,256]{2,1,0:T(4,128)S(1)}, u32[]{:S(2)}, u32[]{:S(2)}) collective-permute-start(f32[24,4,256]{2,1,0:T(4,128)S(1)} %collective-permute-done.11.refs_2_), channel_id=1, source_target_pairs={{0,4},{4,0},{8,12},{12,8},{16,20},{20,16},{24,28},{28,24},{1,5},{5... | collective-permute-start | bytes 294920 | tf_op jit(solution)/shard_map/ppermute | solution.py:457
  30.6 6.3 %collective-permute-start.14 = (f32[24,4,256]{2,1,0:T(4,128)S(1)}, f32[24,4,256]{2,1,0:T(4,128)S(1)}, u32[]{:S(2)}, u32[]{:S(2)}) collective-permute-start(f32[24,4,256]{2,1,0:T(4,128)S(1)} %collective-permute-done.13.refs_4_), channel_id=1, source_target_pairs={{0,4},{4,0},{8,12},{12,8},{16,20},{20,16},{24,28},{28,24},{1,5},{5... | collective-permute-start | bytes 294920 | tf_op jit(solution)/shard_map/ppermute | solution.py:457
  31.1 6.9 %collective-permute-start.16 = (f32[24,4,256]{2,1,0:T(4,128)S(1)}, f32[24,4,256]{2,1,0:T(4,128)S(1)}, u32[]{:S(2)}, u32[]{:S(2)}) collective-permute-start(f32[24,4,256]{2,1,0:T(4,128)S(1)} %collective-permute-done.15.refs_6_), channel_id=1, source_target_pairs={{0,4},{4,0},{8,12},{12,8},{16,20},{20,16},{24,28},{28,24},{1,5},{5... | collective-permute-start | bytes 294920 | tf_op jit(solution)/shard_map/ppermute | solution.py:457
  40.1 7.9 %collective-permute-start.17 = (f32[24,256]{1,0:T(8,128)S(1)}, f32[24,256]{1,0:T(8,128)S(1)}, u32[]{:S(2)}, u32[]{:S(2)}) collective-permute-start(f32[24,256]{1,0:T(8,128)S(1)} %project_next.1.refs_0_), channel_id=1, source_target_pairs={{0,1},{1,0},{2,3},{3,2},{4,5},{5,4},{6,7},{7,6},{8,9},{9,8},{10,11... | collective-permute-start | bytes 73736 | tf_op jit(solution)/shard_map/ppermute | solution.py:457
  40.2 7.8 %collective-permute-start.18 = (f32[24,256]{1,0:T(8,128)S(1)}, f32[24,256]{1,0:T(8,128)S(1)}, u32[]{:S(2)}, u32[]{:S(2)}) collective-permute-start(f32[24,256]{1,0:T(8,128)S(1)} %project_next.1.refs_0_), channel_id=1, source_target_pairs={{0,2},{1,3},{2,0},{3,1},{4,6},{5,7},{6,4},{7,5},{8,10},{9,11},{10,... | collective-permute-start | bytes 73736 | tf_op jit(solution)/shard_map/ppermute | solution.py:457
  41.7 6.3 %collective-permute-start.19 = (f32[24,256]{1,0:T(8,128)S(1)}, f32[24,256]{1,0:T(8,128)S(1)}, u32[]{:S(2)}, u32[]{:S(2)}) collective-permute-start(f32[24,256]{1,0:T(8,128)S(1)} %project_next.1.refs_0_), channel_id=1, source_target_pairs={{0,3},{1,2},{2,1},{3,0},{4,7},{5,6},{6,5},{7,4},{8,11},{9,10},{10,... | collective-permute-start | bytes 73736 | tf_op jit(solution)/shard_map/ppermute | solution.py:457
  42.0 6.0 %copy-start.3 = (f32[2048]{0:T(1024)S(1)}, f32[2048]{0:T(1024)}, u32[]{:S(2)}) copy-start(f32[2048]{0:T(1024)} %param.13) | copy-start | bytes 24580

commit v3 on v2

v3 whole, which is shorter than its diff:
```python
import functools

import jax
import jax.numpy as jnp
from jax import lax
from jax.experimental import pallas as pl
from jax.experimental.pallas import tpu as pltpu
from jax.sharding import PartitionSpec as P


BALANCE_ROUNDS = 6
EPS = 1e-06
FB = 256
GT = 64
MT = 16
F32 = jnp.float32
BF16 = jnp.bfloat16
MIB = 2**20

VMEM = pl.BlockSpec(memory_space=pltpu.VMEM)
HBM = pl.BlockSpec(memory_space=pltpu.HBM)

PAIRS = [(i, j) for i in range(4) for j in range(i, 4)]


def _nt(a, b, precision=None):
    return lax.dot_general(
        a, b, (((1,), (1,)), ((), ())), precision=precision, preferred_element_type=F32
    )


def _split(x):
    hi = x.astype(BF16)
    return hi, (x - hi.astype(F32)).astype(BF16)


def _iota(shape, dim):
    return lax.broadcasted_iota(jnp.int32, shape, dim)


def _store_by_column(ref, rows, start):
    ref[0:start, :] = rows[0:start]
    for j in range(4):
        for i in range(4):
            source = start + 4 * j + i
            ref[start + 4 * i + j : start + 4 * i + j + 1, :] = rows[source : source + 1]
    if rows.shape[0] > start + 16:
        ref[start + 16 : rows.shape[0], :] = rows[start + 16 :]


def deal_kernel(s_hbm, sil_ref, sde_ref, q_ref, part_ref, sems):
    tokens, _, width = s_hbm.shape
    rows = 4 * GT
    flat = s_hbm.reshape(4 * tokens, width)

    def copy(c):
        return pltpu.make_async_copy(
            flat.at[:, pl.ds(pl.multiple_of(c * 128, 128), 128)], sil_ref.at[c], sems.at[c]
        )

    for c in range(width // 128):
        copy(c).start()
    r, q = _iota((rows, rows), 0), _iota((rows, rows), 1)
    perm = jnp.where(q == 4 * (r % GT) + r // GT, 1.0, 0.0).astype(BF16)
    part_ref[...] = jnp.zeros_like(part_ref)

    def body(k, _):
        copy(2 * k).wait()
        copy(2 * k + 1).wait()
        for g in range(tokens // GT):
            own, mine = pl.ds(g * rows, rows), pl.ds(g * GT, GT)
            x = jnp.concatenate([sil_ref[2 * k, own, :], sil_ref[2 * k + 1, own, :]], axis=1)
            y = jnp.dot(perm, x, preferred_element_type=F32)
            for i in range(4):
                sde_ref[k, i, mine, :] = y[i * GT : (i + 1) * GT].astype(BF16)
            y = y * y
            y = (y[0:GT] + y[GT : 2 * GT]) + (y[2 * GT : 3 * GT] + y[3 * GT :])
            part_ref[mine, :] += y[:, :128] + y[:, 128:]
        return 0

    lax.fori_loop(0, width // FB, body, 0)
    q_ref[...] = jnp.sum(part_ref[...].T.reshape(16, 8, tokens), axis=0)


def deal(streams):
    tokens, _, width = streams.shape
    tiles = width // 128
    return pl.pallas_call(
        deal_kernel,
        out_shape=(
            jax.ShapeDtypeStruct((tiles, 4 * tokens, 128), BF16),
            jax.ShapeDtypeStruct((width // FB, 4, tokens, FB), BF16),
            jax.ShapeDtypeStruct((8, tokens), F32),
        ),
        in_specs=[HBM],
        out_specs=(VMEM, VMEM, VMEM),
        scratch_shapes=[pltpu.VMEM((tokens, 128), F32), pltpu.SemaphoreType.DMA((tiles,))],
        compiler_params=pltpu.CompilerParams(vmem_limit_bytes=20 * MIB),
        cost_estimate=pl.CostEstimate(
            flops=6_000_000_000, bytes_accessed=10 * MIB, transcendentals=0
        ),
        name="deal",
    )(pltpu.with_memory_space_constraint(streams, pltpu.HBM))


def grams_kernel(sde_ref, b_ref, g_ref, column_ref):
    blocks, _, tokens, _ = sde_ref.shape

    def chunk(c, _):
        at = pl.ds(pl.multiple_of(c * 16, 16), 16)
        sums = [None] * 15
        for k in range(blocks):
            for h in range(FB // 128):
                lanes = slice(h * 128, (h + 1) * 128)
                wide = [sde_ref[k, i, at, lanes].astype(F32) for i in range(4)]
                wide.append(b_ref[at, k * FB + h * 128 : k * FB + (h + 1) * 128].astype(F32))
                products = [wide[i] * wide[j] for i, j in PAIRS]
                products += [wide[i] * wide[4] for i in range(5)]
                sums = [p if s is None else s + p for s, p in zip(sums, products)]
        lane = _iota((16, 128), 1)
        column = jnp.zeros((16, 128), F32)
        for p in range(15):
            column = jnp.where(lane == p, jnp.sum(sums[p], axis=1, keepdims=True), column)
        column_ref[at, :] = column
        return 0

    lax.fori_loop(0, tokens // 16, chunk, 0)
    g_ref[...] = column_ref[...].T[0:16]


def grams_of(sde, branch):
    tokens = sde.shape[2]
    return pl.pallas_call(
        grams_kernel,
        out_shape=jax.ShapeDtypeStruct((16, tokens), F32),
        in_specs=[VMEM, VMEM],
        out_specs=VMEM,
        scratch_shapes=[pltpu.VMEM((tokens, 128), F32)],
        compiler_params=pltpu.CompilerParams(vmem_limit_bytes=8 * MIB),
        cost_estimate=pl.CostEstimate(
            flops=3_000_000_000, bytes_accessed=5 * MIB, transcendentals=0
        ),
        name="grams",
    )(sde, branch)


def _owner(s, permuted):
    return jnp.bitwise_xor(lax.axis_index("dp"), s) if permuted else s


def raw_kernel(permuted, *refs):
    w_refs, (sde_ref, q_ref, out_ref, wide_ref, lhs_ref) = refs[:-5], refs[-5:]
    count = w_refs[0].shape[0]
    pad = wide_ref.shape[1]
    blocks = sde_ref.shape[0]
    wide_ref[...] = jnp.zeros_like(wide_ref)
    for s in range(blocks):
        owner = _owner(s, permuted)
        for i in range(4):
            wide_ref[i, 0:count, :] = w_refs[s][:, i, :]
            hi, lo = _split(wide_ref[i])
            lhs_ref[owner, i, 0:pad, :] = hi
            lhs_ref[owner, i, pad : 2 * pad, :] = lo
    total = None
    for s in range(blocks):
        for i in range(4):
            part = _nt(lhs_ref[s, i], sde_ref[s, i])
            total = part if total is None else total + part
    _store_by_column(out_ref, total[0:20] + total[pad : pad + 20], 4)
    out_ref[20:21, :] = jnp.sum(q_ref[...], axis=0, keepdims=True)
    out_ref[21:24, :] = jnp.zeros((3, out_ref.shape[1]), F32)


def raw(weights, sde, squares, permuted):
    blocks, _, tokens, _ = sde.shape
    return pl.pallas_call(
        functools.partial(raw_kernel, permuted),
        out_shape=jax.ShapeDtypeStruct((24, tokens), F32),
        in_specs=[VMEM] * (len(weights) + 2),
        out_specs=VMEM,
        scratch_shapes=[
            pltpu.VMEM((4, 32, FB), F32),
            pltpu.VMEM((blocks, 4, 64, FB), BF16),
        ],
        compiler_params=pltpu.CompilerParams(vmem_limit_bytes=12 * MIB),
        cost_estimate=pl.CostEstimate(
            flops=2_000_000_000, bytes_accessed=5 * MIB, transcendentals=0
        ),
        name="raw",
    )(*weights, sde, squares)


def pair_kernel(*refs):
    w_refs, out_ref = refs[:-1], refs[-1]
    count = w_refs[0].shape[0]
    for s, w_ref in enumerate(w_refs):
        for j in range(4):
            out_ref[s, j * count : (j + 1) * count, :] = w_ref[:, j, :]


def pair(*weights):
    count = weights[0].shape[0]
    return pl.pallas_call(
        pair_kernel,
        out_shape=jax.ShapeDtypeStruct((len(weights), 4 * count, FB), F32),
        in_specs=[VMEM] * len(weights),
        out_specs=VMEM,
        compiler_params=pltpu.CompilerParams(vmem_limit_bytes=4 * MIB),
        cost_estimate=pl.CostEstimate(flops=100_000_000, bytes_accessed=MIB, transcendentals=0),
        name="pair",
    )(*weights)


def next_kernel(order, permuted, *refs):
    w_refs, (sde_ref, b_ref, coef_ref, g_ref, out_ref, lhs_ref) = refs[:-6], refs[-6:]
    rows = w_refs[0].shape[1]
    count = rows // 4
    blocks = sde_ref.shape[0]
    places = [(w_ref, n) for w_ref in w_refs for n in range(w_ref.shape[0])]
    for s, (w_ref, n) in zip(order, places):
        owner = _owner(s, permuted)
        hi, lo = _split(w_ref[n])
        lhs_ref[owner, 0:rows, :] = hi
        lhs_ref[owner, rows : 2 * rows, :] = lo
    mixed = None
    for i in range(5):
        total = None
        for s in range(blocks):
            right = sde_ref[s, i] if i < 4 else b_ref[:, s * FB : (s + 1) * FB]
            part = _nt(lhs_ref[s], right)
            total = part if total is None else total + part
        total = total[0:rows] + total[rows : 2 * rows]
        for j in range(4):
            part = coef_ref[4 * i + j : 4 * i + j + 1, :] * total[j * count : (j + 1) * count]
            mixed = part if mixed is None else mixed + part
    _store_by_column(out_ref, mixed, 8)
    out_ref[count:, :] = g_ref[...]


def project_next(weights, order, sde, branch, coef, gram, permuted):
    blocks, _, tokens, _ = sde.shape
    rows = weights[0].shape[1]
    return pl.pallas_call(
        functools.partial(next_kernel, order, permuted),
        out_shape=jax.ShapeDtypeStruct((rows // 4 + gram.shape[0], tokens), F32),
        in_specs=[VMEM] * (len(weights) + 4),
        out_specs=VMEM,
        scratch_shapes=[pltpu.VMEM((blocks, 2 * rows, FB), BF16)],
        compiler_params=pltpu.CompilerParams(vmem_limit_bytes=14 * MIB),
        cost_estimate=pl.CostEstimate(
            flops=3_000_000_000, bytes_accessed=6 * MIB, transcendentals=0
        ),
        name="project_next",
    )(*weights, sde, branch, coef, gram)


def _balance(columns):
    for _ in range(BALANCE_ROUNDS):
        inverse = 1.0 / (columns[0] + columns[1] + columns[2] + columns[3])
        columns = [c * inverse for c in columns]
        columns = [c * (1.0 / jnp.sum(c, axis=0, keepdims=True)) for c in columns]
    return columns


def _sum4(refs, at):
    return (refs[0][at] + refs[1][at]) + (refs[2][at] + refs[3][at])


def _column(ref, start, step):
    wide = ref.shape[1]
    here = _iota((4, wide), 1) == start + step * _iota((4, wide), 0)
    return jnp.sum(jnp.where(here, jnp.broadcast_to(ref[...], (4, wide)), 0.0), axis=1, keepdims=True)


def _scored(raw_rows, inverse, scale, bias):
    return scale * (raw_rows * inverse) + bias


def first_kernel(features, *refs):
    r_refs = refs[0:4]
    bias_ref, scale_ref, coef_ref = refs[4:]
    squares = _sum4(r_refs, (slice(20, 21), slice(None)))
    inverse = 1.0 / jnp.sqrt(squares / features + EPS)
    raw_post = _sum4(r_refs, (slice(0, 4), slice(None)))
    score = _scored(raw_post, inverse, _column(scale_ref, 0, 0), _column(bias_ref, 0, 1))
    coef_ref[16:20, :] = 2.0 * jax.nn.sigmoid(score)
    columns = []
    for i in range(4):
        raw_rows = _sum4(r_refs, (slice(4 + 4 * i, 8 + 4 * i), slice(None)))
        score = _scored(raw_rows, inverse, _column(scale_ref, 1, 0), _column(bias_ref, 4 + i, 4))
        columns.append(jnp.exp(score))
    columns = _balance(columns)
    for i in range(4):
        coef_ref[4 * i : 4 * i + 4, :] = columns[i]
    coef_ref[20:24, :] = jnp.zeros_like(coef_ref[20:24, :])


def first(raws, bias, scale, features):
    tokens = raws[0].shape[1]
    return pl.pallas_call(
        functools.partial(first_kernel, features),
        out_shape=jax.ShapeDtypeStruct((24, tokens), F32),
        in_specs=[VMEM] * 6,
        out_specs=VMEM,
        compiler_params=pltpu.CompilerParams(vmem_limit_bytes=4 * MIB),
        cost_estimate=pl.CostEstimate(
            flops=1_000_000_000, bytes_accessed=MIB, transcendentals=20000
        ),
        name="first",
    )(*raws, bias, scale)


def weave_kernel(coef_ref, left_ref):
    tokens = coef_ref.shape[1]
    rows = 4 * MT
    wide = 2 * rows + 2 * MT
    m, q = _iota((64, wide), 0), _iota((64, wide), 1)
    of_branch = q >= 2 * rows
    low = jnp.where(of_branch, (q - 2 * rows) // MT, q // rows)
    source = jnp.where(of_branch, 4, q % 4)
    pick = jnp.where(m // 4 == low * 8 + source, 1.0, 0.0).astype(BF16)
    r, q = _iota((rows, wide), 0), _iota((rows, wide), 1)
    token = jnp.where(q >= 2 * rows, (q - 2 * rows) % MT, (q % rows) // 4)
    same = token == r // 4
    r, m = _iota((rows, 64), 0), _iota((rows, 64), 1)
    keep = (m % 4) == (r % 4)
    hi, lo = _split(jnp.concatenate([coef_ref[...], jnp.zeros((8, tokens), F32)], axis=0))
    coef = jnp.concatenate([hi, lo], axis=0)
    for g in range(tokens // MT):
        start = g * MT // 128 * 128
        lane, r = _iota((rows, 128), 1), _iota((rows, 128), 0)
        expand = jnp.where(lane == g * MT - start + r // 4, 1.0, 0.0).astype(BF16)
        held = _nt(expand, coef[:, start : start + 128])
        held = jnp.where(keep, held, 0.0).astype(BF16)
        spread = jnp.dot(held, pick, preferred_element_type=F32)
        left_ref[g] = jnp.where(same, spread, 0.0).astype(BF16)


def weave(coef):
    tokens = coef.shape[1]
    return pl.pallas_call(
        weave_kernel,
        out_shape=jax.ShapeDtypeStruct((tokens // MT, 4 * MT, 10 * MT), BF16),
        in_specs=[VMEM],
        out_specs=VMEM,
        compiler_params=pltpu.CompilerParams(vmem_limit_bytes=6 * MIB),
        cost_estimate=pl.CostEstimate(
            flops=1_000_000_000, bytes_accessed=MIB, transcendentals=0
        ),
        name="weave",
    )(coef)


def mix_kernel(left_ref, sil_ref, b_ref, out_hbm, stage_ref, sems):
    tiles, tokens = sil_ref.shape[0], sil_ref.shape[1] // 4
    rows = 4 * MT
    flat = out_hbm.reshape(4 * tokens, tiles * 128)

    def copy(c):
        return pltpu.make_async_copy(
            stage_ref.at[c], flat.at[:, pl.ds(pl.multiple_of(c * 128, 128), 128)], sems.at[c]
        )

    def body(k, _):
        lanes = pl.ds(pl.multiple_of(k * FB, FB), FB)
        for g in range(tokens // MT):
            own = pl.ds(g * rows, rows)
            x = jnp.concatenate([sil_ref[2 * k, own, :], sil_ref[2 * k + 1, own, :]], axis=1)
            b = b_ref[pl.ds(g * MT, MT), lanes]
            right = jnp.concatenate([x, x, b, b], axis=0)
            y = jnp.dot(left_ref[g], right, preferred_element_type=F32)
            y = y.astype(BF16)
            stage_ref[2 * k, own, :] = y[:, :128]
            stage_ref[2 * k + 1, own, :] = y[:, 128:]
        copy(2 * k).start()
        copy(2 * k + 1).start()
        return 0

    lax.fori_loop(0, tiles // 2, body, 0)
    for c in range(tiles):
        copy(c).wait()


def mix(left, sil, branch):
    tiles, tokens = sil.shape[0], sil.shape[1] // 4
    return pl.pallas_call(
        mix_kernel,
        out_shape=jax.ShapeDtypeStruct((tokens, 4, tiles * 128), BF16),
        in_specs=[VMEM, VMEM, VMEM],
        out_specs=HBM,
        scratch_shapes=[
            pltpu.VMEM((tiles, 4 * tokens, 128), BF16),
            pltpu.SemaphoreType.DMA((tiles,)),
        ],
        compiler_params=pltpu.CompilerParams(vmem_limit_bytes=14 * MIB),
        cost_estimate=pl.CostEstimate(
            flops=5_000_000_000, bytes_accessed=8 * MIB, transcendentals=0
        ),
        name="mix",
    )(left, sil, branch)


def second_kernel(features, *refs):
    r_refs = refs[0:4]
    coef_ref, bias_ref, scale_ref, sde_ref, b_ref, gain_ref = refs[4:10]
    out_hbm, mix_hbm, mix_ref, column_ref, out_ref, sems, mix_sem = refs[10:]
    tokens, _ = b_ref.shape
    gram = _sum4(r_refs, (slice(24, 40), slice(None)))
    columns = [coef_ref[4 * i : 4 * i + 4, :] for i in range(5)]

    def quadratic(terms):
        total = None
        for p, (i, j) in enumerate(PAIRS):
            part = terms[i] * terms[j] * gram[p : p + 1]
            part = part if i == j else 2.0 * part
            total = part if total is None else total + part
        for i in range(4):
            total = total + 2.0 * (terms[i] * terms[4]) * gram[10 + i : 11 + i]
        return total + terms[4] * terms[4] * gram[14:15]

    squares = jnp.maximum(jnp.sum(quadratic(columns), axis=0, keepdims=True), 0.0)
    inverse = 1.0 / jnp.sqrt(squares / features + EPS)
    everything = slice(None)
    pre_raw = _sum4(r_refs, (slice(0, 4), everything))
    score = _scored(pre_raw, inverse, _column(scale_ref, 2, 0), _column(bias_ref, 20, 1))
    pre_next = jax.nn.sigmoid(score)
    post_raw = _sum4(r_refs, (slice(4, 8), everything))
    score = _scored(post_raw, inverse, _column(scale_ref, 3, 0), _column(bias_ref, 24, 1))
    mix_ref[0:4, :] = 2.0 * jax.nn.sigmoid(score)
    following = []
    for i in range(4):
        raw_rows = _sum4(r_refs, (slice(8 + 4 * i, 12 + 4 * i), everything))
        score = _scored(raw_rows, inverse, _column(scale_ref, 4, 0), _column(bias_ref, 28 + i, 4))
        following.append(jnp.exp(score))
    following = _balance(following)
    for i in range(4):
        for j in range(4):
            mix_ref[4 + 4 * j + i : 5 + 4 * j + i, :] = following[i][j : j + 1]
    mix_copy = pltpu.make_async_copy(mix_ref, mix_hbm, mix_sem)
    mix_copy.start()

    joint = [jnp.sum(pre_next * c, axis=0, keepdims=True) for c in columns]
    united = jnp.maximum(quadratic(joint), 0.0)
    root = 1.0 / jnp.sqrt(united / (features // 4) + EPS)
    stacked = jnp.concatenate([j * root for j in joint] + [jnp.zeros((3, tokens), F32)], axis=0)
    column_ref[:, 0:8] = stacked.T
    blocks = sde_ref.shape[0]

    def copy(c):
        at = pl.ds(pl.multiple_of(c * 16, 16), 16)
        return pltpu.make_async_copy(out_ref.at[at], out_hbm.at[at], sems.at[c])

    def body(c, _):
        at = pl.ds(pl.multiple_of(c * 16, 16), 16)
        weights = [column_ref[at, i : i + 1] for i in range(5)]
        for k in range(blocks):
            lanes = pl.ds(k * FB, FB)
            total = weights[4] * b_ref[at, lanes].astype(F32)
            for i in range(4):
                total = total + weights[i] * sde_ref[k, i, at, :].astype(F32)
            out_ref[at, lanes] = (total * gain_ref[:, lanes]).astype(BF16)
        copy(c).start()
        return 0

    lax.fori_loop(0, tokens // 16, body, 0)
    for c in range(tokens // 16):
        copy(c).wait()
    mix_copy.wait()


def second(raws, coef, bias, scale, sde, branch, gain, features):
    tokens, width = branch.shape
    return pl.pallas_call(
        functools.partial(second_kernel, features),
        out_shape=(
            jax.ShapeDtypeStruct((tokens, width), BF16),
            jax.ShapeDtypeStruct((20, tokens), F32),
        ),
        in_specs=[VMEM] * 10,
        out_specs=(HBM, HBM),
        scratch_shapes=[
            pltpu.VMEM((20, tokens), F32),
            pltpu.VMEM((tokens, 128), F32),
            pltpu.VMEM((tokens, width), BF16),
            pltpu.SemaphoreType.DMA((tokens // 16,)),
            pltpu.SemaphoreType.DMA,
        ],
        compiler_params=pltpu.CompilerParams(vmem_limit_bytes=14 * MIB),
        cost_estimate=pl.CostEstimate(
            flops=3_000_000_000, bytes_accessed=6 * MIB, transcendentals=20000
        ),
        name="second",
    )(*raws, coef, bias, scale, sde, branch, gain)


def _swap(x, axis, count, s):
    return lax.ppermute(x, axis, [(i, i ^ s) for i in range(count)])


def by_block(weight, width):
    whole = lax.all_gather(weight, "dp", axis=2, tiled=True)
    return [whole[:, :, k * FB : (k + 1) * FB] for k in range(width // FB)]


def gather_merge(weight, count, width):
    if count != 8 or count * weight.shape[2] != width or weight.shape[2] != FB:
        return by_block(weight, width), False
    blocks = {0: weight}
    for s in (2, 4, 6):
        blocks[s] = _swap(weight, "dp", count, s)
    for s in (0, 2, 4, 6):
        blocks[s + 1] = _swap(blocks[s], "dp", count, 1)
    return [blocks[s] for s in range(count)], True


def gather_next(weight, count, width):
    if count != 8 or count * weight.shape[2] != width or weight.shape[2] != FB:
        return [pair(*by_block(weight, width))], tuple(range(width // FB))
    far = _swap(weight, "dp", count, 2)
    here = pair(weight, far)
    there = _swap(here, "dp", count, 4)
    near = _swap(here, "dp", count, 1)
    across = _swap(there, "dp", count, 1)
    return [here, near, there, across], (0, 2, 1, 3, 4, 6, 5, 7)


def everyone(x, count):
    return [x] + [_swap(x, "mp", count, s) for s in range(1, count)]


def solution(mesh):
    n_dp, n_mp = mesh.shape["dp"], mesh.shape["mp"]

    def local(streams, branch, merge_weight, next_weight, blend_bias, blend_scale, norm_gain):
        count, width = streams.shape[1:]
        features = count * width * n_mp
        merge_blocks, permuted = gather_merge(merge_weight, n_dp, width)
        next_blocks, order = gather_next(next_weight, n_dp, width)
        gain, bias, scale = norm_gain[None, :], blend_bias[None, :], blend_scale[None, :]
        sil, sde, squares = deal(streams)
        gram = grams_of(sde, branch)
        raws = everyone(raw(merge_blocks, sde, squares, permuted), n_mp)
        coef = first(raws, bias, scale, features)
        streams_out = mix(weave(coef), sil, branch)
        next_raw = project_next(next_blocks, order, sde, branch, coef, gram, permuted)
        next_raws = everyone(next_raw, n_mp)
        branch_in, next_mix = second(
            next_raws, coef, bias, scale, sde, branch, gain, features
        )
        return streams_out, branch_in, next_mix.T

    placed = (
        P("dp", None, "mp"),
        P("dp", "mp"),
        P(None, None, ("mp", "dp")),
        P(None, None, ("mp", "dp")),
        P(),
        P(),
        P("mp"),
    )
    return jax.shard_map(
        local,
        mesh=mesh,
        in_specs=placed,
        out_specs=(P("dp", None, "mp"), P("dp", "mp"), P("dp", None)),
        check_vma=False,
    )
```

time: 52.1 us -> 45.4 us (0.87)
  waiting for transfers between devices: 5.97 us -> 2.22 us
  starting transfers between devices: 23.2 us -> 20.4 us
  Pallas kernels: 22 us -> 20.8 us
  local copies, waits for them, and re-layouts: 0.02 us -> 0.92 us
    ppermute x20 -> x17, waiting for transfers between devices: 5.97 us -> 2.22 us  [_swap(): return lax.ppermute(x, axis, [(i, i ^ s) for i in range(count)])]
    ppermute x20 -> x17, starting transfers between devices: 23.2 us -> 20.4 us  [_swap(): return lax.ppermute(x, axis, [(i, i ^ s) for i in range(count)])]
    pallas_call x1, Pallas kernels: 5.95 us -> 3.71 us  [mix(): pl.pallas_call(mix_kernel, out_shape=jax.ShapeDtypeStruct((tokens, 4, til...]
    pallas_call x3 -> x5, Pallas kernels: 6.7 us -> 8.41 us  [the longest x1 3.9 us: deal(): pl.pallas_call(deal_kernel, out_shape=(jax.ShapeDtypeStruct((tiles, 4 * t...]
    unnamed x12, local copies, waits for them, and re-layouts: 0.02 us -> 0.92 us
    pallas_call x1, Pallas kernels: 3.95 us -> 3.3 us  [second(): pl.pallas_call(functools.partial(second_kernel, features), out_shape=(jax...]
  transfers between devices with their start and end apart: 20 -> 17, of which waited for: 5 -> 2; matrix products, arithmetic and copies ran while one was open for 0% -> 0% of each run, Pallas kernels for 31% -> 34%
where the time goes in v3:
time: 45.4 us; the launch traced here: 45.3 us
  Pallas kernels  20.8 us (46%)
  starting transfers between devices  20.4 us (45%)
  waiting for transfers between devices  2.22 us (5%)
  local copies, waits for them, and re-layouts  0.92 us (2%)
  between operations  0.83 us (2%)
    ppermute x17, starting transfers between devices, _swap(): return lax.ppermute(x, axis, [(i, i ^ s) for i in range(count)])  20.4 us
    pallas_call x1, Pallas kernels, deal(): pl.pallas_call(deal_kernel, out_shape=(jax.ShapeDtypeStruct((tiles, 4 * t...  3.9 us
    pallas_call x1, Pallas kernels, mix(): pl.pallas_call(mix_kernel, out_shape=jax.ShapeDtypeStruct((tokens, 4, til...  3.71 us
    pallas_call x1, Pallas kernels, grams_of(): pl.pallas_call(grams_kernel, out_shape=jax.ShapeDtypeStruct((16, tokens),...  3.71 us
    pallas_call x1, Pallas kernels, second(): pl.pallas_call(functools.partial(second_kernel, features), out_shape=(jax...  3.3 us
    pallas_call x1, Pallas kernels, weave(): pl.pallas_call(weave_kernel, out_shape=jax.ShapeDtypeStruct((tokens // MT...  2.28 us
    ppermute x17, waiting for transfers between devices, _swap(): return lax.ppermute(x, axis, [(i, i ^ s) for i in range(count)])  2.22 us
    pallas_call x1, Pallas kernels, project_next(): pl.pallas_call(functools.partial(next_kernel, order, permuted), out_shape...  1.91 us
  transfers between devices with their start and end apart: 17, of which 2 were waited for; matrix products, arithmetic and copies ran while one was open for 0% of the time, Pallas kernels for 34%

profile of v3, /device:TPU:0, one launch (start us, length us, event | category | flops | bytes accessed | tf_op | source)
XLA Modules:
  0.0 45.3 jit_solution(15348851554717894470)
XLA Ops:
  0.6 3.1 %collective-permute-start.10 = (f32[24,4,256]{2,1,0:T(4,128)}, f32[24,4,256]{2,1,0:T(4,128)S(1)}, u32[]{:S(2)}, u32[]{:S(2)}) collective-permute-start(f32[24,4,256]{2,1,0:T(4,128)} %refs_0_.3), channel_id=1, source_target_pairs={{0,8},{4,12},{8,0},{12,4},{16,24},{20,28},{24,16},{28,20},{1,9},{5... | collective-permute-start | bytes 294920 | tf_op jit(solution)/shard_map/ppermute | solution.py:497
  3.7 2.6 %collective-permute-start.3 = (f32[20,4,256]{2,1,0:T(4,128)}, f32[20,4,256]{2,1,0:T(4,128)S(1)}, u32[]{:S(2)}, u32[]{:S(2)}) collective-permute-start(f32[20,4,256]{2,1,0:T(4,128)} %refs_0_.2), channel_id=1, source_target_pairs={{0,16},{4,20},{8,24},{12,28},{16,0},{20,4},{24,8},{28,12},{1,17},{... | collective-permute-start | bytes 245768 | tf_op jit(solution)/shard_map/ppermute | solution.py:497
  6.3 0.4 collective-permute-start.1
  6.8 1.3 %collective-permute-start.5 = (f32[20,4,256]{2,1,0:T(4,128)}, f32[20,4,256]{2,1,0:T(4,128)S(1)}, u32[]{:S(2)}, u32[]{:S(2)}) collective-permute-start(f32[20,4,256]{2,1,0:T(4,128)} %refs_0_.2), channel_id=1, source_target_pairs={{0,24},{4,28},{8,16},{12,20},{16,8},{20,12},{24,0},{28,4},{1,25},{... | collective-permute-start | bytes 245768 | tf_op jit(solution)/shard_map/ppermute | solution.py:497
  8.1 1.5 %collective-permute-start = (f32[20,4,256]{2,1,0:T(4,128)}, f32[20,4,256]{2,1,0:T(4,128)S(1)}, u32[]{:S(2)}, u32[]{:S(2)}) collective-permute-start(f32[20,4,256]{2,1,0:T(4,128)} %refs_0_.2), channel_id=1, source_target_pairs={{0,4},{4,0},{8,12},{12,8},{16,20},{20,16},{24,28},{28,24},{1,5},{5... | collective-permute-start | bytes 245768 | tf_op jit(solution)/shard_map/ppermute | solution.py:497
  9.7 0.5 %collective-permute-done.3.refs_4_ = f32[20,4,256]{2,1,0:T(4,128)S(1)} collective-permute-done((f32[20,4,256]{2,1,0:T(4,128)}, f32[20,4,256]{2,1,0:T(4,128)S(1)}, u32[]{:S(2)}, u32[]{:S(2)}) %collective-permute-start.3) | collective-permute-done | bytes 81952 | tf_op jit(solution)/shard_map/ppermute | solution.py:497
  10.2 1.5 %collective-permute-start.4 = (f32[20,4,256]{2,1,0:T(4,128)S(1)}, f32[20,4,256]{2,1,0:T(4,128)S(1)}, u32[]{:S(2)}, u32[]{:S(2)}) collective-permute-start(f32[20,4,256]{2,1,0:T(4,128)S(1)} %collective-permute-done.3.refs_4_), channel_id=1, source_target_pairs={{0,4},{4,0},{8,12},{12,8},{16,20},{20,16},{24,28},{28,24},{1,5},{5... | collective-permute-start | bytes 245768 | tf_op jit(solution)/shard_map/ppermute | solution.py:497
  11.7 0.0 collective-permute-done.1.refs_2_
  11.7 0.8 %collective-permute-start.2 = (f32[20,4,256]{2,1,0:T(4,128)S(1)}, f32[20,4,256]{2,1,0:T(4,128)S(1)}, u32[]{:S(2)}, u32[]{:S(2)}) collective-permute-start(f32[20,4,256]{2,1,0:T(4,128)S(1)} %collective-permute-done.1.refs_2_), channel_id=1, source_target_pairs={{0,4},{4,0},{8,12},{12,8},{16,20},{20,16},{24,28},{28,24},{1,5},{5... | collective-permute-start | bytes 245768 | tf_op jit(solution)/shard_map/ppermute | solution.py:497
  12.6 1.6 %collective-permute-done.5.refs_6_ = f32[20,4,256]{2,1,0:T(4,128)S(1)} collective-permute-done((f32[20,4,256]{2,1,0:T(4,128)}, f32[20,4,256]{2,1,0:T(4,128)S(1)}, u32[]{:S(2)}, u32[]{:S(2)}) %collective-permute-start.5) | collective-permute-done | bytes 81952 | tf_op jit(solution)/shard_map/ppermute | solution.py:497
  14.2 1.5 %collective-permute-start.6 = (f32[20,4,256]{2,1,0:T(4,128)S(1)}, f32[20,4,256]{2,1,0:T(4,128)S(1)}, u32[]{:S(2)}, u32[]{:S(2)}) collective-permute-start(f32[20,4,256]{2,1,0:T(4,128)S(1)} %collective-permute-done.5.refs_6_), channel_id=1, source_target_pairs={{0,4},{4,0},{8,12},{12,8},{16,20},{20,16},{24,28},{28,24},{1,5},{5... | collective-permute-start | bytes 245768 | tf_op jit(solution)/shard_map/ppermute | solution.py:497
  15.7 0.0 collective-permute-done.10.refs_1_
  15.7 0.0 copy-start
  15.7 0.9 %copy-done = f32[24,4,256]{2,1,0:T(4,128)S(1)} copy-done((f32[24,4,256]{2,1,0:T(4,128)S(1)}, f32[24,4,256]{2,1,0:T(4,128)}, u32[]{:S(2)}) %copy-start) | copy-done | bytes 98328
  16.6 0.1 pair.1.refs_0_
  16.7 0.0 copy-start.2
  16.7 1.6 %collective-permute-start.12 = (f32[2,96,256]{2,1,0:T(8,128)S(1)}, f32[2,96,256]{2,1,0:T(8,128)S(1)}, u32[]{:S(2)}, u32[]{:S(2)}) collective-permute-start(f32[2,96,256]{2,1,0:T(8,128)S(1)} %pair.1.refs_0_), channel_id=1, source_target_pairs={{0,16},{4,20},{8,24},{12,28},{16,0},{20,4},{24,8},{28,12},{1,17},{... | collective-permute-start | bytes 589832 | tf_op jit(solution)/shard_map/ppermute | solution.py:497
  18.3 3.9 %deal.1 = (bf16[16,1024,128]{2,1,0:T(8,128)(2,1)S(1)}, bf16[8,4,256,256]{3,2,1,0:T(8,128)(2,1)S(1)}, f32[8,256]{1,0:T(8,128)S(1)}) custom-call(bf16[256,4,2048]{2,1,0:T(4,128)(2,1)} %s_hbm.1), custom_call_target="tpu_custom_call" | custom-call | flops 6000000000 | bytes 10485760 | tf_op jit(solution)/shard_map/deal/pallas_call | solution.py:88
  22.2 0.0 copy-start.1
  22.2 0.0 collective-permute-done.refs_1_
  22.2 0.6 %collective-permute-start.11 = (f32[2,96,256]{2,1,0:T(8,128)S(1)}, f32[2,96,256]{2,1,0:T(8,128)S(1)}, u32[]{:S(2)}, u32[]{:S(2)}) collective-permute-start(f32[2,96,256]{2,1,0:T(8,128)S(1)} %pair.1.refs_0_), channel_id=1, source_target_pairs={{0,4},{4,0},{8,12},{12,8},{16,20},{20,16},{24,28},{28,24},{1,5},{5... | collective-permute-start | bytes 589832 | tf_op jit(solution)/shard_map/ppermute | solution.py:497
  22.8 0.0 collective-permute-done.4.refs_5_
  22.8 0.0 collective-permute-done.2.refs_3_
  22.8 0.0 collective-permute-done.6.refs_7_
  22.8 0.0 copy-done.2
  22.8 1.7 %raw.1.refs_0_ = f32[24,256]{1,0:T(8,128)S(1)} custom-call(f32[20,4,256]{2,1,0:T(4,128)S(1)} %copy-done.2, f32[20,4,256]{2,1,0:T(4,128)S(1)} %collective-permute-done.refs_1_, f32[20,4,256]{2,1,0:T(4,128)S(1)} %collective-permute-done.1.refs_2_, f32[20,4,256]{2,1,0:T(4,128)S(1)} %collective-permute-done.2.refs_3_, ...), custom_call_target="tpu_custom_call" | custom-call | flops 2000000000 | bytes 5242880 | tf_op jit(solution)/shard_map/raw/pallas_call | solution.py:176
  24.5 0.0 copy-start.4
  24.5 0.0 copy-start.5
  24.6 0.1 collective-permute-start.9
  24.6 1.6 %collective-permute-start.8 = (f32[24,256]{1,0:T(8,128)S(1)}, f32[24,256]{1,0:T(8,128)S(1)}, u32[]{:S(2)}, u32[]{:S(2)}) collective-permute-start(f32[24,256]{1,0:T(8,128)S(1)} %raw.1.refs_0_), channel_id=1, source_target_pairs={{0,2},{1,3},{2,0},{3,1},{4,6},{5,7},{6,4},{7,5},{8,10},{9,11},{10,... | collective-permute-start | bytes 73736 | tf_op jit(solution)/shard_map/ppermute | solution.py:497
  26.2 0.3 collective-permute-start.7
  26.5 0.0 collective-permute-done.12.refs_2_
  26.5 1.5 %collective-permute-start.13 = (f32[2,96,256]{2,1,0:T(8,128)S(1)}, f32[2,96,256]{2,1,0:T(8,128)S(1)}, u32[]{:S(2)}, u32[]{:S(2)}) collective-permute-start(f32[2,96,256]{2,1,0:T(8,128)S(1)} %collective-permute-done.12.refs_2_), channel_id=1, source_target_pairs={{0,4},{4,0},{8,12},{12,8},{16,20},{20,16},{24,28},{28,24},{1,5},{5... | collective-permute-start | bytes 589832 | tf_op jit(solution)/shard_map/ppermute | solution.py:497
  28.0 0.0 copy-done.1
  28.0 3.7 %grams.1.refs_7_ = f32[16,256]{1,0:T(8,128)S(1)} custom-call(bf16[8,4,256,256]{3,2,1,0:T(8,128)(2,1)S(1)} %get-tuple-element.8.refs_8_.sde_ref.refs_4_.refs_7_, bf16[256,2048]{1,0:T(8,128)(2,1)S(1)} %copy-done.1), custom_call_target="tpu_custom_call" | custom-call | flops 3000000000 | bytes 5242880 | tf_op jit(solution)/shard_map/grams/pallas_call | solution.py:133
  31.7 0.0 collective-permute-done.9.refs_3_
  31.7 0.0 collective-permute-done.8.refs_2_
  31.7 0.0 collective-permute-done.7.refs_1_
  31.8 0.0 copy-done.4
  31.8 0.0 copy-done.5
  31.8 0.3 first.1.coef_ref.refs_6_.refs_4_
  32.0 2.3 %weave.1.left_ref = bf16[16,64,160]{2,1,0:T(8,128)(2,1)S(1)} custom-call(f32[24,256]{1,0:T(8,128)S(1)} %first.1.coef_ref.refs_6_.refs_4_), custom_call_target="tpu_custom_call" | custom-call | flops 1000000000 | bytes 1048576 | tf_op jit(solution)/shard_map/weave/pallas_call | solution.py:341
  34.3 0.0 collective-permute-done.11.refs_1_
  34.3 0.0 collective-permute-done.13.refs_3_
  34.3 1.9 %project_next.1.refs_0_ = f32[40,256]{1,0:T(8,128)S(1)} custom-call(f32[2,96,256]{2,1,0:T(8,128)S(1)} %pair.1.refs_0_, f32[2,96,256]{2,1,0:T(8,128)S(1)} %collective-permute-done.11.refs_1_, f32[2,96,256]{2,1,0:T(8,128)S(1)} %collective-permute-done.12.refs_2_, f32[2,96,256]{2,1,0:T(8,128)S(1)} %collective-permute-done.13.refs_3_, ...), custom_call_target="tpu_custom_call" | custom-call | flops 3000000000 | bytes 6291456 | tf_op jit(solution)/shard_map/project_next/pallas_call | solution.py:243
  36.3 0.9 %collective-permute-start.16 = (f32[40,256]{1,0:T(8,128)S(1)}, f32[40,256]{1,0:T(8,128)S(1)}, u32[]{:S(2)}, u32[]{:S(2)}) collective-permute-start(f32[40,256]{1,0:T(8,128)S(1)} %project_next.1.refs_0_), channel_id=1, source_target_pairs={{0,3},{1,2},{2,1},{3,0},{4,7},{5,6},{6,5},{7,4},{8,11},{9,10},{10,... | collective-permute-start | bytes 122888 | tf_op jit(solution)/shard_map/ppermute | solution.py:497
  37.2 0.7 %collective-permute-start.15 = (f32[40,256]{1,0:T(8,128)S(1)}, f32[40,256]{1,0:T(8,128)S(1)}, u32[]{:S(2)}, u32[]{:S(2)}) collective-permute-start(f32[40,256]{1,0:T(8,128)S(1)} %project_next.1.refs_0_), channel_id=1, source_target_pairs={{0,2},{1,3},{2,0},{3,1},{4,6},{5,7},{6,4},{7,5},{8,10},{9,11},{10,... | collective-permute-start | bytes 122888 | tf_op jit(solution)/shard_map/ppermute | solution.py:497
  37.9 0.3 collective-permute-start.14
  38.2 0.0 copy-start.3
  38.2 3.7 %mix.1 = bf16[256,4,2048]{2,1,0:T(4,128)(2,1)} custom-call(bf16[16,64,160]{2,1,0:T(8,128)(2,1)S(1)} %weave.1.left_ref, bf16[16,1024,128]{2,1,0:T(8,128)(2,1)S(1)} %get-tuple-element.10.sil_ref, bf16[256,2048]{1,0:T(8,128)(2,1)S(1)} %copy-done.1), custom_call_target="tpu_custom_call" | custom-call | flops 5000000000 | bytes 8388608 | tf_op jit(solution)/shard_map/mix/pallas_call | solution.py:386
  41.9 0.0 collective-permute-done.16.refs_3_
  41.9 0.0 collective-permute-done.15.refs_2_
  41.9 0.0 collective-permute-done.14.refs_1_
  41.9 0.0 copy-done.3
  42.0 3.3 %second.1 = (bf16[256,2048]{1,0:T(8,128)(2,1)}, f32[20,256]{1,0:T(8,128)}) custom-call(f32[40,256]{1,0:T(8,128)S(1)} %project_next.1.refs_0_, f32[40,256]{1,0:T(8,128)S(1)} %collective-permute-done.14.refs_1_, f32[40,256]{1,0:T(8,128)S(1)} %collective-permute-done.15.refs_2_, f32[40,256]{1,0:T(8,128)S(1)} %collective-permute-done.16.refs_3_, ...), custom_call_target="tpu_custom_call" | custom-call | flops 3000000000 | bytes 6291456 | tf_op jit(solution)/shard_map/second/pallas_call | solution.py:473
Async XLA Ops:
  0.6 15.1 %collective-permute-start.10 = (f32[24,4,256]{2,1,0:T(4,128)}, f32[24,4,256]{2,1,0:T(4,128)S(1)}, u32[]{:S(2)}, u32[]{:S(2)}) collective-permute-start(f32[24,4,256]{2,1,0:T(4,128)} %refs_0_.3), channel_id=1, source_target_pairs={{0,8},{4,12},{8,0},{12,4},{16,24},{20,28},{24,16},{28,20},{1,9},{5... | collective-permute-start | bytes 294920 | tf_op jit(solution)/shard_map/ppermute | solution.py:497
  3.7 6.5 %collective-permute-start.3 = (f32[20,4,256]{2,1,0:T(4,128)}, f32[20,4,256]{2,1,0:T(4,128)S(1)}, u32[]{:S(2)}, u32[]{:S(2)}) collective-permute-start(f32[20,4,256]{2,1,0:T(4,128)} %refs_0_.2), channel_id=1, source_target_pairs={{0,16},{4,20},{8,24},{12,28},{16,0},{20,4},{24,8},{28,12},{1,17},{... | collective-permute-start | bytes 245768 | tf_op jit(solution)/shard_map/ppermute | solution.py:497
  6.3 5.4 %collective-permute-start.1 = (f32[20,4,256]{2,1,0:T(4,128)}, f32[20,4,256]{2,1,0:T(4,128)S(1)}, u32[]{:S(2)}, u32[]{:S(2)}) collective-permute-start(f32[20,4,256]{2,1,0:T(4,128)} %refs_0_.2), channel_id=1, source_target_pairs={{0,8},{4,12},{8,0},{12,4},{16,24},{20,28},{24,16},{28,20},{1,9},{5... | collective-permute-start | bytes 245768 | tf_op jit(solution)/shard_map/ppermute | solution.py:497
  6.8 7.4 %collective-permute-start.5 = (f32[20,4,256]{2,1,0:T(4,128)}, f32[20,4,256]{2,1,0:T(4,128)S(1)}, u32[]{:S(2)}, u32[]{:S(2)}) collective-permute-start(f32[20,4,256]{2,1,0:T(4,128)} %refs_0_.2), channel_id=1, source_target_pairs={{0,24},{4,28},{8,16},{12,20},{16,8},{20,12},{24,0},{28,4},{1,25},{... | collective-permute-start | bytes 245768 | tf_op jit(solution)/shard_map/ppermute | solution.py:497
  8.1 14.1 %collective-permute-start = (f32[20,4,256]{2,1,0:T(4,128)}, f32[20,4,256]{2,1,0:T(4,128)S(1)}, u32[]{:S(2)}, u32[]{:S(2)}) collective-permute-start(f32[20,4,256]{2,1,0:T(4,128)} %refs_0_.2), channel_id=1, source_target_pairs={{0,4},{4,0},{8,12},{12,8},{16,20},{20,16},{24,28},{28,24},{1,5},{5... | collective-permute-start | bytes 245768 | tf_op jit(solution)/shard_map/ppermute | solution.py:497
  10.2 12.6 %collective-permute-start.4 = (f32[20,4,256]{2,1,0:T(4,128)S(1)}, f32[20,4,256]{2,1,0:T(4,128)S(1)}, u32[]{:S(2)}, u32[]{:S(2)}) collective-permute-start(f32[20,4,256]{2,1,0:T(4,128)S(1)} %collective-permute-done.3.refs_4_), channel_id=1, source_target_pairs={{0,4},{4,0},{8,12},{12,8},{16,20},{20,16},{24,28},{28,24},{1,5},{5... | collective-permute-start | bytes 245768 | tf_op jit(solution)/shard_map/ppermute | solution.py:497
  11.7 11.1 %collective-permute-start.2 = (f32[20,4,256]{2,1,0:T(4,128)S(1)}, f32[20,4,256]{2,1,0:T(4,128)S(1)}, u32[]{:S(2)}, u32[]{:S(2)}) collective-permute-start(f32[20,4,256]{2,1,0:T(4,128)S(1)} %collective-permute-done.1.refs_2_), channel_id=1, source_target_pairs={{0,4},{4,0},{8,12},{12,8},{16,20},{20,16},{24,28},{28,24},{1,5},{5... | collective-permute-start | bytes 245768 | tf_op jit(solution)/shard_map/ppermute | solution.py:497
  14.2 8.6 %collective-permute-start.6 = (f32[20,4,256]{2,1,0:T(4,128)S(1)}, f32[20,4,256]{2,1,0:T(4,128)S(1)}, u32[]{:S(2)}, u32[]{:S(2)}) collective-permute-start(f32[20,4,256]{2,1,0:T(4,128)S(1)} %collective-permute-done.5.refs_6_), channel_id=1, source_target_pairs={{0,4},{4,0},{8,12},{12,8},{16,20},{20,16},{24,28},{28,24},{1,5},{5... | collective-permute-start | bytes 245768 | tf_op jit(solution)/shard_map/ppermute | solution.py:497
  15.7 0.9 %copy-start = (f32[24,4,256]{2,1,0:T(4,128)S(1)}, f32[24,4,256]{2,1,0:T(4,128)}, u32[]{:S(2)}) copy-start(f32[24,4,256]{2,1,0:T(4,128)} %refs_0_.3) | copy-start | bytes 294916
  16.7 6.1 %copy-start.2 = (f32[20,4,256]{2,1,0:T(4,128)S(1)}, f32[20,4,256]{2,1,0:T(4,128)}, u32[]{:S(2)}) copy-start(f32[20,4,256]{2,1,0:T(4,128)} %refs_0_.2) | copy-start | bytes 245764
  16.7 9.8 %collective-permute-start.12 = (f32[2,96,256]{2,1,0:T(8,128)S(1)}, f32[2,96,256]{2,1,0:T(8,128)S(1)}, u32[]{:S(2)}, u32[]{:S(2)}) collective-permute-start(f32[2,96,256]{2,1,0:T(8,128)S(1)} %pair.1.refs_0_), channel_id=1, source_target_pairs={{0,16},{4,20},{8,24},{12,28},{16,0},{20,4},{24,8},{28,12},{1,17},{... | collective-permute-start | bytes 589832 | tf_op jit(solution)/shard_map/ppermute | solution.py:497
  22.2 5.8 %copy-start.1 = (bf16[256,2048]{1,0:T(8,128)(2,1)S(1)}, bf16[256,2048]{1,0:T(8,128)(2,1)}, u32[]{:S(2)}) copy-start(bf16[256,2048]{1,0:T(8,128)(2,1)} %refs_8_.1) | copy-start | bytes 3145732
  22.2 12.1 %collective-permute-start.11 = (f32[2,96,256]{2,1,0:T(8,128)S(1)}, f32[2,96,256]{2,1,0:T(8,128)S(1)}, u32[]{:S(2)}, u32[]{:S(2)}) collective-permute-start(f32[2,96,256]{2,1,0:T(8,128)S(1)} %pair.1.refs_0_), channel_id=1, source_target_pairs={{0,4},{4,0},{8,12},{12,8},{16,20},{20,16},{24,28},{28,24},{1,5},{5... | collective-permute-start | bytes 589832 | tf_op jit(solution)/shard_map/ppermute | solution.py:497
  24.5 7.2 %copy-start.4 = (f32[44]{0:T(128)S(1)}, f32[44]{0:T(128)}, u32[]{:S(2)}) copy-start(f32[44]{0:T(128)} %param.11) | copy-start | bytes 532
  24.5 7.2 %copy-start.5 = (f32[5]{0:T(128)S(1)}, f32[5]{0:T(128)}, u32[]{:S(2)}) copy-start(f32[5]{0:T(128)} %param.12) | copy-start | bytes 64
  24.6 7.2 %collective-permute-start.9 = (f32[24,256]{1,0:T(8,128)S(1)}, f32[24,256]{1,0:T(8,128)S(1)}, u32[]{:S(2)}, u32[]{:S(2)}) collective-permute-start(f32[24,256]{1,0:T(8,128)S(1)} %raw.1.refs_0_), channel_id=1, source_target_pairs={{0,3},{1,2},{2,1},{3,0},{4,7},{5,6},{6,5},{7,4},{8,11},{9,10},{10,... | collective-permute-start | bytes 73736 | tf_op jit(solution)/shard_map/ppermute | solution.py:497
  24.6 7.1 %collective-permute-start.8 = (f32[24,256]{1,0:T(8,128)S(1)}, f32[24,256]{1,0:T(8,128)S(1)}, u32[]{:S(2)}, u32[]{:S(2)}) collective-permute-start(f32[24,256]{1,0:T(8,128)S(1)} %raw.1.refs_0_), channel_id=1, source_target_pairs={{0,2},{1,3},{2,0},{3,1},{4,6},{5,7},{6,4},{7,5},{8,10},{9,11},{10,... | collective-permute-start | bytes 73736 | tf_op jit(solution)/shard_map/ppermute | solution.py:497
  26.2 5.5 %collective-permute-start.7 = (f32[24,256]{1,0:T(8,128)S(1)}, f32[24,256]{1,0:T(8,128)S(1)}, u32[]{:S(2)}, u32[]{:S(2)}) collective-permute-start(f32[24,256]{1,0:T(8,128)S(1)} %raw.1.refs_0_), channel_id=1, source_target_pairs={{0,1},{1,0},{2,3},{3,2},{4,5},{5,4},{6,7},{7,6},{8,9},{9,8},{10,11... | collective-permute-start | bytes 73736 | tf_op jit(solution)/shard_map/ppermute | solution.py:497
  26.5 7.8 %collective-permute-start.13 = (f32[2,96,256]{2,1,0:T(8,128)S(1)}, f32[2,96,256]{2,1,0:T(8,128)S(1)}, u32[]{:S(2)}, u32[]{:S(2)}) collective-permute-start(f32[2,96,256]{2,1,0:T(8,128)S(1)} %collective-permute-done.12.refs_2_), channel_id=1, source_target_pairs={{0,4},{4,0},{8,12},{12,8},{16,20},{20,16},{24,28},{28,24},{1,5},{5... | collective-permute-start | bytes 589832 | tf_op jit(solution)/shard_map/ppermute | solution.py:497
  36.3 5.7 %collective-permute-start.16 = (f32[40,256]{1,0:T(8,128)S(1)}, f32[40,256]{1,0:T(8,128)S(1)}, u32[]{:S(2)}, u32[]{:S(2)}) collective-permute-start(f32[40,256]{1,0:T(8,128)S(1)} %project_next.1.refs_0_), channel_id=1, source_target_pairs={{0,3},{1,2},{2,1},{3,0},{4,7},{5,6},{6,5},{7,4},{8,11},{9,10},{10,... | collective-permute-start | bytes 122888 | tf_op jit(solution)/shard_map/ppermute | solution.py:497
  37.2 4.8 %collective-permute-start.15 = (f32[40,256]{1,0:T(8,128)S(1)}, f32[40,256]{1,0:T(8,128)S(1)}, u32[]{:S(2)}, u32[]{:S(2)}) collective-permute-start(f32[40,256]{1,0:T(8,128)S(1)} %project_next.1.refs_0_), channel_id=1, source_target_pairs={{0,2},{1,3},{2,0},{3,1},{4,6},{5,7},{6,4},{7,5},{8,10},{9,11},{10,... | collective-permute-start | bytes 122888 | tf_op jit(solution)/shard_map/ppermute | solution.py:497
  37.9 4.0 %collective-permute-start.14 = (f32[40,256]{1,0:T(8,128)S(1)}, f32[40,256]{1,0:T(8,128)S(1)}, u32[]{:S(2)}, u32[]{:S(2)}) collective-permute-start(f32[40,256]{1,0:T(8,128)S(1)} %project_next.1.refs_0_), channel_id=1, source_target_pairs={{0,1},{1,0},{2,3},{3,2},{4,5},{5,4},{6,7},{7,6},{8,9},{9,8},{10,11... | collective-permute-start | bytes 122888 | tf_op jit(solution)/shard_map/ppermute | solution.py:497
  38.2 3.8 %copy-start.3 = (f32[2048]{0:T(1024)S(1)}, f32[2048]{0:T(1024)}, u32[]{:S(2)}) copy-start(f32[2048]{0:T(1024)} %param.13) | copy-start | bytes 24580

commit v4 on v3

--- a/solution.py
+++ b/solution.py
@@ -20,6 +20,7 @@
 VMEM = pl.BlockSpec(memory_space=pltpu.VMEM)
 HBM = pl.BlockSpec(memory_space=pltpu.HBM)
 
+RAW_EARLY, RAW_LATE = (0, 1, 2, 3, 4, 6), (5, 7)
 PAIRS = [(i, j) for i in range(4) for j in range(i, 4)]
 
 
@@ -103,11 +104,11 @@
     )(pltpu.with_memory_space_constraint(streams, pltpu.HBM))
 
 
-def grams_kernel(sde_ref, b_ref, g_ref, column_ref):
-    blocks, _, tokens, _ = sde_ref.shape
+def grams_kernel(start, sde_ref, b_ref, g_ref, column_ref):
+    blocks, tokens = sde_ref.shape[0], g_ref.shape[1]
 
     def chunk(c, _):
-        at = pl.ds(pl.multiple_of(c * 16, 16), 16)
+        at = pl.ds(pl.multiple_of(start + c * 16, 16), 16)
         sums = [None] * 15
         for k in range(blocks):
             for h in range(FB // 128):
@@ -121,17 +122,16 @@
         column = jnp.zeros((16, 128), F32)
         for p in range(15):
             column = jnp.where(lane == p, jnp.sum(sums[p], axis=1, keepdims=True), column)
-        column_ref[at, :] = column
+        column_ref[pl.ds(pl.multiple_of(c * 16, 16), 16), :] = column
         return 0
 
     lax.fori_loop(0, tokens // 16, chunk, 0)
     g_ref[...] = column_ref[...].T[0:16]
 
 
-def grams_of(sde, branch):
-    tokens = sde.shape[2]
-    return pl.pallas_call(
-        grams_kernel,
+def grams_of(sde, branch, start, tokens):
+    return pl.pallas_call(
+        functools.partial(grams_kernel, start),
         out_shape=jax.ShapeDtypeStruct((16, tokens), F32),
         in_specs=[VMEM, VMEM],
         out_specs=VMEM,
@@ -140,7 +140,6 @@
         cost_estimate=pl.CostEstimate(
             flops=3_000_000_000, bytes_accessed=5 * MIB, transcendentals=0
         ),
-        name="grams",
     )(sde, branch)
 
 
@@ -148,46 +147,47 @@
     return jnp.bitwise_xor(lax.axis_index("dp"), s) if permuted else s
 
 
-def raw_kernel(permuted, *refs):
-    w_refs, (sde_ref, q_ref, out_ref, wide_ref, lhs_ref) = refs[:-5], refs[-5:]
-    count = w_refs[0].shape[0]
-    pad = wide_ref.shape[1]
-    blocks = sde_ref.shape[0]
+def raw_kernel(order, permuted, last, *refs):
+    count = len(order)
+    w_refs, (sde_ref, extra_ref, out_ref, wide_ref, lhs_ref) = refs[:count], refs[count:]
+    rows, pad = w_refs[0].shape[0], wide_ref.shape[1]
     wide_ref[...] = jnp.zeros_like(wide_ref)
-    for s in range(blocks):
+    total = None
+    for n, (s, w_ref) in enumerate(zip(order, w_refs)):
         owner = _owner(s, permuted)
         for i in range(4):
-            wide_ref[i, 0:count, :] = w_refs[s][:, i, :]
+            wide_ref[i, 0:rows, :] = w_ref[:, i, :]
             hi, lo = _split(wide_ref[i])
-            lhs_ref[owner, i, 0:pad, :] = hi
-            lhs_ref[owner, i, pad : 2 * pad, :] = lo
-    total = None
-    for s in range(blocks):
-        for i in range(4):
-            part = _nt(lhs_ref[s, i], sde_ref[s, i])
+            lhs_ref[n, i, 0:pad, :] = hi
+            lhs_ref[n, i, pad : 2 * pad, :] = lo
+            part = _nt(lhs_ref[n, i], sde_ref[owner, i])
             total = part if total is None else total + part
-    _store_by_column(out_ref, total[0:20] + total[pad : pad + 20], 4)
-    out_ref[20:21, :] = jnp.sum(q_ref[...], axis=0, keepdims=True)
-    out_ref[21:24, :] = jnp.zeros((3, out_ref.shape[1]), F32)
-
-
-def raw(weights, sde, squares, permuted):
-    blocks, _, tokens, _ = sde.shape
-    return pl.pallas_call(
-        functools.partial(raw_kernel, permuted),
+    total = total[0:20] + total[pad : pad + 20]
+    if last:
+        _store_by_column(out_ref, total + extra_ref[0:20, :], 4)
+        out_ref[20:24, :] = extra_ref[20:24, :]
+    else:
+        out_ref[0:20, :] = total
+        out_ref[20:21, :] = jnp.sum(extra_ref[...], axis=0, keepdims=True)
+        out_ref[21:24, :] = jnp.zeros((3, total.shape[1]), F32)
+
+
+def raw(weights, order, sde, extra, permuted, last):
+    tokens = sde.shape[2]
+    return pl.pallas_call(
+        functools.partial(raw_kernel, order, permuted, last),
         out_shape=jax.ShapeDtypeStruct((24, tokens), F32),
-        in_specs=[VMEM] * (len(weights) + 2),
+        in_specs=[VMEM] * (len(order) + 2),
         out_specs=VMEM,
         scratch_shapes=[
             pltpu.VMEM((4, 32, FB), F32),
-            pltpu.VMEM((blocks, 4, 64, FB), BF16),
+            pltpu.VMEM((len(order), 4, 64, FB), BF16),
         ],
         compiler_params=pltpu.CompilerParams(vmem_limit_bytes=12 * MIB),
         cost_estimate=pl.CostEstimate(
             flops=2_000_000_000, bytes_accessed=5 * MIB, transcendentals=0
         ),
-        name="raw",
-    )(*weights, sde, squares)
+    )(*[weights[s] for s in order], sde, extra)
 
 
 def pair_kernel(*refs):
@@ -211,47 +211,76 @@
     )(*weights)
 
 
-def next_kernel(order, permuted, *refs):
-    w_refs, (sde_ref, b_ref, coef_ref, g_ref, out_ref, lhs_ref) = refs[:-6], refs[-6:]
+def _projected(order, permuted, w_refs, sde_ref, b_ref, lhs_ref):
     rows = w_refs[0].shape[1]
-    count = rows // 4
-    blocks = sde_ref.shape[0]
     places = [(w_ref, n) for w_ref in w_refs for n in range(w_ref.shape[0])]
-    for s, (w_ref, n) in zip(order, places):
-        owner = _owner(s, permuted)
+    owners = [_owner(s, permuted) for s in order]
+    for s, (w_ref, n) in enumerate(places):
         hi, lo = _split(w_ref[n])
-        lhs_ref[owner, 0:rows, :] = hi
-        lhs_ref[owner, rows : 2 * rows, :] = lo
-    mixed = None
+        lhs_ref[s, 0:rows, :] = hi
+        lhs_ref[s, rows : 2 * rows, :] = lo
     for i in range(5):
         total = None
-        for s in range(blocks):
-            right = sde_ref[s, i] if i < 4 else b_ref[:, s * FB : (s + 1) * FB]
+        for s, owner in enumerate(owners):
+            if i < 4:
+                right = sde_ref[owner, i]
+            else:
+                right = b_ref[:, pl.ds(pl.multiple_of(owner * FB, FB), FB)]
             part = _nt(lhs_ref[s], right)
             total = part if total is None else total + part
-        total = total[0:rows] + total[rows : 2 * rows]
+        yield total[0:rows] + total[rows : 2 * rows]
+
+
+def early_kernel(order, permuted, *refs):
+    w_refs, (sde_ref, b_ref, out_ref, lhs_ref) = refs[:-4], refs[-4:]
+    for i, total in enumerate(_projected(order, permuted, w_refs, sde_ref, b_ref, lhs_ref)):
+        out_ref[i] = total
+
+
+def late_kernel(order, permuted, *refs):
+    w_refs, refs = refs[:-8], refs[-8:]
+    sde_ref, b_ref, early_ref, coef_ref, left_ref, right_ref, out_ref, lhs_ref = refs
+    count = w_refs[0].shape[1] // 4
+    mixed = None
+    for i, total in enumerate(_projected(order, permuted, w_refs, sde_ref, b_ref, lhs_ref)):
+        total = total + early_ref[i]
         for j in range(4):
             part = coef_ref[4 * i + j : 4 * i + j + 1, :] * total[j * count : (j + 1) * count]
             mixed = part if mixed is None else mixed + part
     _store_by_column(out_ref, mixed, 8)
-    out_ref[count:, :] = g_ref[...]
-
-
-def project_next(weights, order, sde, branch, coef, gram, permuted):
-    blocks, _, tokens, _ = sde.shape
-    rows = weights[0].shape[1]
-    return pl.pallas_call(
-        functools.partial(next_kernel, order, permuted),
-        out_shape=jax.ShapeDtypeStruct((rows // 4 + gram.shape[0], tokens), F32),
-        in_specs=[VMEM] * (len(weights) + 4),
+    out_ref[count:, :] = jnp.concatenate([left_ref[...], right_ref[...]], axis=1)
+
+
+def project_early(weights, order, sde, branch, permuted):
+    rows, tokens = weights[0].shape[1], sde.shape[2]
+    return pl.pallas_call(
+        functools.partial(early_kernel, order, permuted),
+        out_shape=jax.ShapeDtypeStruct((5, rows, tokens), F32),
+        in_specs=[VMEM] * (len(weights) + 2),
         out_specs=VMEM,
-        scratch_shapes=[pltpu.VMEM((blocks, 2 * rows, FB), BF16)],
+        scratch_shapes=[pltpu.VMEM((len(order), 2 * rows, FB), BF16)],
         compiler_params=pltpu.CompilerParams(vmem_limit_bytes=14 * MIB),
         cost_estimate=pl.CostEstimate(
             flops=3_000_000_000, bytes_accessed=6 * MIB, transcendentals=0
         ),
-        name="project_next",
-    )(*weights, sde, branch, coef, gram)
+        name="project_early",
+    )(*weights, sde, branch)
+
+
+def project_late(weights, order, sde, branch, early, coef, grams, permuted):
+    rows, tokens = weights[0].shape[1], sde.shape[2]
+    return pl.pallas_call(
+        functools.partial(late_kernel, order, permuted),
+        out_shape=jax.ShapeDtypeStruct((rows // 4 + grams[0].shape[0], tokens), F32),
+        in_specs=[VMEM] * (len(weights) + 6),
+        out_specs=VMEM,
+        scratch_shapes=[pltpu.VMEM((len(order), 2 * rows, FB), BF16)],
+        compiler_params=pltpu.CompilerParams(vmem_limit_bytes=14 * MIB),
+        cost_estimate=pl.CostEstimate(
+            flops=3_000_000_000, bytes_accessed=6 * MIB, transcendentals=0
+        ),
+        name="project_late",
+    )(*weights, sde, branch, early, coef, *grams)
 
 
 def _balance(columns):
@@ -403,7 +432,7 @@
 def second_kernel(features, *refs):
     r_refs = refs[0:4]
     coef_ref, bias_ref, scale_ref, sde_ref, b_ref, gain_ref = refs[4:10]
-    out_hbm, mix_hbm, mix_ref, column_ref, out_ref, sems, mix_sem = refs[10:]
+    out_hbm, mix_hbm, mix_ref, column_ref, w5_ref, out_ref, sems, mix_sem = refs[10:]
     tokens, _ = b_ref.shape
     gram = _sum4(r_refs, (slice(24, 40), slice(None)))
     columns = [coef_ref[4 * i : 4 * i + 4, :] for i in range(5)]
@@ -445,25 +474,30 @@
     stacked = jnp.concatenate([j * root for j in joint] + [jnp.zeros((3, tokens), F32)], axis=0)
     column_ref[:, 0:8] = stacked.T
     blocks = sde_ref.shape[0]
+    for i in range(5):
+        w5_ref[i] = jnp.broadcast_to(column_ref[:, i : i + 1], (tokens, 128))
 
     def copy(c):
-        at = pl.ds(pl.multiple_of(c * 16, 16), 16)
+        at = pl.ds(pl.multiple_of(c * 32, 32), 32)
         return pltpu.make_async_copy(out_ref.at[at], out_hbm.at[at], sems.at[c])
 
     def body(c, _):
-        at = pl.ds(pl.multiple_of(c * 16, 16), 16)
-        weights = [column_ref[at, i : i + 1] for i in range(5)]
-        for k in range(blocks):
-            lanes = pl.ds(k * FB, FB)
-            total = weights[4] * b_ref[at, lanes].astype(F32)
-            for i in range(4):
-                total = total + weights[i] * sde_ref[k, i, at, :].astype(F32)
-            out_ref[at, lanes] = (total * gain_ref[:, lanes]).astype(BF16)
+        for u in range(2):
+            at = pl.ds(pl.multiple_of(c * 32 + u * 16, 16), 16)
+            weights = [w5_ref[i, at, :] for i in range(5)]
+            for k in range(blocks):
+                for h in range(FB // 128):
+                    part = slice(h * 128, (h + 1) * 128)
+                    lanes = slice(k * FB + h * 128, k * FB + (h + 1) * 128)
+                    total = weights[4] * b_ref[at, lanes].astype(F32)
+                    for i in range(4):
+                        total = total + weights[i] * sde_ref[k, i, at, part].astype(F32)
+                    out_ref[at, lanes] = (total * gain_ref[:, lanes]).astype(BF16)
         copy(c).start()
         return 0
 
-    lax.fori_loop(0, tokens // 16, body, 0)
-    for c in range(tokens // 16):
+    lax.fori_loop(0, tokens // 32, body, 0)
+    for c in range(tokens // 32):
         copy(c).wait()
     mix_copy.wait()
 
@@ -481,6 +515,7 @@
         scratch_shapes=[
             pltpu.VMEM((20, tokens), F32),
             pltpu.VMEM((tokens, 128), F32),
+            pltpu.VMEM((5, tokens, 128), F32),
             pltpu.VMEM((tokens, width), BF16),
             pltpu.SemaphoreType.DMA((tokens // 16,)),
             pltpu.SemaphoreType.DMA,
@@ -515,7 +550,8 @@
 
 def gather_next(weight, count, width):
     if count != 8 or count * weight.shape[2] != width or weight.shape[2] != FB:
-        return [pair(*by_block(weight, width))], tuple(range(width // FB))
+        blocks = by_block(weight, width)
+        return [pair(*blocks[:-2]), pair(*blocks[-2:])], tuple(range(width // FB))
     far = _swap(weight, "dp", count, 2)
     here = pair(weight, far)
     there = _swap(here, "dp", count, 4)
@@ -534,15 +570,22 @@
     def local(streams, branch, merge_weight, next_weight, blend_bias, blend_scale, norm_gain):
         count, width = streams.shape[1:]
         features = count * width * n_mp
+        tokens = streams.shape[0]
         merge_blocks, permuted = gather_merge(merge_weight, n_dp, width)
         next_blocks, order = gather_next(next_weight, n_dp, width)
         gain, bias, scale = norm_gain[None, :], blend_bias[None, :], blend_scale[None, :]
         sil, sde, squares = deal(streams)
-        gram = grams_of(sde, branch)
-        raws = everyone(raw(merge_blocks, sde, squares, permuted), n_mp)
+        part = raw(merge_blocks, RAW_EARLY, sde, squares, permuted, False)
+        part = raw(merge_blocks, RAW_LATE, sde, part, permuted, True)
+        raws = everyone(part, n_mp)
+        half = tokens // 2
+        grams = [grams_of(sde, branch, 0, half), grams_of(sde, branch, half, tokens - half)]
         coef = first(raws, bias, scale, features)
         streams_out = mix(weave(coef), sil, branch)
-        next_raw = project_next(next_blocks, order, sde, branch, coef, gram, permuted)
+        early = project_early(next_blocks[:-1], order[:-2], sde, branch, permuted)
+        next_raw = project_late(
+            next_blocks[-1:], order[-2:], sde, branch, early, coef, grams, permuted
+        )
         next_raws = everyone(next_raw, n_mp)
         branch_in, next_mix = second(
             next_raws, coef, bias, scale, sde, branch, gain, features

time: 45.4 us -> 47.6 us (1.048)
  waiting for transfers between devices: 2.22 us -> 6.14 us
  local copies, waits for them, and re-layouts: 0.92 us -> 0.03 us
  Pallas kernels: 20.8 us -> 20.2 us
    ppermute x17, waiting for transfers between devices: 2.22 us -> 6.14 us  [_swap(): return lax.ppermute(x, axis, [(i, i ^ s) for i in range(count)])]
    unnamed x12, local copies, waits for them, and re-layouts: 0.92 us -> 0.03 us
    pallas_call x1, Pallas kernels: 3.3 us -> 2.53 us  [second(): pl.pallas_call(functools.partial(second_kernel, features), out_shape=(jax...]
    pallas_call x3 -> x6, Pallas kernels: 7.33 us -> 7.37 us  [the longest x2 3.77 us: grams_of(): pl.pallas_call(functools.partial(grams_kernel, start), out_shape=jax.Shap...]
  transfers between devices with their start and end apart: 17 -> 17, of which waited for: 2 -> 3; matrix products, arithmetic and copies ran while one was open for 0% -> 0% of each run, Pallas kernels for 34% -> 36%
where the time goes in v4:
time: 47.6 us; the launch traced here: 47.5 us
  starting transfers between devices  20.3 us (43%)
  Pallas kernels  20.2 us (42%)
  waiting for transfers between devices  6.14 us (13%)
  between operations  0.81 us (2%)
    ppermute x17, starting transfers between devices, _swap(): return lax.ppermute(x, axis, [(i, i ^ s) for i in range(count)])  20.3 us
    ppermute x17, waiting for transfers between devices, _swap(): return lax.ppermute(x, axis, [(i, i ^ s) for i in range(count)])  6.14 us
    pallas_call x1, Pallas kernels, deal(): pl.pallas_call(deal_kernel, out_shape=(jax.ShapeDtypeStruct((tiles, 4 * t...  3.9 us
    pallas_call x1, Pallas kernels, mix(): pl.pallas_call(mix_kernel, out_shape=jax.ShapeDtypeStruct((tokens, 4, til...  3.84 us
    pallas_call x2, Pallas kernels, grams_of(): pl.pallas_call(functools.partial(grams_kernel, start), out_shape=jax.Shap...  3.77 us
    pallas_call x1, Pallas kernels, second(): pl.pallas_call(functools.partial(second_kernel, features), out_shape=(jax...  2.53 us
    pallas_call x1, Pallas kernels, weave(): pl.pallas_call(weave_kernel, out_shape=jax.ShapeDtypeStruct((tokens // MT...  2.28 us
    pallas_call x2, Pallas kernels, raw(): pl.pallas_call(functools.partial(raw_kernel, order, permuted, last), out_...  1.57 us
  transfers between devices with their start and end apart: 17, of which 3 were waited for; matrix products, arithmetic and copies ran while one was open for 0% of the time, Pallas kernels for 36%

profile of v4, /device:TPU:0, one launch (start us, length us, event | category | flops | bytes accessed | tf_op | source)
XLA Modules:
  0.0 47.5 jit_solution(5666296185272943888)
XLA Ops:
  0.6 0.0 copy-start.1
  0.6 3.1 %collective-permute-start.5 = (f32[20,4,256]{2,1,0:T(4,128)}, f32[20,4,256]{2,1,0:T(4,128)S(1)}, u32[]{:S(2)}, u32[]{:S(2)}) collective-permute-start(f32[20,4,256]{2,1,0:T(4,128)} %refs_0_.2), channel_id=1, source_target_pairs={{0,8},{4,12},{8,0},{12,4},{16,24},{20,28},{24,16},{28,20},{1,9},{5... | collective-permute-start | bytes 245768 | tf_op jit(solution)/shard_map/ppermute | solution.py:532
  3.8 2.6 %collective-permute-start = (f32[20,4,256]{2,1,0:T(4,128)}, f32[20,4,256]{2,1,0:T(4,128)S(1)}, u32[]{:S(2)}, u32[]{:S(2)}) collective-permute-start(f32[20,4,256]{2,1,0:T(4,128)} %refs_0_.2), channel_id=1, source_target_pairs={{0,16},{4,20},{8,24},{12,28},{16,0},{20,4},{24,8},{28,12},{1,17},{... | collective-permute-start | bytes 245768 | tf_op jit(solution)/shard_map/ppermute | solution.py:532
  6.3 0.0 collective-permute-start.2
  6.3 1.7 %collective-permute-start.4 = (f32[20,4,256]{2,1,0:T(4,128)}, f32[20,4,256]{2,1,0:T(4,128)S(1)}, u32[]{:S(2)}, u32[]{:S(2)}) collective-permute-start(f32[20,4,256]{2,1,0:T(4,128)} %refs_0_.2), channel_id=1, source_target_pairs={{0,4},{4,0},{8,12},{12,8},{16,20},{20,16},{24,28},{28,24},{1,5},{5... | collective-permute-start | bytes 245768 | tf_op jit(solution)/shard_map/ppermute | solution.py:532
  8.1 0.7 %collective-permute-start.10 = (f32[24,4,256]{2,1,0:T(4,128)}, f32[24,4,256]{2,1,0:T(4,128)S(1)}, u32[]{:S(2)}, u32[]{:S(2)}) collective-permute-start(f32[24,4,256]{2,1,0:T(4,128)} %refs_0_.3), channel_id=1, source_target_pairs={{0,8},{4,12},{8,0},{12,4},{16,24},{20,28},{24,16},{28,20},{1,9},{5... | collective-permute-start | bytes 294920 | tf_op jit(solution)/shard_map/ppermute | solution.py:532
  8.8 3.9 %deal.1 = (bf16[16,1024,128]{2,1,0:T(8,128)(2,1)S(1)}, bf16[8,4,256,256]{3,2,1,0:T(8,128)(2,1)S(1)}, f32[8,256]{1,0:T(8,128)S(1)}) custom-call(bf16[256,4,2048]{2,1,0:T(4,128)(2,1)} %s_hbm.1), custom_call_target="tpu_custom_call" | custom-call | flops 6000000000 | bytes 10485760 | tf_op jit(solution)/shard_map/deal/pallas_call | solution.py:89
  12.7 0.0 collective-permute-done.5.refs_2_
  12.7 0.6 %collective-permute-start.6 = (f32[20,4,256]{2,1,0:T(4,128)S(1)}, f32[20,4,256]{2,1,0:T(4,128)S(1)}, u32[]{:S(2)}, u32[]{:S(2)}) collective-permute-start(f32[20,4,256]{2,1,0:T(4,128)S(1)} %collective-permute-done.5.refs_2_), channel_id=1, source_target_pairs={{0,4},{4,0},{8,12},{12,8},{16,20},{20,16},{24,28},{28,24},{1,5},{5... | collective-permute-start | bytes 245768 | tf_op jit(solution)/shard_map/ppermute | solution.py:532
  13.2 0.0 copy-done.1
  13.3 0.0 copy-start
  13.3 0.0 copy-start.2
  13.3 1.9 %shard_map.96.refs_5_ = f32[16,128]{1,0:T(8,128)S(1)} custom-call(bf16[8,4,256,256]{3,2,1,0:T(8,128)(2,1)S(1)} %get-tuple-element.8.refs_6_.refs_2_.refs_3_.sde_ref.refs_1_.refs_7_, bf16[256,2048]{1,0:T(8,128)(2,1)S(1)} %copy-done.1), custom_call_target="tpu_custom_call" | custom-call | flops 3000000000 | bytes 5242880 | tf_op jit(solution)/shard_map/pallas_call | solution.py:133
  15.1 0.0 collective-permute-done.refs_4_
  15.1 1.6 %collective-permute-start.1 = (f32[20,4,256]{2,1,0:T(4,128)S(1)}, f32[20,4,256]{2,1,0:T(4,128)S(1)}, u32[]{:S(2)}, u32[]{:S(2)}) collective-permute-start(f32[20,4,256]{2,1,0:T(4,128)S(1)} %collective-permute-done.refs_4_), channel_id=1, source_target_pairs={{0,4},{4,0},{8,12},{12,8},{16,20},{20,16},{24,28},{28,24},{1,5},{5... | collective-permute-start | bytes 245768 | tf_op jit(solution)/shard_map/ppermute | solution.py:532
  16.7 0.0 collective-permute-done.2.refs_5_
  16.7 0.5 %collective-permute-start.3 = (f32[20,4,256]{2,1,0:T(4,128)S(1)}, f32[20,4,256]{2,1,0:T(4,128)S(1)}, u32[]{:S(2)}, u32[]{:S(2)}) collective-permute-start(f32[20,4,256]{2,1,0:T(4,128)S(1)} %collective-permute-done.2.refs_5_), channel_id=1, source_target_pairs={{0,4},{4,0},{8,12},{12,8},{16,20},{20,16},{24,28},{28,24},{1,5},{5... | collective-permute-start | bytes 245768 | tf_op jit(solution)/shard_map/ppermute | solution.py:532
  17.2 0.0 collective-permute-done.10.refs_1_
  17.2 0.0 copy-done
  17.2 0.1 pair.1.refs_0_
  17.3 3.6 %collective-permute-start.11 = (f32[2,96,256]{2,1,0:T(8,128)S(1)}, f32[2,96,256]{2,1,0:T(8,128)S(1)}, u32[]{:S(2)}, u32[]{:S(2)}) collective-permute-start(f32[2,96,256]{2,1,0:T(8,128)S(1)} %pair.1.refs_0_), channel_id=1, source_target_pairs={{0,16},{4,20},{8,24},{12,28},{16,0},{20,4},{24,8},{28,12},{1,17},{... | collective-permute-start | bytes 589832 | tf_op jit(solution)/shard_map/ppermute | solution.py:532
  20.9 0.0 collective-permute-done.4.refs_1_
  20.9 1.5 %collective-permute-start.13 = (f32[2,96,256]{2,1,0:T(8,128)S(1)}, f32[2,96,256]{2,1,0:T(8,128)S(1)}, u32[]{:S(2)}, u32[]{:S(2)}) collective-permute-start(f32[2,96,256]{2,1,0:T(8,128)S(1)} %pair.1.refs_0_), channel_id=1, source_target_pairs={{0,4},{4,0},{8,12},{12,8},{16,20},{20,16},{24,28},{28,24},{1,5},{5... | collective-permute-start | bytes 589832 | tf_op jit(solution)/shard_map/ppermute | solution.py:532
  22.4 0.0 collective-permute-done.6.refs_3_
  22.4 0.0 copy-done.2
  22.4 1.1 %shard_map.94.refs_3_ = f32[24,256]{1,0:T(8,128)S(1)} custom-call(f32[20,4,256]{2,1,0:T(4,128)S(1)} %copy-done.2, f32[20,4,256]{2,1,0:T(4,128)S(1)} %collective-permute-done.4.refs_1_, f32[20,4,256]{2,1,0:T(4,128)S(1)} %collective-permute-done.5.refs_2_, f32[20,4,256]{2,1,0:T(4,128)S(1)} %collective-permute-done.6.refs_3_, ...), custom_call_target="tpu_custom_call" | custom-call | flops 2000000000 | bytes 5242880 | tf_op jit(solution)/shard_map/pallas_call | solution.py:177
  23.5 0.0 collective-permute-done.1.refs_0_
  23.5 0.0 collective-permute-done.3.refs_1_
  23.5 0.5 shard_map.95.refs_0_
  24.0 0.0 copy-start.4
  24.0 0.0 copy-start.5
  24.0 0.1 collective-permute-start.7
  24.1 1.6 %collective-permute-start.8 = (f32[24,256]{1,0:T(8,128)S(1)}, f32[24,256]{1,0:T(8,128)S(1)}, u32[]{:S(2)}, u32[]{:S(2)}) collective-permute-start(f32[24,256]{1,0:T(8,128)S(1)} %shard_map.95.refs_0_), channel_id=1, source_target_pairs={{0,2},{1,3},{2,0},{3,1},{4,6},{5,7},{6,4},{7,5},{8,10},{9,11},{10,... | collective-permute-start | bytes 73736 | tf_op jit(solution)/shard_map/ppermute | solution.py:532
  25.7 0.3 collective-permute-start.9
  25.9 1.9 %shard_map.97.refs_6_ = f32[16,128]{1,0:T(8,128)S(1)} custom-call(bf16[8,4,256,256]{3,2,1,0:T(8,128)(2,1)S(1)} %get-tuple-element.8.refs_6_.refs_2_.refs_3_.sde_ref.refs_1_.refs_7_, bf16[256,2048]{1,0:T(8,128)(2,1)S(1)} %copy-done.1), custom_call_target="tpu_custom_call" | custom-call | flops 3000000000 | bytes 5242880 | tf_op jit(solution)/shard_map/pallas_call | solution.py:133
  27.8 0.0 collective-permute-done.7.refs_1_
  27.8 0.2 collective-permute-done.8.refs_2_
  28.0 0.9 %collective-permute-done.9.refs_3_ = f32[24,256]{1,0:T(8,128)S(1)} collective-permute-done((f32[24,256]{1,0:T(8,128)S(1)}, f32[24,256]{1,0:T(8,128)S(1)}, u32[]{:S(2)}, u32[]{:S(2)}) %collective-permute-start.9) | collective-permute-done | bytes 24608 | tf_op jit(solution)/shard_map/ppermute | solution.py:532
  28.9 0.0 copy-done.4
  28.9 0.0 copy-done.5
  28.9 0.3 first.1.coef_ref.refs_4_
  29.2 2.3 %weave.1.left_ref = bf16[16,64,160]{2,1,0:T(8,128)(2,1)S(1)} custom-call(f32[24,256]{1,0:T(8,128)S(1)} %first.1.coef_ref.refs_4_), custom_call_target="tpu_custom_call" | custom-call | flops 1000000000 | bytes 1048576 | tf_op jit(solution)/shard_map/weave/pallas_call | solution.py:370
  31.5 0.0 collective-permute-done.11.refs_2_
  31.5 0.6 %collective-permute-start.12 = (f32[2,96,256]{2,1,0:T(8,128)S(1)}, f32[2,96,256]{2,1,0:T(8,128)S(1)}, u32[]{:S(2)}, u32[]{:S(2)}) collective-permute-start(f32[2,96,256]{2,1,0:T(8,128)S(1)} %collective-permute-done.11.refs_2_), channel_id=1, source_target_pairs={{0,4},{4,0},{8,12},{12,8},{16,20},{20,16},{24,28},{28,24},{1,5},{5... | collective-permute-start | bytes 589832 | tf_op jit(solution)/shard_map/ppermute | solution.py:532
  32.0 0.0 collective-permute-done.13.refs_1_
  32.0 1.4 %project_early.1.refs_3_ = f32[5,96,256]{2,1,0:T(8,128)S(1)} custom-call(f32[2,96,256]{2,1,0:T(8,128)S(1)} %pair.1.refs_0_, f32[2,96,256]{2,1,0:T(8,128)S(1)} %collective-permute-done.13.refs_1_, f32[2,96,256]{2,1,0:T(8,128)S(1)} %collective-permute-done.11.refs_2_, ...), custom_call_target="tpu_custom_call" | custom-call | flops 3000000000 | bytes 6291456 | tf_op jit(solution)/shard_map/project_early/pallas_call | solution.py:256
  33.5 5.0 %collective-permute-done.12.refs_0_ = f32[2,96,256]{2,1,0:T(8,128)S(1)} collective-permute-done((f32[2,96,256]{2,1,0:T(8,128)S(1)}, f32[2,96,256]{2,1,0:T(8,128)S(1)}, u32[]{:S(2)}, u32[]{:S(2)}) %collective-permute-start.12) | collective-permute-done | bytes 196640 | tf_op jit(solution)/shard_map/ppermute | solution.py:532
  38.5 0.6 %project_late.1.refs_0_ = f32[40,256]{1,0:T(8,128)S(1)} custom-call(f32[2,96,256]{2,1,0:T(8,128)S(1)} %collective-permute-done.12.refs_0_, bf16[8,4,256,256]{3,2,1,0:T(8,128)(2,1)S(1)} %get-tuple-element.8.refs_6_.refs_2_.refs_3_.sde_ref.refs_1_.refs_7_, bf16[256,2048]{1,0:T(8,128)(2,1)S(1)} %copy-done.1, f32[5,96,256]{2,1,0:T(8,128)S(1)} %project_early.1.refs_3_, ...), custom_call_target="tpu_custom_call" | custom-call | flops 3000000000 | bytes 6291456 | tf_op jit(solution)/shard_map/project_late/pallas_call | solution.py:272
  39.1 0.1 collective-permute-start.14
  39.2 0.8 %collective-permute-start.15 = (f32[40,256]{1,0:T(8,128)S(1)}, f32[40,256]{1,0:T(8,128)S(1)}, u32[]{:S(2)}, u32[]{:S(2)}) collective-permute-start(f32[40,256]{1,0:T(8,128)S(1)} %project_late.1.refs_0_), channel_id=1, source_target_pairs={{0,2},{1,3},{2,0},{3,1},{4,6},{5,7},{6,4},{7,5},{8,10},{9,11},{10,... | collective-permute-start | bytes 122888 | tf_op jit(solution)/shard_map/ppermute | solution.py:532
  40.0 1.0 %collective-permute-start.16 = (f32[40,256]{1,0:T(8,128)S(1)}, f32[40,256]{1,0:T(8,128)S(1)}, u32[]{:S(2)}, u32[]{:S(2)}) collective-permute-start(f32[40,256]{1,0:T(8,128)S(1)} %project_late.1.refs_0_), channel_id=1, source_target_pairs={{0,3},{1,2},{2,1},{3,0},{4,7},{5,6},{6,5},{7,4},{8,11},{9,10},{10,... | collective-permute-start | bytes 122888 | tf_op jit(solution)/shard_map/ppermute | solution.py:532
  41.0 0.0 copy-start.3
  41.0 3.8 %mix.1 = bf16[256,4,2048]{2,1,0:T(4,128)(2,1)} custom-call(bf16[16,64,160]{2,1,0:T(8,128)(2,1)S(1)} %weave.1.left_ref, bf16[16,1024,128]{2,1,0:T(8,128)(2,1)S(1)} %get-tuple-element.10.sil_ref, bf16[256,2048]{1,0:T(8,128)(2,1)S(1)} %copy-done.1), custom_call_target="tpu_custom_call" | custom-call | flops 5000000000 | bytes 8388608 | tf_op jit(solution)/shard_map/mix/pallas_call | solution.py:415
  44.9 0.0 collective-permute-done.14.refs_1_
  44.9 0.0 collective-permute-done.15.refs_2_
  44.9 0.0 collective-permute-done.16.refs_3_
  44.9 0.0 copy-done.3
  44.9 2.5 %second.1 = (bf16[256,2048]{1,0:T(8,128)(2,1)}, f32[20,256]{1,0:T(8,128)}) custom-call(f32[40,256]{1,0:T(8,128)S(1)} %project_late.1.refs_0_, f32[40,256]{1,0:T(8,128)S(1)} %collective-permute-done.14.refs_1_, f32[40,256]{1,0:T(8,128)S(1)} %collective-permute-done.15.refs_2_, f32[40,256]{1,0:T(8,128)S(1)} %collective-permute-done.16.refs_3_, ...), custom_call_target="tpu_custom_call" | custom-call | flops 3000000000 | bytes 6291456 | tf_op jit(solution)/shard_map/second/pallas_call | solution.py:507
Async XLA Ops:
  0.6 12.6 %copy-start.1 = (bf16[256,2048]{1,0:T(8,128)(2,1)S(1)}, bf16[256,2048]{1,0:T(8,128)(2,1)}, u32[]{:S(2)}) copy-start(bf16[256,2048]{1,0:T(8,128)(2,1)} %refs_8_.1) | copy-start | bytes 3145732
  0.6 12.0 %collective-permute-start.5 = (f32[20,4,256]{2,1,0:T(4,128)}, f32[20,4,256]{2,1,0:T(4,128)S(1)}, u32[]{:S(2)}, u32[]{:S(2)}) collective-permute-start(f32[20,4,256]{2,1,0:T(4,128)} %refs_0_.2), channel_id=1, source_target_pairs={{0,8},{4,12},{8,0},{12,4},{16,24},{20,28},{24,16},{28,20},{1,9},{5... | collective-permute-start | bytes 245768 | tf_op jit(solution)/shard_map/ppermute | solution.py:532
  3.8 11.4 %collective-permute-start = (f32[20,4,256]{2,1,0:T(4,128)}, f32[20,4,256]{2,1,0:T(4,128)S(1)}, u32[]{:S(2)}, u32[]{:S(2)}) collective-permute-start(f32[20,4,256]{2,1,0:T(4,128)} %refs_0_.2), channel_id=1, source_target_pairs={{0,16},{4,20},{8,24},{12,28},{16,0},{20,4},{24,8},{28,12},{1,17},{... | collective-permute-start | bytes 245768 | tf_op jit(solution)/shard_map/ppermute | solution.py:532
  6.3 10.4 %collective-permute-start.2 = (f32[20,4,256]{2,1,0:T(4,128)}, f32[20,4,256]{2,1,0:T(4,128)S(1)}, u32[]{:S(2)}, u32[]{:S(2)}) collective-permute-start(f32[20,4,256]{2,1,0:T(4,128)} %refs_0_.2), channel_id=1, source_target_pairs={{0,24},{4,28},{8,16},{12,20},{16,8},{20,12},{24,0},{28,4},{1,25},{... | collective-permute-start | bytes 245768 | tf_op jit(solution)/shard_map/ppermute | solution.py:532
  6.3 14.5 %collective-permute-start.4 = (f32[20,4,256]{2,1,0:T(4,128)}, f32[20,4,256]{2,1,0:T(4,128)S(1)}, u32[]{:S(2)}, u32[]{:S(2)}) collective-permute-start(f32[20,4,256]{2,1,0:T(4,128)} %refs_0_.2), channel_id=1, source_target_pairs={{0,4},{4,0},{8,12},{12,8},{16,20},{20,16},{24,28},{28,24},{1,5},{5... | collective-permute-start | bytes 245768 | tf_op jit(solution)/shard_map/ppermute | solution.py:532
  8.1 9.1 %collective-permute-start.10 = (f32[24,4,256]{2,1,0:T(4,128)}, f32[24,4,256]{2,1,0:T(4,128)S(1)}, u32[]{:S(2)}, u32[]{:S(2)}) collective-permute-start(f32[24,4,256]{2,1,0:T(4,128)} %refs_0_.3), channel_id=1, source_target_pairs={{0,8},{4,12},{8,0},{12,4},{16,24},{20,28},{24,16},{28,20},{1,9},{5... | collective-permute-start | bytes 294920 | tf_op jit(solution)/shard_map/ppermute | solution.py:532
  12.7 9.7 %collective-permute-start.6 = (f32[20,4,256]{2,1,0:T(4,128)S(1)}, f32[20,4,256]{2,1,0:T(4,128)S(1)}, u32[]{:S(2)}, u32[]{:S(2)}) collective-permute-start(f32[20,4,256]{2,1,0:T(4,128)S(1)} %collective-permute-done.5.refs_2_), channel_id=1, source_target_pairs={{0,4},{4,0},{8,12},{12,8},{16,20},{20,16},{24,28},{28,24},{1,5},{5... | collective-permute-start | bytes 245768 | tf_op jit(solution)/shard_map/ppermute | solution.py:532
  13.3 4.0 %copy-start = (f32[24,4,256]{2,1,0:T(4,128)S(1)}, f32[24,4,256]{2,1,0:T(4,128)}, u32[]{:S(2)}) copy-start(f32[24,4,256]{2,1,0:T(4,128)} %refs_0_.3) | copy-start | bytes 294916
  13.3 9.1 %copy-start.2 = (f32[20,4,256]{2,1,0:T(4,128)S(1)}, f32[20,4,256]{2,1,0:T(4,128)}, u32[]{:S(2)}) copy-start(f32[20,4,256]{2,1,0:T(4,128)} %refs_0_.2) | copy-start | bytes 245764
  15.1 8.4 %collective-permute-start.1 = (f32[20,4,256]{2,1,0:T(4,128)S(1)}, f32[20,4,256]{2,1,0:T(4,128)S(1)}, u32[]{:S(2)}, u32[]{:S(2)}) collective-permute-start(f32[20,4,256]{2,1,0:T(4,128)S(1)} %collective-permute-done.refs_4_), channel_id=1, source_target_pairs={{0,4},{4,0},{8,12},{12,8},{16,20},{20,16},{24,28},{28,24},{1,5},{5... | collective-permute-start | bytes 245768 | tf_op jit(solution)/shard_map/ppermute | solution.py:532
  16.7 6.8 %collective-permute-start.3 = (f32[20,4,256]{2,1,0:T(4,128)S(1)}, f32[20,4,256]{2,1,0:T(4,128)S(1)}, u32[]{:S(2)}, u32[]{:S(2)}) collective-permute-start(f32[20,4,256]{2,1,0:T(4,128)S(1)} %collective-permute-done.2.refs_5_), channel_id=1, source_target_pairs={{0,4},{4,0},{8,12},{12,8},{16,20},{20,16},{24,28},{28,24},{1,5},{5... | collective-permute-start | bytes 245768 | tf_op jit(solution)/shard_map/ppermute | solution.py:532
  17.3 14.2 %collective-permute-start.11 = (f32[2,96,256]{2,1,0:T(8,128)S(1)}, f32[2,96,256]{2,1,0:T(8,128)S(1)}, u32[]{:S(2)}, u32[]{:S(2)}) collective-permute-start(f32[2,96,256]{2,1,0:T(8,128)S(1)} %pair.1.refs_0_), channel_id=1, source_target_pairs={{0,16},{4,20},{8,24},{12,28},{16,0},{20,4},{24,8},{28,12},{1,17},{... | collective-permute-start | bytes 589832 | tf_op jit(solution)/shard_map/ppermute | solution.py:532
  20.9 11.2 %collective-permute-start.13 = (f32[2,96,256]{2,1,0:T(8,128)S(1)}, f32[2,96,256]{2,1,0:T(8,128)S(1)}, u32[]{:S(2)}, u32[]{:S(2)}) collective-permute-start(f32[2,96,256]{2,1,0:T(8,128)S(1)} %pair.1.refs_0_), channel_id=1, source_target_pairs={{0,4},{4,0},{8,12},{12,8},{16,20},{20,16},{24,28},{28,24},{1,5},{5... | collective-permute-start | bytes 589832 | tf_op jit(solution)/shard_map/ppermute | solution.py:532
  24.0 4.9 %copy-start.4 = (f32[44]{0:T(128)S(1)}, f32[44]{0:T(128)}, u32[]{:S(2)}) copy-start(f32[44]{0:T(128)} %param.11) | copy-start | bytes 532
  24.0 4.9 %copy-start.5 = (f32[5]{0:T(128)S(1)}, f32[5]{0:T(128)}, u32[]{:S(2)}) copy-start(f32[5]{0:T(128)} %param.12) | copy-start | bytes 64
  24.0 3.8 %collective-permute-start.7 = (f32[24,256]{1,0:T(8,128)S(1)}, f32[24,256]{1,0:T(8,128)S(1)}, u32[]{:S(2)}, u32[]{:S(2)}) collective-permute-start(f32[24,256]{1,0:T(8,128)S(1)} %shard_map.95.refs_0_), channel_id=1, source_target_pairs={{0,1},{1,0},{2,3},{3,2},{4,5},{5,4},{6,7},{7,6},{8,9},{9,8},{10,11... | collective-permute-start | bytes 73736 | tf_op jit(solution)/shard_map/ppermute | solution.py:532
  24.1 3.9 %collective-permute-start.8 = (f32[24,256]{1,0:T(8,128)S(1)}, f32[24,256]{1,0:T(8,128)S(1)}, u32[]{:S(2)}, u32[]{:S(2)}) collective-permute-start(f32[24,256]{1,0:T(8,128)S(1)} %shard_map.95.refs_0_), channel_id=1, source_target_pairs={{0,2},{1,3},{2,0},{3,1},{4,6},{5,7},{6,4},{7,5},{8,10},{9,11},{10,... | collective-permute-start | bytes 73736 | tf_op jit(solution)/shard_map/ppermute | solution.py:532
  25.7 3.3 %collective-permute-start.9 = (f32[24,256]{1,0:T(8,128)S(1)}, f32[24,256]{1,0:T(8,128)S(1)}, u32[]{:S(2)}, u32[]{:S(2)}) collective-permute-start(f32[24,256]{1,0:T(8,128)S(1)} %shard_map.95.refs_0_), channel_id=1, source_target_pairs={{0,3},{1,2},{2,1},{3,0},{4,7},{5,6},{6,5},{7,4},{8,11},{9,10},{10,... | collective-permute-start | bytes 73736 | tf_op jit(solution)/shard_map/ppermute | solution.py:532
  31.5 7.0 %collective-permute-start.12 = (f32[2,96,256]{2,1,0:T(8,128)S(1)}, f32[2,96,256]{2,1,0:T(8,128)S(1)}, u32[]{:S(2)}, u32[]{:S(2)}) collective-permute-start(f32[2,96,256]{2,1,0:T(8,128)S(1)} %collective-permute-done.11.refs_2_), channel_id=1, source_target_pairs={{0,4},{4,0},{8,12},{12,8},{16,20},{20,16},{24,28},{28,24},{1,5},{5... | collective-permute-start | bytes 589832 | tf_op jit(solution)/shard_map/ppermute | solution.py:532
  39.1 5.8 %collective-permute-start.14 = (f32[40,256]{1,0:T(8,128)S(1)}, f32[40,256]{1,0:T(8,128)S(1)}, u32[]{:S(2)}, u32[]{:S(2)}) collective-permute-start(f32[40,256]{1,0:T(8,128)S(1)} %project_late.1.refs_0_), channel_id=1, source_target_pairs={{0,1},{1,0},{2,3},{3,2},{4,5},{5,4},{6,7},{7,6},{8,9},{9,8},{10,11... | collective-permute-start | bytes 122888 | tf_op jit(solution)/shard_map/ppermute | solution.py:532
  39.2 5.7 %collective-permute-start.15 = (f32[40,256]{1,0:T(8,128)S(1)}, f32[40,256]{1,0:T(8,128)S(1)}, u32[]{:S(2)}, u32[]{:S(2)}) collective-permute-start(f32[40,256]{1,0:T(8,128)S(1)} %project_late.1.refs_0_), channel_id=1, source_target_pairs={{0,2},{1,3},{2,0},{3,1},{4,6},{5,7},{6,4},{7,5},{8,10},{9,11},{10,... | collective-permute-start | bytes 122888 | tf_op jit(solution)/shard_map/ppermute | solution.py:532
  40.0 4.9 %collective-permute-start.16 = (f32[40,256]{1,0:T(8,128)S(1)}, f32[40,256]{1,0:T(8,128)S(1)}, u32[]{:S(2)}, u32[]{:S(2)}) collective-permute-start(f32[40,256]{1,0:T(8,128)S(1)} %project_late.1.refs_0_), channel_id=1, source_target_pairs={{0,3},{1,2},{2,1},{3,0},{4,7},{5,6},{6,5},{7,4},{8,11},{9,10},{10,... | collective-permute-start | bytes 122888 | tf_op jit(solution)/shard_map/ppermute | solution.py:532
  41.0 3.9 %copy-start.3 = (f32[2048]{0:T(1024)S(1)}, f32[2048]{0:T(1024)}, u32[]{:S(2)}) copy-start(f32[2048]{0:T(1024)} %param.13) | copy-start | bytes 24580

commit v5 on v4

--- a/solution.py
+++ b/solution.py
@@ -284,9 +284,13 @@
 
 
 def _balance(columns):
-    for _ in range(BALANCE_ROUNDS):
-        inverse = 1.0 / (columns[0] + columns[1] + columns[2] + columns[3])
-        columns = [c * inverse for c in columns]
+    for turn in range(BALANCE_ROUNDS):
+        total = columns[0] + columns[1] + columns[2] + columns[3]
+        if turn == 0:
+            columns = [c / total for c in columns]
+        else:
+            inverse = 1.0 / total
+            columns = [c * inverse for c in columns]
         columns = [c * (1.0 / jnp.sum(c, axis=0, keepdims=True)) for c in columns]
     return columns
 
@@ -348,21 +352,23 @@
     low = jnp.where(of_branch, (q - 2 * rows) // MT, q // rows)
     source = jnp.where(of_branch, 4, q % 4)
     pick = jnp.where(m // 4 == low * 8 + source, 1.0, 0.0).astype(BF16)
-    r, q = _iota((rows, wide), 0), _iota((rows, wide), 1)
+    half = min(tokens, 128)
+    r, q = _iota((4 * half, wide), 0), _iota((4 * half, wide), 1)
     token = jnp.where(q >= 2 * rows, (q - 2 * rows) % MT, (q % rows) // 4)
-    same = token == r // 4
-    r, m = _iota((rows, 64), 0), _iota((rows, 64), 1)
+    same = token == (r // 4) % MT
+    r, m = _iota((4 * half, 64), 0), _iota((4 * half, 64), 1)
     keep = (m % 4) == (r % 4)
+    r, lane = _iota((4 * half, half), 0), _iota((4 * half, half), 1)
+    expand = jnp.where(lane == r // 4, 1.0, 0.0).astype(BF16)
     hi, lo = _split(jnp.concatenate([coef_ref[...], jnp.zeros((8, tokens), F32)], axis=0))
     coef = jnp.concatenate([hi, lo], axis=0)
-    for g in range(tokens // MT):
-        start = g * MT // 128 * 128
-        lane, r = _iota((rows, 128), 1), _iota((rows, 128), 0)
-        expand = jnp.where(lane == g * MT - start + r // 4, 1.0, 0.0).astype(BF16)
-        held = _nt(expand, coef[:, start : start + 128])
+    for h in range(tokens // half):
+        held = _nt(expand, coef[:, h * half : (h + 1) * half])
         held = jnp.where(keep, held, 0.0).astype(BF16)
         spread = jnp.dot(held, pick, preferred_element_type=F32)
-        left_ref[g] = jnp.where(same, spread, 0.0).astype(BF16)
+        spread = jnp.where(same, spread, 0.0).astype(BF16)
+        for g in range(half // MT):
+            left_ref[h * (half // MT) + g] = spread[g * rows : (g + 1) * rows]
 
 
 def weave(coef):
@@ -380,7 +386,8 @@
     )(coef)
 
 
-def mix_kernel(left_ref, sil_ref, b_ref, out_hbm, stage_ref, sems):
+def mix_kernel(start, stop, left_ref, sil_ref, b_ref, *refs):
+    out_hbm, stage_ref, sems = refs[-3:]
     tiles, tokens = sil_ref.shape[0], sil_ref.shape[1] // 4
     rows = 4 * MT
     flat = out_hbm.reshape(4 * tokens, tiles * 128)
@@ -405,28 +412,29 @@
         copy(2 * k + 1).start()
         return 0
 
-    lax.fori_loop(0, tiles // 2, body, 0)
-    for c in range(tiles):
+    lax.fori_loop(start, stop, body, 0)
+    for c in range(2 * start, 2 * stop):
         copy(c).wait()
 
 
-def mix(left, sil, branch):
-    tiles, tokens = sil.shape[0], sil.shape[1] // 4
-    return pl.pallas_call(
-        mix_kernel,
+def mix(left, sil, branch, start, stop, merged):
+    tiles, tokens = sil.shape[0], branch.shape[0]
+    before = [] if merged is None else [merged]
+    return pl.pallas_call(
+        functools.partial(mix_kernel, start, stop),
         out_shape=jax.ShapeDtypeStruct((tokens, 4, tiles * 128), BF16),
-        in_specs=[VMEM, VMEM, VMEM],
+        in_specs=[VMEM, VMEM, VMEM] + [HBM] * len(before),
         out_specs=HBM,
         scratch_shapes=[
             pltpu.VMEM((tiles, 4 * tokens, 128), BF16),
             pltpu.SemaphoreType.DMA((tiles,)),
         ],
+        input_output_aliases={3: 0} if before else {},
         compiler_params=pltpu.CompilerParams(vmem_limit_bytes=14 * MIB),
         cost_estimate=pl.CostEstimate(
-            flops=5_000_000_000, bytes_accessed=8 * MIB, transcendentals=0
-        ),
-        name="mix",
-    )(left, sil, branch)
+            flops=2_000_000_000, bytes_accessed=4 * MIB, transcendentals=0
+        ),
+    )(left, sil, branch, *before)
 
 
 def second_kernel(features, *refs):
@@ -581,7 +589,10 @@
         half = tokens // 2
         grams = [grams_of(sde, branch, 0, half), grams_of(sde, branch, half, tokens - half)]
         coef = first(raws, bias, scale, features)
-        streams_out = mix(weave(coef), sil, branch)
+        left = weave(coef)
+        blocks = width // FB
+        merged = mix(left, sil, branch, 0, blocks // 4, None)
+        streams_out = mix(left, sil, branch, blocks // 4, blocks, merged)
         early = project_early(next_blocks[:-1], order[:-2], sde, branch, permuted)
         next_raw = project_late(
             next_blocks[-1:], order[-2:], sde, branch, early, coef, grams, permuted

time: 47.6 us -> 54.5 us (1.14)
  waiting for transfers between devices: 6.14 us -> 15.3 us
  starting transfers between devices: 20.3 us -> 18.8 us
  Pallas kernels: 20.2 us -> 19.5 us
    ppermute x17, waiting for transfers between devices: 6.14 us -> 15.3 us  [_swap(): return lax.ppermute(x, axis, [(i, i ^ s) for i in range(count)])]
    pallas_call x1, Pallas kernels: 2.28 us -> 0.58 us  [weave(): pl.pallas_call(weave_kernel, out_shape=jax.ShapeDtypeStruct((tokens // MT...]
    ppermute x17, starting transfers between devices: 20.3 us -> 18.8 us  [_swap(): return lax.ppermute(x, axis, [(i, i ^ s) for i in range(count)])]
    pallas_call x1 -> x2, Pallas kernels: 3.84 us -> 4.8 us  [mix(): pl.pallas_call(functools.partial(mix_kernel, start, stop), out_shape=jax....]
  transfers between devices with their start and end apart: 17 -> 17, of which waited for: 3 -> 6; matrix products, arithmetic and copies ran while one was open for 0% -> 0% of each run, Pallas kernels for 36% -> 30%
where the time goes in v5:
time: 54.5 us; the launch traced here: 54.4 us
  Pallas kernels  19.5 us (36%)
  starting transfers between devices  18.8 us (34%)
  waiting for transfers between devices  15.3 us (28%)
  between operations  0.82 us (2%)
    ppermute x17, starting transfers between devices, _swap(): return lax.ppermute(x, axis, [(i, i ^ s) for i in range(count)])  18.8 us
    ppermute x17, waiting for transfers between devices, _swap(): return lax.ppermute(x, axis, [(i, i ^ s) for i in range(count)])  15.3 us
    pallas_call x2, Pallas kernels, mix(): pl.pallas_call(functools.partial(mix_kernel, start, stop), out_shape=jax....  4.8 us
    pallas_call x1, Pallas kernels, deal(): pl.pallas_call(deal_kernel, out_shape=(jax.ShapeDtypeStruct((tiles, 4 * t...  3.9 us
    pallas_call x2, Pallas kernels, grams_of(): pl.pallas_call(functools.partial(grams_kernel, start), out_shape=jax.Shap...  3.75 us
    pallas_call x1, Pallas kernels, second(): pl.pallas_call(functools.partial(second_kernel, features), out_shape=(jax...  2.52 us
    pallas_call x2, Pallas kernels, raw(): pl.pallas_call(functools.partial(raw_kernel, order, permuted, last), out_...  1.55 us
    pallas_call x1, Pallas kernels, project_early(): pl.pallas_call(functools.partial(early_kernel, order, permuted), out_shap...  1.42 us
  transfers between devices with their start and end apart: 17, of which 6 were waited for; matrix products, arithmetic and copies ran while one was open for 0% of the time, Pallas kernels for 30%

profile of v5, /device:TPU:0, one launch (start us, length us, event | category | flops | bytes accessed | tf_op | source)
XLA Modules:
  0.0 54.4 jit_solution(2068585401450099464)
XLA Ops:
  0.6 0.0 copy-start
  0.6 3.1 %collective-permute-start.4 = (f32[20,4,256]{2,1,0:T(4,128)}, f32[20,4,256]{2,1,0:T(4,128)S(1)}, u32[]{:S(2)}, u32[]{:S(2)}) collective-permute-start(f32[20,4,256]{2,1,0:T(4,128)} %refs_0_.2), channel_id=1, source_target_pairs={{0,4},{4,0},{8,12},{12,8},{16,20},{20,16},{24,28},{28,24},{1,5},{5... | collective-permute-start | bytes 245768 | tf_op jit(solution)/shard_map/ppermute | solution.py:540
  3.7 3.6 %collective-permute-start.2 = (f32[20,4,256]{2,1,0:T(4,128)}, f32[20,4,256]{2,1,0:T(4,128)S(1)}, u32[]{:S(2)}, u32[]{:S(2)}) collective-permute-start(f32[20,4,256]{2,1,0:T(4,128)} %refs_0_.2), channel_id=1, source_target_pairs={{0,24},{4,28},{8,16},{12,20},{16,8},{20,12},{24,0},{28,4},{1,25},{... | collective-permute-start | bytes 245768 | tf_op jit(solution)/shard_map/ppermute | solution.py:540
  7.3 0.0 collective-permute-start
  7.3 0.8 %collective-permute-start.5 = (f32[20,4,256]{2,1,0:T(4,128)}, f32[20,4,256]{2,1,0:T(4,128)S(1)}, u32[]{:S(2)}, u32[]{:S(2)}) collective-permute-start(f32[20,4,256]{2,1,0:T(4,128)} %refs_0_.2), channel_id=1, source_target_pairs={{0,8},{4,12},{8,0},{12,4},{16,24},{20,28},{24,16},{28,20},{1,9},{5... | collective-permute-start | bytes 245768 | tf_op jit(solution)/shard_map/ppermute | solution.py:540
  8.1 1.2 %collective-permute-start.10 = (f32[24,4,256]{2,1,0:T(4,128)}, f32[24,4,256]{2,1,0:T(4,128)S(1)}, u32[]{:S(2)}, u32[]{:S(2)}) collective-permute-start(f32[24,4,256]{2,1,0:T(4,128)} %refs_0_.3), channel_id=1, source_target_pairs={{0,8},{4,12},{8,0},{12,4},{16,24},{20,28},{24,16},{28,20},{1,9},{5... | collective-permute-start | bytes 294920 | tf_op jit(solution)/shard_map/ppermute | solution.py:540
  9.3 3.9 %deal.1 = (bf16[16,1024,128]{2,1,0:T(8,128)(2,1)S(1)}, bf16[8,4,256,256]{3,2,1,0:T(8,128)(2,1)S(1)}, f32[8,256]{1,0:T(8,128)S(1)}) custom-call(bf16[256,4,2048]{2,1,0:T(4,128)(2,1)} %s_hbm.1), custom_call_target="tpu_custom_call" | custom-call | flops 6000000000 | bytes 10485760 | tf_op jit(solution)/shard_map/deal/pallas_call | solution.py:89
  13.2 1.4 %collective-permute-done.5.refs_2_ = f32[20,4,256]{2,1,0:T(4,128)S(1)} collective-permute-done((f32[20,4,256]{2,1,0:T(4,128)}, f32[20,4,256]{2,1,0:T(4,128)S(1)}, u32[]{:S(2)}, u32[]{:S(2)}) %collective-permute-start.5) | collective-permute-done | bytes 81952 | tf_op jit(solution)/shard_map/ppermute | solution.py:540
  14.6 0.4 collective-permute-start.6
  15.0 0.0 copy-done
  15.0 0.0 copy-start.2
  15.0 1.9 %shard_map.99.refs_6_ = f32[16,128]{1,0:T(8,128)S(1)} custom-call(bf16[8,4,256,256]{3,2,1,0:T(8,128)(2,1)S(1)} %get-tuple-element.8.refs_6_.refs_2_.refs_3_.sde_ref.refs_1_.refs_7_, bf16[256,2048]{1,0:T(8,128)(2,1)S(1)} %copy-done), custom_call_target="tpu_custom_call" | custom-call | flops 3000000000 | bytes 5242880 | tf_op jit(solution)/shard_map/pallas_call | solution.py:133
  16.9 0.0 collective-permute-done.2.refs_5_
  16.9 1.6 %collective-permute-start.3 = (f32[20,4,256]{2,1,0:T(4,128)S(1)}, f32[20,4,256]{2,1,0:T(4,128)S(1)}, u32[]{:S(2)}, u32[]{:S(2)}) collective-permute-start(f32[20,4,256]{2,1,0:T(4,128)S(1)} %collective-permute-done.2.refs_5_), channel_id=1, source_target_pairs={{0,4},{4,0},{8,12},{12,8},{16,20},{20,16},{24,28},{28,24},{1,5},{5... | collective-permute-start | bytes 245768 | tf_op jit(solution)/shard_map/ppermute | solution.py:540
  18.5 0.0 collective-permute-done.refs_4_
  18.5 0.4 collective-permute-start.1
  19.0 0.0 collective-permute-done.4.refs_1_
  19.0 0.8 %collective-permute-done.6.refs_3_ = f32[20,4,256]{2,1,0:T(4,128)S(1)} collective-permute-done((f32[20,4,256]{2,1,0:T(4,128)S(1)}, f32[20,4,256]{2,1,0:T(4,128)S(1)}, u32[]{:S(2)}, u32[]{:S(2)}) %collective-permute-start.6) | collective-permute-done | bytes 81952 | tf_op jit(solution)/shard_map/ppermute | solution.py:540
  19.8 0.0 copy-done.2
  19.8 1.1 %shard_map.94.refs_3_ = f32[24,256]{1,0:T(8,128)S(1)} custom-call(f32[20,4,256]{2,1,0:T(4,128)S(1)} %copy-done.2, f32[20,4,256]{2,1,0:T(4,128)S(1)} %collective-permute-done.4.refs_1_, f32[20,4,256]{2,1,0:T(4,128)S(1)} %collective-permute-done.5.refs_2_, f32[20,4,256]{2,1,0:T(4,128)S(1)} %collective-permute-done.6.refs_3_, ...), custom_call_target="tpu_custom_call" | custom-call | flops 2000000000 | bytes 5242880 | tf_op jit(solution)/shard_map/pallas_call | solution.py:177
  20.9 0.5 %collective-permute-done.3.refs_1_ = f32[20,4,256]{2,1,0:T(4,128)S(1)} collective-permute-done((f32[20,4,256]{2,1,0:T(4,128)S(1)}, f32[20,4,256]{2,1,0:T(4,128)S(1)}, u32[]{:S(2)}, u32[]{:S(2)}) %collective-permute-start.3) | collective-permute-done | bytes 81952 | tf_op jit(solution)/shard_map/ppermute | solution.py:540
  21.4 1.6 %collective-permute-done.1.refs_0_ = f32[20,4,256]{2,1,0:T(4,128)S(1)} collective-permute-done((f32[20,4,256]{2,1,0:T(4,128)S(1)}, f32[20,4,256]{2,1,0:T(4,128)S(1)}, u32[]{:S(2)}, u32[]{:S(2)}) %collective-permute-start.1) | collective-permute-done | bytes 81952 | tf_op jit(solution)/shard_map/ppermute | solution.py:540
  23.0 0.5 shard_map.95.refs_0_
  23.5 0.0 copy-start.1
  23.5 0.0 copy-start.4
  23.5 0.0 copy-start.5
  23.5 0.1 collective-permute-start.9
  23.6 1.6 %collective-permute-start.8 = (f32[24,256]{1,0:T(8,128)S(1)}, f32[24,256]{1,0:T(8,128)S(1)}, u32[]{:S(2)}, u32[]{:S(2)}) collective-permute-start(f32[24,256]{1,0:T(8,128)S(1)} %shard_map.95.refs_0_), channel_id=1, source_target_pairs={{0,2},{1,3},{2,0},{3,1},{4,6},{5,7},{6,4},{7,5},{8,10},{9,11},{10,... | collective-permute-start | bytes 73736 | tf_op jit(solution)/shard_map/ppermute | solution.py:540
  25.1 0.3 collective-permute-start.7
  25.4 1.9 %shard_map.98.refs_5_ = f32[16,128]{1,0:T(8,128)S(1)} custom-call(bf16[8,4,256,256]{3,2,1,0:T(8,128)(2,1)S(1)} %get-tuple-element.8.refs_6_.refs_2_.refs_3_.sde_ref.refs_1_.refs_7_, bf16[256,2048]{1,0:T(8,128)(2,1)S(1)} %copy-done), custom_call_target="tpu_custom_call" | custom-call | flops 3000000000 | bytes 5242880 | tf_op jit(solution)/shard_map/pallas_call | solution.py:133
  27.3 0.0 collective-permute-done.10.refs_1_
  27.3 0.0 copy-done.1
  27.3 0.1 pair.1.refs_0_
  27.4 0.9 %collective-permute-start.13 = (f32[2,96,256]{2,1,0:T(8,128)S(1)}, f32[2,96,256]{2,1,0:T(8,128)S(1)}, u32[]{:S(2)}, u32[]{:S(2)}) collective-permute-start(f32[2,96,256]{2,1,0:T(8,128)S(1)} %pair.1.refs_0_), channel_id=1, source_target_pairs={{0,4},{4,0},{8,12},{12,8},{16,20},{20,16},{24,28},{28,24},{1,5},{5... | collective-permute-start | bytes 589832 | tf_op jit(solution)/shard_map/ppermute | solution.py:540
  28.3 1.6 %collective-permute-start.11 = (f32[2,96,256]{2,1,0:T(8,128)S(1)}, f32[2,96,256]{2,1,0:T(8,128)S(1)}, u32[]{:S(2)}, u32[]{:S(2)}) collective-permute-start(f32[2,96,256]{2,1,0:T(8,128)S(1)} %pair.1.refs_0_), channel_id=1, source_target_pairs={{0,16},{4,20},{8,24},{12,28},{16,0},{20,4},{24,8},{28,12},{1,17},{... | collective-permute-start | bytes 589832 | tf_op jit(solution)/shard_map/ppermute | solution.py:540
  30.0 0.0 collective-permute-done.9.refs_3_
  30.0 0.0 collective-permute-done.8.refs_2_
  30.0 0.0 collective-permute-done.7.refs_1_
  30.0 0.0 copy-done.4
  30.0 0.0 copy-done.5
  30.0 0.3 first.1.coef_ref.refs_4_
  30.3 0.6 %weave.1.left_ref = bf16[16,64,160]{2,1,0:T(8,128)(2,1)S(1)} custom-call(f32[24,256]{1,0:T(8,128)S(1)} %first.1.coef_ref.refs_4_), custom_call_target="tpu_custom_call" | custom-call | flops 1000000000 | bytes 1048576 | tf_op jit(solution)/shard_map/weave/pallas_call | solution.py:376
  30.9 1.7 %shard_map.96.refs_0_ = bf16[256,4,2048]{2,1,0:T(4,128)(2,1)} custom-call(bf16[16,64,160]{2,1,0:T(8,128)(2,1)S(1)} %weave.1.left_ref, bf16[16,1024,128]{2,1,0:T(8,128)(2,1)S(1)} %get-tuple-element.10.sil_ref, bf16[256,2048]{1,0:T(8,128)(2,1)S(1)} %copy-done), custom_call_target="tpu_custom_call" | custom-call | flops 2000000000 | bytes 4194304 | tf_op jit(solution)/shard_map/pallas_call | solution.py:423
  32.6 7.6 %collective-permute-done.11.refs_2_ = f32[2,96,256]{2,1,0:T(8,128)S(1)} collective-permute-done((f32[2,96,256]{2,1,0:T(8,128)S(1)}, f32[2,96,256]{2,1,0:T(8,128)S(1)}, u32[]{:S(2)}, u32[]{:S(2)}) %collective-permute-start.11) | collective-permute-done | bytes 196640 | tf_op jit(solution)/shard_map/ppermute | solution.py:540
  40.2 1.2 %collective-permute-start.12 = (f32[2,96,256]{2,1,0:T(8,128)S(1)}, f32[2,96,256]{2,1,0:T(8,128)S(1)}, u32[]{:S(2)}, u32[]{:S(2)}) collective-permute-start(f32[2,96,256]{2,1,0:T(8,128)S(1)} %collective-permute-done.11.refs_2_), channel_id=1, source_target_pairs={{0,4},{4,0},{8,12},{12,8},{16,20},{20,16},{24,28},{28,24},{1,5},{5... | collective-permute-start | bytes 589832 | tf_op jit(solution)/shard_map/ppermute | solution.py:540
  41.4 0.0 collective-permute-done.13.refs_1_
  41.4 1.4 %project_early.1.refs_3_ = f32[5,96,256]{2,1,0:T(8,128)S(1)} custom-call(f32[2,96,256]{2,1,0:T(8,128)S(1)} %pair.1.refs_0_, f32[2,96,256]{2,1,0:T(8,128)S(1)} %collective-permute-done.13.refs_1_, f32[2,96,256]{2,1,0:T(8,128)S(1)} %collective-permute-done.11.refs_2_, ...), custom_call_target="tpu_custom_call" | custom-call | flops 3000000000 | bytes 6291456 | tf_op jit(solution)/shard_map/project_early/pallas_call | solution.py:256
  42.8 3.4 %collective-permute-done.12.refs_0_ = f32[2,96,256]{2,1,0:T(8,128)S(1)} collective-permute-done((f32[2,96,256]{2,1,0:T(8,128)S(1)}, f32[2,96,256]{2,1,0:T(8,128)S(1)}, u32[]{:S(2)}, u32[]{:S(2)}) %collective-permute-start.12) | collective-permute-done | bytes 196640 | tf_op jit(solution)/shard_map/ppermute | solution.py:540
  46.2 0.6 %project_late.1.refs_0_ = f32[40,256]{1,0:T(8,128)S(1)} custom-call(f32[2,96,256]{2,1,0:T(8,128)S(1)} %collective-permute-done.12.refs_0_, bf16[8,4,256,256]{3,2,1,0:T(8,128)(2,1)S(1)} %get-tuple-element.8.refs_6_.refs_2_.refs_3_.sde_ref.refs_1_.refs_7_, bf16[256,2048]{1,0:T(8,128)(2,1)S(1)} %copy-done, f32[5,96,256]{2,1,0:T(8,128)S(1)} %project_early.1.refs_3_, ...), custom_call_target="tpu_custom_call" | custom-call | flops 3000000000 | bytes 6291456 | tf_op jit(solution)/shard_map/project_late/pallas_call | solution.py:272
  46.8 0.0 copy-start.3
  46.8 0.1 collective-permute-start.16
  46.9 1.3 %collective-permute-start.15 = (f32[40,256]{1,0:T(8,128)S(1)}, f32[40,256]{1,0:T(8,128)S(1)}, u32[]{:S(2)}, u32[]{:S(2)}) collective-permute-start(f32[40,256]{1,0:T(8,128)S(1)} %project_late.1.refs_0_), channel_id=1, source_target_pairs={{0,2},{1,3},{2,0},{3,1},{4,6},{5,7},{6,4},{7,5},{8,10},{9,11},{10,... | collective-permute-start | bytes 122888 | tf_op jit(solution)/shard_map/ppermute | solution.py:540
  48.2 0.5 collective-permute-start.14
  48.7 3.1 %shard_map.97 = bf16[256,4,2048]{2,1,0:T(4,128)(2,1)} custom-call(bf16[16,64,160]{2,1,0:T(8,128)(2,1)S(1)} %weave.1.left_ref, bf16[16,1024,128]{2,1,0:T(8,128)(2,1)S(1)} %get-tuple-element.10.sil_ref, bf16[256,2048]{1,0:T(8,128)(2,1)S(1)} %copy-done, bf16[256,4,2048]{2,1,0:T(4,128)(2,1)} %shard_map.96.refs_0_), custom_call_target="tpu_custom_call", output_to_operand_aliasing={{}: (3, {})} | custom-call | flops 2000000000 | bytes 4194304 | tf_op jit(solution)/shard_map/pallas_call | solution.py:423
  51.8 0.0 collective-permute-done.16.refs_3_
  51.8 0.0 collective-permute-done.15.refs_2_
  51.9 0.0 collective-permute-done.14.refs_1_
  51.9 0.0 copy-done.3
  51.9 2.5 %second.1 = (bf16[256,2048]{1,0:T(8,128)(2,1)}, f32[20,256]{1,0:T(8,128)}) custom-call(f32[40,256]{1,0:T(8,128)S(1)} %project_late.1.refs_0_, f32[40,256]{1,0:T(8,128)S(1)} %collective-permute-done.14.refs_1_, f32[40,256]{1,0:T(8,128)S(1)} %collective-permute-done.15.refs_2_, f32[40,256]{1,0:T(8,128)S(1)} %collective-permute-done.16.refs_3_, ...), custom_call_target="tpu_custom_call" | custom-call | flops 3000000000 | bytes 6291456 | tf_op jit(solution)/shard_map/second/pallas_call | solution.py:515
Async XLA Ops:
  0.6 14.4 %copy-start = (bf16[256,2048]{1,0:T(8,128)(2,1)S(1)}, bf16[256,2048]{1,0:T(8,128)(2,1)}, u32[]{:S(2)}) copy-start(bf16[256,2048]{1,0:T(8,128)(2,1)} %refs_8_.1) | copy-start | bytes 3145732
  0.6 18.4 %collective-permute-start.4 = (f32[20,4,256]{2,1,0:T(4,128)}, f32[20,4,256]{2,1,0:T(4,128)S(1)}, u32[]{:S(2)}, u32[]{:S(2)}) collective-permute-start(f32[20,4,256]{2,1,0:T(4,128)} %refs_0_.2), channel_id=1, source_target_pairs={{0,4},{4,0},{8,12},{12,8},{16,20},{20,16},{24,28},{28,24},{1,5},{5... | collective-permute-start | bytes 245768 | tf_op jit(solution)/shard_map/ppermute | solution.py:540
  3.7 13.2 %collective-permute-start.2 = (f32[20,4,256]{2,1,0:T(4,128)}, f32[20,4,256]{2,1,0:T(4,128)S(1)}, u32[]{:S(2)}, u32[]{:S(2)}) collective-permute-start(f32[20,4,256]{2,1,0:T(4,128)} %refs_0_.2), channel_id=1, source_target_pairs={{0,24},{4,28},{8,16},{12,20},{16,8},{20,12},{24,0},{28,4},{1,25},{... | collective-permute-start | bytes 245768 | tf_op jit(solution)/shard_map/ppermute | solution.py:540
  7.3 11.2 %collective-permute-start = (f32[20,4,256]{2,1,0:T(4,128)}, f32[20,4,256]{2,1,0:T(4,128)S(1)}, u32[]{:S(2)}, u32[]{:S(2)}) collective-permute-start(f32[20,4,256]{2,1,0:T(4,128)} %refs_0_.2), channel_id=1, source_target_pairs={{0,16},{4,20},{8,24},{12,28},{16,0},{20,4},{24,8},{28,12},{1,17},{... | collective-permute-start | bytes 245768 | tf_op jit(solution)/shard_map/ppermute | solution.py:540
  7.3 7.3 %collective-permute-start.5 = (f32[20,4,256]{2,1,0:T(4,128)}, f32[20,4,256]{2,1,0:T(4,128)S(1)}, u32[]{:S(2)}, u32[]{:S(2)}) collective-permute-start(f32[20,4,256]{2,1,0:T(4,128)} %refs_0_.2), channel_id=1, source_target_pairs={{0,8},{4,12},{8,0},{12,4},{16,24},{20,28},{24,16},{28,20},{1,9},{5... | collective-permute-start | bytes 245768 | tf_op jit(solution)/shard_map/ppermute | solution.py:540
  8.1 19.2 %collective-permute-start.10 = (f32[24,4,256]{2,1,0:T(4,128)}, f32[24,4,256]{2,1,0:T(4,128)S(1)}, u32[]{:S(2)}, u32[]{:S(2)}) collective-permute-start(f32[24,4,256]{2,1,0:T(4,128)} %refs_0_.3), channel_id=1, source_target_pairs={{0,8},{4,12},{8,0},{12,4},{16,24},{20,28},{24,16},{28,20},{1,9},{5... | collective-permute-start | bytes 294920 | tf_op jit(solution)/shard_map/ppermute | solution.py:540
  14.6 5.2 %collective-permute-start.6 = (f32[20,4,256]{2,1,0:T(4,128)S(1)}, f32[20,4,256]{2,1,0:T(4,128)S(1)}, u32[]{:S(2)}, u32[]{:S(2)}) collective-permute-start(f32[20,4,256]{2,1,0:T(4,128)S(1)} %collective-permute-done.5.refs_2_), channel_id=1, source_target_pairs={{0,4},{4,0},{8,12},{12,8},{16,20},{20,16},{24,28},{28,24},{1,5},{5... | collective-permute-start | bytes 245768 | tf_op jit(solution)/shard_map/ppermute | solution.py:540
  15.0 4.7 %copy-start.2 = (f32[20,4,256]{2,1,0:T(4,128)S(1)}, f32[20,4,256]{2,1,0:T(4,128)}, u32[]{:S(2)}) copy-start(f32[20,4,256]{2,1,0:T(4,128)} %refs_0_.2) | copy-start | bytes 245764
  16.9 4.5 %collective-permute-start.3 = (f32[20,4,256]{2,1,0:T(4,128)S(1)}, f32[20,4,256]{2,1,0:T(4,128)S(1)}, u32[]{:S(2)}, u32[]{:S(2)}) collective-permute-start(f32[20,4,256]{2,1,0:T(4,128)S(1)} %collective-permute-done.2.refs_5_), channel_id=1, source_target_pairs={{0,4},{4,0},{8,12},{12,8},{16,20},{20,16},{24,28},{28,24},{1,5},{5... | collective-permute-start | bytes 245768 | tf_op jit(solution)/shard_map/ppermute | solution.py:540
  18.5 4.4 %collective-permute-start.1 = (f32[20,4,256]{2,1,0:T(4,128)S(1)}, f32[20,4,256]{2,1,0:T(4,128)S(1)}, u32[]{:S(2)}, u32[]{:S(2)}) collective-permute-start(f32[20,4,256]{2,1,0:T(4,128)S(1)} %collective-permute-done.refs_4_), channel_id=1, source_target_pairs={{0,4},{4,0},{8,12},{12,8},{16,20},{20,16},{24,28},{28,24},{1,5},{5... | collective-permute-start | bytes 245768 | tf_op jit(solution)/shard_map/ppermute | solution.py:540
  23.5 3.8 %copy-start.1 = (f32[24,4,256]{2,1,0:T(4,128)S(1)}, f32[24,4,256]{2,1,0:T(4,128)}, u32[]{:S(2)}) copy-start(f32[24,4,256]{2,1,0:T(4,128)} %refs_0_.3) | copy-start | bytes 294916
  23.5 6.5 %copy-start.4 = (f32[44]{0:T(128)S(1)}, f32[44]{0:T(128)}, u32[]{:S(2)}) copy-start(f32[44]{0:T(128)} %param.11) | copy-start | bytes 532
  23.5 6.5 %copy-start.5 = (f32[5]{0:T(128)S(1)}, f32[5]{0:T(128)}, u32[]{:S(2)}) copy-start(f32[5]{0:T(128)} %param.12) | copy-start | bytes 64
  23.5 6.5 %collective-permute-start.9 = (f32[24,256]{1,0:T(8,128)S(1)}, f32[24,256]{1,0:T(8,128)S(1)}, u32[]{:S(2)}, u32[]{:S(2)}) collective-permute-start(f32[24,256]{1,0:T(8,128)S(1)} %shard_map.95.refs_0_), channel_id=1, source_target_pairs={{0,3},{1,2},{2,1},{3,0},{4,7},{5,6},{6,5},{7,4},{8,11},{9,10},{10,... | collective-permute-start | bytes 73736 | tf_op jit(solution)/shard_map/ppermute | solution.py:540
  23.6 6.4 %collective-permute-start.8 = (f32[24,256]{1,0:T(8,128)S(1)}, f32[24,256]{1,0:T(8,128)S(1)}, u32[]{:S(2)}, u32[]{:S(2)}) collective-permute-start(f32[24,256]{1,0:T(8,128)S(1)} %shard_map.95.refs_0_), channel_id=1, source_target_pairs={{0,2},{1,3},{2,0},{3,1},{4,6},{5,7},{6,4},{7,5},{8,10},{9,11},{10,... | collective-permute-start | bytes 73736 | tf_op jit(solution)/shard_map/ppermute | solution.py:540
  25.1 4.9 %collective-permute-start.7 = (f32[24,256]{1,0:T(8,128)S(1)}, f32[24,256]{1,0:T(8,128)S(1)}, u32[]{:S(2)}, u32[]{:S(2)}) collective-permute-start(f32[24,256]{1,0:T(8,128)S(1)} %shard_map.95.refs_0_), channel_id=1, source_target_pairs={{0,1},{1,0},{2,3},{3,2},{4,5},{5,4},{6,7},{7,6},{8,9},{9,8},{10,11... | collective-permute-start | bytes 73736 | tf_op jit(solution)/shard_map/ppermute | solution.py:540
  27.4 14.0 %collective-permute-start.13 = (f32[2,96,256]{2,1,0:T(8,128)S(1)}, f32[2,96,256]{2,1,0:T(8,128)S(1)}, u32[]{:S(2)}, u32[]{:S(2)}) collective-permute-start(f32[2,96,256]{2,1,0:T(8,128)S(1)} %pair.1.refs_0_), channel_id=1, source_target_pairs={{0,4},{4,0},{8,12},{12,8},{16,20},{20,16},{24,28},{28,24},{1,5},{5... | collective-permute-start | bytes 589832 | tf_op jit(solution)/shard_map/ppermute | solution.py:540
  28.3 11.9 %collective-permute-start.11 = (f32[2,96,256]{2,1,0:T(8,128)S(1)}, f32[2,96,256]{2,1,0:T(8,128)S(1)}, u32[]{:S(2)}, u32[]{:S(2)}) collective-permute-start(f32[2,96,256]{2,1,0:T(8,128)S(1)} %pair.1.refs_0_), channel_id=1, source_target_pairs={{0,16},{4,20},{8,24},{12,28},{16,0},{20,4},{24,8},{28,12},{1,17},{... | collective-permute-start | bytes 589832 | tf_op jit(solution)/shard_map/ppermute | solution.py:540
  40.2 5.9 %collective-permute-start.12 = (f32[2,96,256]{2,1,0:T(8,128)S(1)}, f32[2,96,256]{2,1,0:T(8,128)S(1)}, u32[]{:S(2)}, u32[]{:S(2)}) collective-permute-start(f32[2,96,256]{2,1,0:T(8,128)S(1)} %collective-permute-done.11.refs_2_), channel_id=1, source_target_pairs={{0,4},{4,0},{8,12},{12,8},{16,20},{20,16},{24,28},{28,24},{1,5},{5... | collective-permute-start | bytes 589832 | tf_op jit(solution)/shard_map/ppermute | solution.py:540
  46.8 5.1 %copy-start.3 = (f32[2048]{0:T(1024)S(1)}, f32[2048]{0:T(1024)}, u32[]{:S(2)}) copy-start(f32[2048]{0:T(1024)} %param.13) | copy-start | bytes 24580
  46.8 5.1 %collective-permute-start.16 = (f32[40,256]{1,0:T(8,128)S(1)}, f32[40,256]{1,0:T(8,128)S(1)}, u32[]{:S(2)}, u32[]{:S(2)}) collective-permute-start(f32[40,256]{1,0:T(8,128)S(1)} %project_late.1.refs_0_), channel_id=1, source_target_pairs={{0,3},{1,2},{2,1},{3,0},{4,7},{5,6},{6,5},{7,4},{8,11},{9,10},{10,... | collective-permute-start | bytes 122888 | tf_op jit(solution)/shard_map/ppermute | solution.py:540
  46.9 5.0 %collective-permute-start.15 = (f32[40,256]{1,0:T(8,128)S(1)}, f32[40,256]{1,0:T(8,128)S(1)}, u32[]{:S(2)}, u32[]{:S(2)}) collective-permute-start(f32[40,256]{1,0:T(8,128)S(1)} %project_late.1.refs_0_), channel_id=1, source_target_pairs={{0,2},{1,3},{2,0},{3,1},{4,6},{5,7},{6,4},{7,5},{8,10},{9,11},{10,... | collective-permute-start | bytes 122888 | tf_op jit(solution)/shard_map/ppermute | solution.py:540
  48.2 3.7 %collective-permute-start.14 = (f32[40,256]{1,0:T(8,128)S(1)}, f32[40,256]{1,0:T(8,128)S(1)}, u32[]{:S(2)}, u32[]{:S(2)}) collective-permute-start(f32[40,256]{1,0:T(8,128)S(1)} %project_late.1.refs_0_), channel_id=1, source_target_pairs={{0,1},{1,0},{2,3},{3,2},{4,5},{5,4},{6,7},{7,6},{8,9},{9,8},{10,11... | collective-permute-start | bytes 122888 | tf_op jit(solution)/shard_map/ppermute | solution.py:540
